TPU v7x, 32 devices: a whole 2x2x4 slice. The times are simulated.
32 devices in a mesh: dp: 4 (over z), gx: 4 (over y, x), gy: 2 (over core).
Axes of the slice: x: 2, y: 2, z: 4, core: 2. Of those that a mesh axis runs over, the one named last changes fastest.
Arguments:
- block_input: bfloat16 [2, 576, 8192], P('gy', 'gx', 'dp'), may hold values from -6 to 6
- lengths: int32 [8, 6], P(('dp', 'gy')), may hold values from 0 to 512, as said below
- ln1_gain: float32 [2, 576], P('gy', 'gx'), may hold values from 0.1 to 1.9
- ln1_bias: float32 [2, 576], P('gy', 'gx'), may hold values from -3 to 3
- w_qkv: bfloat16 [2, 576, 3, 1152], P('gy', 'dp', None, 'gx'), may hold values from -0.1875 to 0.1875
- qv_bias: float32 [2, 1152], P(None, 'gx'), may hold values from -3 to 3
- w_out: bfloat16 [1152, 2, 576], P('gx', 'gy', 'dp'), may hold values from -1 to 1
- out_bias: float32 [2, 576], P('gy', 'gx'), may hold values from -3 to 3
- ln2_gain: float32 [2, 576], P('gy', 'gx'), may hold values from 0.1 to 1.9
- ln2_bias: float32 [2, 576], P('gy', 'gx'), may hold values from -3 to 3
- w_up: bfloat16 [2, 576, 4304], P('gy', 'dp', 'gx'), may hold values from -0.1875 to 0.1875
- up_bias: float32 [4304], P('gx'), may hold values from -3 to 3
- w_down: bfloat16 [4304, 2, 576], P('gx', 'gy', 'dp'), may hold values from -0.09375 to 0.09375
- down_bias: float32 [2, 576], P('gy', 'gx'), may hold values from -3 to 3
- cotangent: bfloat16 [2, 576, 8192], P('gy', 'gx', 'dp'), may hold values from -6 to 6
Outputs:
- block_output: bfloat16 [2, 576, 8192], P('gy', 'gx', 'dp')
- input_grad: float32 [2, 576, 8192], P('gy', 'gx', 'dp')
- grad_ln1_gain: float32 [2, 576], P('gy', 'gx')
- grad_ln1_bias: float32 [2, 576], P('gy', 'gx')
- grad_w_qkv: float32 [2, 576, 3, 1152], P('gy', 'dp', None, 'gx')
- grad_qv_bias: float32 [2, 1152], P(None, 'gx')
- grad_w_out: float32 [1152, 2, 576], P('gx', 'gy', 'dp')
- grad_out_bias: float32 [2, 576], P('gy', 'gx')
- grad_ln2_gain: float32 [2, 576], P('gy', 'gx')
- grad_ln2_bias: float32 [2, 576], P('gy', 'gx')
- grad_w_up: float32 [2, 576, 4304], P('gy', 'dp', 'gx')
- grad_up_bias: float32 [4304], P('gx')
- grad_w_down: float32 [4304, 2, 576], P('gx', 'gy', 'dp')
- grad_down_bias: float32 [2, 576], P('gy', 'gx')
Inputs may be any that keep to these rules, and one draw needn't show every extreme that they name: In each row the nonzero lengths come first, each between 100 and 512, and sum to at most 1024; a zero marks an unused slot; the first slot of every row is used; some row holds a picture of 512 patches.
All inputs are finite; a program needn't handle non-finite values.
Results may differ from a plain program's by a relative error of at most 0.019.
Values may be sent and summed in bfloat16 or wider, within the bound.
A program may use at most 128 MiB of HBM per device.

v0:
```python
import jax
import jax.numpy as jnp
from jax import lax
from jax.sharding import PartitionSpec as P

D = 1152
HEAD_DIM = 72


EPSILON = 1e-06
CONTRACT_ROWS = (((0,), (0,)), ((), ()))
CONTRACT_COLS = (((1,), (1,)), ((), ()))


def gelu_tanh(pre_act):
    return jax.nn.gelu(pre_act, approximate=True)


def flatten_weights(weights):
    w_query, w_proj, w_raise, w_lower = weights
    return (
        w_query.reshape(w_query.shape[1], -1),
        w_proj.reshape(w_proj.shape[0], -1),
        w_raise.reshape(w_raise.shape[1], -1),
        w_lower.reshape(w_lower.shape[0], -1),
    )


def norm_forward(stream, gain_row, shift_row):
    totals = lax.psum((jnp.sum(stream, axis=1), jnp.sum(stream * stream, axis=1)), ("gx", "gy"))
    average = totals[0] / D
    spread = totals[1] / D - average * average
    inv_std = lax.rsqrt(spread + EPSILON)
    normed = (stream - average[:, None]) * inv_std[:, None]
    return (normed, inv_std, (normed * gain_row + shift_row).astype(jnp.bfloat16))


def norm_backward(grad_hidden, normed, inv_std, gain_row):
    grad_normed = grad_hidden * gain_row
    totals = lax.psum(
        (jnp.sum(grad_normed, axis=1), jnp.sum(grad_normed * normed, axis=1)), ("gx", "gy")
    )
    return inv_std[:, None] * (
        grad_normed - totals[0][:, None] / D - normed * (totals[1][:, None] / D)
    )


def widen(hidden, weight):
    gathered = lax.all_gather(hidden, "gx", axis=1, tiled=True)
    return (
        gathered,
        lax.psum_scatter(
            jnp.dot(gathered, weight, preferred_element_type=jnp.float32),
            "gy",
            scatter_dimension=0,
            tiled=True,
        ),
    )


def narrow(values_in, weight):
    gathered = lax.all_gather(values_in, "gy", axis=0, tiled=True)
    product = jnp.dot(gathered, weight, preferred_element_type=jnp.float32)
    return (
        gathered,
        lax.psum_scatter(
            product.astype(jnp.bfloat16), "gx", scatter_dimension=1, tiled=True
        ).astype(jnp.float32),
    )


def narrow_back(grad_stream, kept_rows, weight):
    gathered = lax.all_gather(grad_stream, "gx", axis=1, tiled=True)
    grad_weight = lax.dot_general(
        kept_rows, gathered, CONTRACT_ROWS, preferred_element_type=jnp.float32
    )
    return (
        grad_weight,
        lax.psum_scatter(
            lax.dot_general(gathered, weight, CONTRACT_COLS, preferred_element_type=jnp.float32),
            "gy",
            scatter_dimension=0,
            tiled=True,
        ),
    )


def widen_back(grad_rows, kept_rows, weight):
    gathered = lax.all_gather(grad_rows, "gy", axis=0, tiled=True)
    grad_weight = lax.dot_general(
        kept_rows, gathered, CONTRACT_ROWS, preferred_element_type=jnp.float32
    )
    product = lax.dot_general(gathered, weight, CONTRACT_COLS, preferred_element_type=jnp.float32)
    return (gathered, grad_weight, lax.psum_scatter(product, "gx", scatter_dimension=1, tiled=True))


def picture_masks(lengths, row_count):
    slot_ends = jnp.cumsum(lengths[0])
    position = lax.iota(jnp.int32, row_count)
    picture = jnp.sum((position[:, None] >= slot_ends[None, :]).astype(jnp.int32), axis=1)
    return (picture, position < slot_ends[-1])


def attention_forward(queries, key_rows, values_in, picture, valid_token):
    row_count = queries.shape[0]
    block_rows = min(512, row_count)
    factor = HEAD_DIM ** (-0.5)
    outputs = []
    totals = []
    for head_index in range(queries.shape[1] // HEAD_DIM):
        column_start = head_index * HEAD_DIM
        key_head = key_rows[:, column_start : column_start + HEAD_DIM]
        value_head = values_in[:, column_start : column_start + HEAD_DIM]
        head_outputs = []
        head_totals = []
        for row_begin in range(0, row_count, block_rows):
            query_block = queries[
                row_begin : row_begin + block_rows, column_start : column_start + HEAD_DIM
            ]
            allowed = (
                picture[row_begin : row_begin + block_rows, None] == picture[None, :]
            ) & valid_token[None, :]
            scores = (
                lax.dot_general(
                    query_block, key_head, CONTRACT_COLS, preferred_element_type=jnp.float32
                )
                * factor
            )
            weight_kept = jnp.where(allowed, jnp.exp(scores), 0.0)
            denominator = jnp.where(
                valid_token[row_begin : row_begin + block_rows], jnp.sum(weight_kept, axis=1), 1.0
            )
            weights_low = (weight_kept / denominator[:, None]).astype(jnp.bfloat16)
            head_outputs.append(
                jnp.dot(weights_low, value_head, preferred_element_type=jnp.float32)
            )
            head_totals.append(denominator)
        outputs.append(jnp.concatenate(head_outputs, axis=0))
        totals.append(jnp.concatenate(head_totals, axis=0))
    return (jnp.concatenate(outputs, axis=1).astype(jnp.bfloat16), jnp.stack(totals))


def attention_backward(queries, key_rows, values_in, grad_attended, totals, picture, valid_token):
    row_count = queries.shape[0]
    block_rows = min(512, row_count)
    factor = HEAD_DIM ** (-0.5)
    query_grads = []
    key_grads = []
    value_grads = []
    for head_index in range(queries.shape[1] // HEAD_DIM):
        column_start = head_index * HEAD_DIM
        key_head = key_rows[:, column_start : column_start + HEAD_DIM]
        value_head = values_in[:, column_start : column_start + HEAD_DIM]
        grad_key = jnp.zeros((row_count, HEAD_DIM), jnp.float32)
        grad_value = jnp.zeros((row_count, HEAD_DIM), jnp.float32)
        head_queries = []
        for row_begin in range(0, row_count, block_rows):
            query_block = queries[
                row_begin : row_begin + block_rows, column_start : column_start + HEAD_DIM
            ]
            grad_block = grad_attended[
                row_begin : row_begin + block_rows, column_start : column_start + HEAD_DIM
            ]
            allowed = (
                picture[row_begin : row_begin + block_rows, None] == picture[None, :]
            ) & valid_token[None, :]
            scores = (
                lax.dot_general(
                    query_block, key_head, CONTRACT_COLS, preferred_element_type=jnp.float32
                )
                * factor
            )
            weight_kept = jnp.where(allowed, jnp.exp(scores), 0.0)
            probs = weight_kept / totals[head_index, row_begin : row_begin + block_rows][:, None]
            grad_probs = lax.dot_general(
                grad_block, value_head, CONTRACT_COLS, preferred_element_type=jnp.float32
            )
            delta = jnp.sum(grad_probs * probs, axis=1)
            grad_scores = (probs * (grad_probs - delta[:, None])).astype(jnp.bfloat16)
            head_queries.append(
                jnp.dot(grad_scores, key_head, preferred_element_type=jnp.float32) * factor
            )
            grad_key = (
                grad_key
                + lax.dot_general(
                    grad_scores, query_block, CONTRACT_ROWS, preferred_element_type=jnp.float32
                )
                * factor
            )
            grad_value = grad_value + lax.dot_general(
                probs.astype(jnp.bfloat16),
                grad_block,
                CONTRACT_ROWS,
                preferred_element_type=jnp.float32,
            )
        query_grads.append(jnp.concatenate(head_queries, axis=0))
        key_grads.append(grad_key)
        value_grads.append(grad_value)
    stacked = jnp.stack(
        [
            jnp.concatenate(query_grads, axis=1),
            jnp.concatenate(key_grads, axis=1),
            jnp.concatenate(value_grads, axis=1),
        ],
        axis=1,
    )
    return stacked.reshape(row_count, -1).astype(jnp.bfloat16)


def local(
    block_input,
    lengths,
    ln1_gain,
    ln1_bias,
    w_qkv,
    qv_bias,
    w_out,
    out_bias,
    ln2_gain,
    ln2_bias,
    w_up,
    up_bias,
    w_down,
    down_bias,
    cotangent,
):
    row_count = block_input.shape[2] // lax.axis_size("gy")
    stream = jnp.transpose(block_input[0]).astype(jnp.float32)
    weights = flatten_weights(
        (
            lax.all_gather(w_qkv, "dp", axis=1, tiled=True),
            lax.all_gather(w_out, "dp", axis=2, tiled=True),
            lax.all_gather(w_up, "dp", axis=1, tiled=True),
            lax.all_gather(w_down, "dp", axis=2, tiled=True),
        )
    )
    normed1, inv_std1, hidden1 = norm_forward(stream, ln1_gain[0], ln1_bias[0])
    rows_first, projected = widen(hidden1, weights[0])
    projected = projected.reshape(row_count, 3, -1)
    queries = (projected[:, 0] + qv_bias[0]).astype(jnp.bfloat16)
    key_rows = projected[:, 1].astype(jnp.bfloat16)
    values_in = (projected[:, 2] + qv_bias[1]).astype(jnp.bfloat16)
    picture, valid_token = picture_masks(lengths, row_count)
    attended, totals = attention_forward(queries, key_rows, values_in, picture, valid_token)
    rows_attended, branch = narrow(attended, weights[1])
    residual = stream + branch + out_bias[0]
    normed2, inv_std2, hidden2 = norm_forward(residual, ln2_gain[0], ln2_bias[0])
    rows_second, pre_act = widen(hidden2, weights[2])
    pre_act = pre_act + up_bias
    activated, gelu_pull = jax.vjp(gelu_tanh, pre_act)
    rows_act, mlp_out = narrow(activated.astype(jnp.bfloat16), weights[3])
    output = jnp.transpose((residual + mlp_out + down_bias[0]).astype(jnp.bfloat16))[None]
    grad_mlp = jnp.transpose(cotangent[0])
    grad_w_down, grad_act = narrow_back(grad_mlp, rows_act, weights[3])
    grad_pre = gelu_pull(grad_act)[0].astype(jnp.bfloat16)
    rows_grad_pre, grad_w_up, grad_hidden2 = widen_back(grad_pre, rows_second, weights[2])
    grad_residual = grad_mlp.astype(jnp.float32) + norm_backward(
        grad_hidden2, normed2, inv_std2, ln2_gain[0]
    )
    grad_branch = grad_residual.astype(jnp.bfloat16)
    grad_w_out, grad_attended = narrow_back(grad_branch, rows_attended, weights[1])
    grad_projected = attention_backward(
        queries,
        key_rows,
        values_in,
        grad_attended.astype(jnp.bfloat16),
        totals,
        picture,
        valid_token,
    )
    rows_grad_proj, grad_w_qkv, grad_hidden1 = widen_back(grad_projected, rows_first, weights[0])
    input_grad = grad_residual + norm_backward(grad_hidden1, normed1, inv_std1, ln1_gain[0])
    column_sums = jnp.sum(rows_grad_proj, axis=0, dtype=jnp.float32).reshape(3, -1)
    small_sums = lax.psum(
        (
            jnp.sum(grad_hidden1 * normed1, axis=0),
            jnp.sum(grad_hidden1, axis=0),
            jnp.sum(grad_branch, axis=0, dtype=jnp.float32),
            jnp.sum(grad_hidden2 * normed2, axis=0),
            jnp.sum(grad_hidden2, axis=0),
            jnp.sum(grad_mlp, axis=0, dtype=jnp.float32),
            jnp.stack([column_sums[0], column_sums[2]]),
            jnp.sum(rows_grad_pre, axis=0, dtype=jnp.float32),
        ),
        "dp",
    )
    weight_sums = (
        lax.psum_scatter(
            grad_w_qkv.reshape(1, grad_w_qkv.shape[0], 3, -1).astype(jnp.bfloat16),
            "dp",
            scatter_dimension=1,
            tiled=True,
        ).astype(jnp.float32),
        lax.psum_scatter(
            grad_w_out.reshape(grad_w_out.shape[0], 1, -1).astype(jnp.bfloat16),
            "dp",
            scatter_dimension=2,
            tiled=True,
        ).astype(jnp.float32),
        lax.psum_scatter(
            grad_w_up.reshape(1, grad_w_up.shape[0], -1).astype(jnp.bfloat16),
            "dp",
            scatter_dimension=1,
            tiled=True,
        ).astype(jnp.float32),
        lax.psum_scatter(
            grad_w_down.reshape(grad_w_down.shape[0], 1, -1).astype(jnp.bfloat16),
            "dp",
            scatter_dimension=2,
            tiled=True,
        ).astype(jnp.float32),
    )
    return (
        output,
        jnp.transpose(input_grad)[None],
        small_sums[0][None],
        small_sums[1][None],
        weight_sums[0],
        small_sums[6],
        weight_sums[1],
        small_sums[2][None],
        small_sums[3][None],
        small_sums[4][None],
        weight_sums[2],
        small_sums[7],
        weight_sums[3],
        small_sums[5][None],
    )


def solution(mesh):
    in_specs = (
        P("gy", "gx", "dp"),
        P(("dp", "gy"), None),
        P("gy", "gx"),
        P("gy", "gx"),
        P("gy", "dp", None, "gx"),
        P(None, "gx"),
        P("gx", "gy", "dp"),
        P("gy", "gx"),
        P("gy", "gx"),
        P("gy", "gx"),
        P("gy", "dp", "gx"),
        P("gx"),
        P("gx", "gy", "dp"),
        P("gy", "gx"),
        P("gy", "gx", "dp"),
    )
    out_specs = (
        P("gy", "gx", "dp"),
        P("gy", "gx", "dp"),
        P("gy", "gx"),
        P("gy", "gx"),
        P("gy", "dp", None, "gx"),
        P(None, "gx"),
        P("gx", "gy", "dp"),
        P("gy", "gx"),
        P("gy", "gx"),
        P("gy", "gx"),
        P("gy", "dp", "gx"),
        P("gx"),
        P("gx", "gy", "dp"),
        P("gy", "gx"),
    )
    return jax.shard_map(local, mesh=mesh, in_specs=in_specs, out_specs=out_specs, check_vma=False)
```

profile of v0, /device:TPU:0, one launch (start us, length us, event | category | flops | bytes accessed | tf_op | source)
XLA Modules:
  0.0 761.8 jit_solution(13659487487546985812)
XLA Ops:
  10.5 25.5 %all-reduce.3 = (f32[2048]{0:T(1024)S(1)}, f32[2048]{0:T(1024)S(1)}) all-reduce(f32[2048]{0:T(1024)S(1)} %fusion.33, f32[2048]{0:T(1024)S(1)} %convert_reduce_fusion.3), channel_id=1, replica_groups=mesh['dp'=4,'gx'=4,'gy'=2] {'gx','gy'}, use_global_device_ids=true, to_apply=%region_5.0 | all-reduce | flops 4096 | bytes 32768 | tf_op jit(solution)/shard_map/psum | solution.py:30
  38.3 25.7 %all_gather.37 = bf16[1,576,3,288]{3,1,2,0:T(8,128)(2,1)S(1)} all-gather(bf16[1,144,3,288]{3,1,2,0:T(8,128)(2,1)S(1)} %copy-done.26), channel_id=1, replica_groups=mesh['dp'=4,'gx'=4,'gy'=2] {'dp'}, dimensions={1}, use_global_device_ids=true | all-gather | bytes 1244160 | tf_op jit(solution)/shard_map/all_gather | solution.py:231
  65.1 10.1 %all-gather.11.cloned.1.call-done = bf16[2048,576]{0,1:T(8,128)(2,1)} async-done(((bf16[2048,144]{0,1:T(8,128)(2,1)}), bf16[2048,576]{0,1:T(8,128)(2,1)}) %all-gather.11.cloned.1.call-update) | async-done | bytes 2359312 | tf_op jit(solution)/shard_map/all_gather | solution.py:49
  83.9 12.6 %reduce-scatter.17.cloned.1.call-done = f32[1024,864]{0,1:T(8,128)} async-done(((f32[2048,864]{0,1:T(8,128)}), f32[1024,864]{0,1:T(8,128)}) %reduce-scatter.17.cloned.1.call-update) | async-done | bytes 3538960 | tf_op jit(solution)/shard_map/reduce_scatter | solution.py:52
  112.4 15.4 %all_gather.39 = bf16[288,1,576]{0,2,1:T(8,128)(2,1)S(1)} all-gather(bf16[288,1,144]{0,2,1:T(8,128)(2,1)S(1)} %copy-done.31), channel_id=1, replica_groups=mesh['dp'=4,'gx'=4,'gy'=2] {'dp'}, dimensions={2}, use_global_device_ids=true | all-gather | bytes 414720 | tf_op jit(solution)/shard_map/all_gather | solution.py:232
  134.6 37.5 %reduce-scatter.19.cloned.1.call-done = bf16[2048,144]{0,1:T(8,128)(2,1)} async-done(((bf16[2048,576]{0,1:T(8,128)(2,1)}), bf16[2048,144]{0,1:T(8,128)(2,1)}) %reduce-scatter.19.cloned.1.call-update) | async-done | bytes 589840 | tf_op jit(solution)/shard_map/reduce_scatter | solution.py:66
  173.4 24.4 %all-reduce.2 = (f32[2048]{0:T(1024)S(1)}, f32[2048]{0:T(1024)S(1)}) all-reduce(f32[2048]{0:T(1024)S(1)} %get-tuple-element.77, f32[2048]{0:T(1024)S(1)} %get-tuple-element.76), channel_id=1, replica_groups=mesh['dp'=4,'gx'=4,'gy'=2] {'gx','gy'}, use_global_device_ids=true, to_apply=%region_19.20 | all-reduce | flops 4096 | bytes 32768 | tf_op jit(solution)/shard_map/psum | solution.py:30
  207.4 9.1 %fusion.12 = f32[2048,1076]{0,1:T(8,128)} fusion(bf16[2048,576]{0,1:T(8,128)(2,1)} %all-gather.23.cloned.1.call-done, bf16[1076,1,576]{0,2,1:T(8,128)(2,1)} %all-gather.21.cloned.1.call-done), kind=kOutput, calls=%fused_computation.61 | convolution fusion | flops 2538602496 | bytes 12413440 | tf_op jit(solution)/shard_map/dot_general | solution.py:80
  216.6 24.9 %all-gather.17.cloned.1.call-done = bf16[1,576,1076]{2,1,0:T(8,128)(2,1)} async-done(((bf16[1,144,1076]{2,1,0:T(8,128)(2,1)}), bf16[1,576,1076]{2,1,0:T(8,128)(2,1)}) %all-gather.17.cloned.1.call-update) | async-done | bytes 1239568 | tf_op jit(solution)/shard_map/all_gather | solution.py:233
  241.5 38.8 %all-gather.15.cloned.1.call-done = bf16[2048,576]{0,1:T(8,128)(2,1)} async-done(((bf16[2048,144]{0,1:T(8,128)(2,1)}), bf16[2048,576]{0,1:T(8,128)(2,1)}) %all-gather.15.cloned.1.call-update) | async-done | bytes 2359312 | tf_op jit(solution)/shard_map/all_gather | solution.py:49
  280.4 9.1 %fusion.17 = f32[2048,1076]{0,1:T(8,128)} fusion(bf16[2048,576]{0,1:T(8,128)(2,1)} %all-gather.15.cloned.1.call-done, bf16[1,576,1076]{2,1,0:T(8,128)(2,1)} %all-gather.17.cloned.1.call-done), kind=kOutput, calls=%fused_computation.66 | convolution fusion | flops 2538602496 | bytes 12413440 | tf_op jit(solution)/shard_map/dot_general | solution.py:53
  289.6 16.7 %reduce-scatter.21.cloned.1.call-done = f32[1024,1076]{0,1:T(8,128)} async-done(((f32[2048,1076]{0,1:T(8,128)}), f32[1024,1076]{0,1:T(8,128)}) %reduce-scatter.21.cloned.1.call-update) | async-done | bytes 4407312 | tf_op jit(solution)/shard_map/reduce_scatter | solution.py:52
  313.6 15.4 %all-gather.25.cloned.1.call-done = bf16[2048,1076]{0,1:T(8,128)(2,1)} async-done(((bf16[1024,1076]{0,1:T(8,128)(2,1)}), bf16[2048,1076]{0,1:T(8,128)(2,1)}) %all-gather.25.cloned.1.call-update) | async-done | bytes 4407312 | tf_op jit(solution)/shard_map/all_gather | solution.py:89
  336.2 58.1 %reduce-scatter.27.cloned.1.call-done = f32[2048,144]{0,1:T(8,128)} async-done(((f32[2048,576]{0,1:T(8,128)}), f32[2048,144]{0,1:T(8,128)}) %reduce-scatter.27.cloned.1.call-update) | async-done | bytes 1179664 | tf_op jit(solution)/shard_map/reduce_scatter | solution.py:94
  397.0 23.5 %all-reduce.1 = (f32[2048]{0:T(1024)}, f32[2048]{0:T(1024)}) all-reduce(f32[2048]{0:T(1024)} %get-tuple-element.71, f32[2048]{0:T(1024)} %get-tuple-element.75), channel_id=1, replica_groups=mesh['dp'=4,'gx'=4,'gy'=2] {'gx','gy'}, use_global_device_ids=true, to_apply=%region_27.28 | all-reduce | flops 4096 | bytes 32768 | tf_op jit(solution)/shard_map/psum | solution.py:40
  424.6 37.9 %all-gather.27.cloned.1.call-done = bf16[2048,576]{0,1:T(8,128)(2,1)} async-done(((bf16[2048,144]{0,1:T(8,128)(2,1)}), bf16[2048,576]{0,1:T(8,128)(2,1)}) %all-gather.27.cloned.1.call-update) | async-done | bytes 2359312 | tf_op jit(solution)/shard_map/all_gather | solution.py:73
  515.1 8.2 %fusion.7 = bf16[1,576,1076]{2,1,0:T(8,128)(2,1)} fusion(bf16[2048,576]{0,1:T(8,128)(2,1)} %all-gather.15.cloned.1.call-done, bf16[2048,1076]{0,1:T(8,128)(2,1)} %all-gather.25.cloned.1.call-done), kind=kOutput, calls=%fused_computation.16 | convolution fusion | flops 2539222272 | bytes 8006144 | tf_op jit(solution)/shard_map/dot_general | solution.py:90
  568.0 12.9 %reduce-scatter.33.cloned.1.call-done = bf16[1,144,1076]{2,1,0:T(8,128)(2,1)} async-done(((bf16[1,576,1076]{2,1,0:T(8,128)(2,1)}), bf16[1,144,1076]{2,1,0:T(8,128)(2,1)}) %reduce-scatter.33.cloned.1.call-update) | async-done | bytes 309904 | tf_op jit(solution)/shard_map/reduce_scatter | solution.py:300
  582.7 20.8 %reduce-scatter.39.cloned.1.call-done = bf16[144,288]{1,0:T(8,128)(2,1)} async-done(((bf16[576,288]{1,0:T(8,128)(2,1)}), bf16[144,288]{1,0:T(8,128)(2,1)}) %reduce-scatter.39.cloned.1.call-update) | async-done | bytes 82960
  608.2 23.1 %reduce-scatter.37.cloned.1.call-done = bf16[144,864]{1,0:T(8,128)(2,1)} async-done(((bf16[576,864]{1,0:T(8,128)(2,1)}), bf16[144,864]{1,0:T(8,128)(2,1)}) %reduce-scatter.37.cloned.1.call-update) | async-done | bytes 248848
  635.9 53.6 %reduce-scatter.31.cloned.1.call-done = f32[2048,144]{0,1:T(8,128)} async-done(((f32[2048,576]{0,1:T(8,128)}), f32[2048,144]{0,1:T(8,128)}) %reduce-scatter.31.cloned.1.call-update) | async-done | bytes 1179664 | tf_op jit(solution)/shard_map/reduce_scatter | solution.py:94
  691.3 23.8 %all-reduce = (f32[2048]{0:T(1024)S(1)}, f32[2048]{0:T(1024)S(1)}) all-reduce(f32[2048]{0:T(1024)S(1)} %get-tuple-element.73, f32[2048]{0:T(1024)S(1)} %get-tuple-element.74), channel_id=1, replica_groups=mesh['dp'=4,'gx'=4,'gy'=2] {'gx','gy'}, use_global_device_ids=true, to_apply=%region_41.42 | all-reduce | flops 4096 | bytes 32768 | tf_op jit(solution)/shard_map/psum | solution.py:40
  715.1 15.1 %reduce-scatter.23.cloned.1.call-done = bf16[2048,144]{0,1:T(8,128)(2,1)} async-done(((bf16[2048,576]{0,1:T(8,128)(2,1)}), bf16[2048,144]{0,1:T(8,128)(2,1)}) %reduce-scatter.23.cloned.1.call-update) | async-done | bytes 589840 | tf_op jit(solution)/shard_map/reduce_scatter | solution.py:66
  734.3 19.6 %all-reduce.4 = (f32[1,144]{1,0:T(1,128)}, f32[1,144]{1,0:T(1,128)}, f32[2,288]{1,0:T(2,128)}, f32[1,144]{1,0:T(1,128)}, f32[1,144]{1,0:T(1,128)}, /*index=5*/f3...) all-reduce(f32[1,144]{1,0:T(1,128)S(1)} %bitcast.245, ...), channel_id=1, replica_groups=mesh['dp'=4,'gx'=4,'gy'=2] {'dp'}, use_global_device_ids=true, to_apply=%region_43.44 | all-reduce | flops 2516 | bytes 20128 | tf_op jit(solution)/shard_map/psum | solution.py:274
  (305 shorter events, 182.8 us)
Async XLA Ops:
  8.0 67.1 %all-gather.11.cloned.1.call-start = ((), (), s32[]{:S(2)}) async-start(), calls=%async_computation.12 | async-start | bytes 2949120 | tf_op jit(solution)/shard_map/all_gather | solution.py:49
  38.3 58.2 %reduce-scatter.17.cloned.1.call-start = ((), (), s32[]{:S(2)}) async-start(), calls=%async_computation.13 | async-start | bytes 10616832 | tf_op jit(solution)/shard_map/reduce_scatter | solution.py:52
  81.7 46.1 %all-gather.13.cloned.1.call-start = ((), (), s32[]{:S(2)}) async-start(), calls=%async_computation.14 | async-start | bytes 1769472 | tf_op jit(solution)/shard_map/all_gather | solution.py:62
  112.4 59.7 %reduce-scatter.19.cloned.1.call-start = ((), (), s32[]{:S(2)}) async-start(), calls=%async_computation.15 | async-start | bytes 2949120 | tf_op jit(solution)/shard_map/reduce_scatter | solution.py:66
  132.8 67.5 %all-gather.21.cloned.1.call-start = ((), (), s32[]{:S(2)}) async-start(), calls=%async_computation.20 | async-start | bytes 1658880 | tf_op jit(solution)/shard_map/all_gather | solution.py:234
  133.3 74.1 %all-gather.23.cloned.1.call-start = ((), (), s32[]{:S(2)}) async-start(), calls=%async_computation.22 | async-start | bytes 2949120 | tf_op jit(solution)/shard_map/all_gather | solution.py:73
  133.9 107.6 %all-gather.17.cloned.1.call-start = ((), (), s32[]{:S(2)}) async-start(), calls=%async_computation.17 | async-start | bytes 1658880 | tf_op jit(solution)/shard_map/all_gather | solution.py:233
  134.5 145.9 %all-gather.15.cloned.1.call-start = ((), (), s32[]{:S(2)}) async-start(), calls=%async_computation.16 | async-start | bytes 2949120 | tf_op jit(solution)/shard_map/all_gather | solution.py:49
  200.2 89.4 %reduce-scatter.25.cloned.1.call-start = ((), (), s32[]{:S(2)}) async-start(), calls=%async_computation.23 | async-start | bytes 13271040 | tf_op jit(solution)/shard_map/reduce_scatter | solution.py:79
  216.5 89.7 %reduce-scatter.21.cloned.1.call-start = ((), (), s32[]{:S(2)}) async-start(), calls=%async_computation.18 | async-start | bytes 13271040 | tf_op jit(solution)/shard_map/reduce_scatter | solution.py:52
  289.5 39.5 %all-gather.25.cloned.1.call-start = ((), (), s32[]{:S(2)}) async-start(), calls=%async_computation.24 | async-start | bytes 6635520 | tf_op jit(solution)/shard_map/all_gather | solution.py:89
  313.6 80.7 %reduce-scatter.27.cloned.1.call-start = ((), (), s32[]{:S(2)}) async-start(), calls=%async_computation.25 | async-start | bytes 5898240 | tf_op jit(solution)/shard_map/reduce_scatter | solution.py:94
  336.1 126.4 %all-gather.27.cloned.1.call-start = ((), (), s32[]{:S(2)}) async-start(), calls=%async_computation.26 | async-start | bytes 2949120 | tf_op jit(solution)/shard_map/all_gather | solution.py:73
  424.6 52.3 %reduce-scatter.29.cloned.1.call-start = ((), (), s32[]{:S(2)}) async-start(), calls=%async_computation.27 | async-start | bytes 3538944 | tf_op jit(solution)/shard_map/reduce_scatter | solution.py:79
  466.8 40.9 %all-gather.19.cloned.1.call-start = ((), (), s32[]{:S(2)}) async-start(), calls=%async_computation.19 | async-start | bytes 6635520 | tf_op jit(solution)/shard_map/all_gather | solution.py:62
  470.6 60.1 %all-gather.29.cloned.1.call-start = ((), (), s32[]{:S(2)}) async-start(), calls=%async_computation.28 | async-start | bytes 5308416 | tf_op jit(solution)/shard_map/all_gather | solution.py:89
  507.6 58.5 %reduce-scatter.35.cloned.1.call-start = ((), (), s32[]{:S(2)}) async-start(), calls=%async_computation.31 | async-start | bytes 1658880 | tf_op jit(solution)/shard_map/reduce_scatter | solution.py:306
  515.1 65.8 %reduce-scatter.33.cloned.1.call-start = ((), (), s32[]{:S(2)}) async-start(), calls=%async_computation.30 | async-start | bytes 1658880 | tf_op jit(solution)/shard_map/reduce_scatter | solution.py:300
  523.3 80.2 %reduce-scatter.39.cloned.1.call-start = ((), (), s32[]{:S(2)}) async-start(), calls=%async_computation.33 | async-start | bytes 552960
  530.6 100.7 %reduce-scatter.37.cloned.1.call-start = ((), (), s32[]{:S(2)}) async-start(), calls=%async_computation.32 | async-start | bytes 1290240
  548.4 141.1 %reduce-scatter.31.cloned.1.call-start = ((), (), s32[]{:S(2)}) async-start(), calls=%async_computation.29 | async-start | bytes 5898240 | tf_op jit(solution)/shard_map/reduce_scatter | solution.py:94
  555.8 174.5 %reduce-scatter.23.cloned.1.call-start = ((), (), s32[]{:S(2)}) async-start(), calls=%async_computation.21 | async-start | bytes 2949120 | tf_op jit(solution)/shard_map/reduce_scatter | solution.py:66
  633.5 96.8 %copy-start.35 = (f32[2048]{0:T(1024)S(1)}, f32[2048]{0:T(1024)}, u32[]{:S(2)}) copy-start(f32[2048]{0:T(1024)} %copy-done.34) | copy-start | bytes 24580
  633.5 96.8 %copy-start.37 = (f32[1,144]{1,0:T(1,128)S(1)}, f32[1,144]{1,0:T(1,128)}, u32[]{:S(2)}) copy-start(f32[1,144]{1,0:T(1,128)} %param.22) | copy-start | bytes 1732
  (64 other events, 1126.6 us)
Sparse Core Ops, SparseCore 0:
  38.4 36.6 all-gather.10
  81.9 14.5 reduce-scatter.16
  112.5 10.5 all-gather.12
  132.9 39.1 reduce-scatter.18
  216.7 16.5 reduce-scatter.24
  289.6 16.5 reduce-scatter.20
  313.7 15.2 all-gather.24
  466.9 9.9 reduce-scatter.28
  478.4 15.2 all-gather.18
  507.7 13.9 all-gather.28
Sparse Core Ops, SparseCore 1:
  134.8 34.3 all-gather.20
  170.9 36.5 all-gather.22
  208.9 32.6 all-gather.16
  244.0 36.4 all-gather.14
  336.2 58.0 reduce-scatter.26
  424.6 37.8 all-gather.26
  515.2 33.0 reduce-scatter.34
  550.4 30.4 reduce-scatter.32
  583.6 19.9 reduce-scatter.38
  605.9 25.3 reduce-scatter.36
  634.1 55.3 reduce-scatter.30
  692.6 37.6 reduce-scatter.22
where the time goes:
time: 766 us; the launch traced here: 762 us
  waiting for transfers between devices  393 us (51%)
  blocking collectives  158 us (21%)
  matrix products  107 us (14%)
  other arithmetic  47.4 us (6%)
  local copies, waits for them, and re-layouts  38.2 us (5%)
  between operations  17.2 us (2%)
    reduce_scatter x2, waiting for transfers between devices, widen_back(): lax.psum_scatter(product, 'gx', scatter_dimension=1, tiled=True)  112 us
    reduce_scatter x2, waiting for transfers between devices, narrow(): lax.psum_scatter(product.astype(jnp.bfloat16), 'gx', scatter_dimension=1,...  52.6 us
    psum x2, blocking collectives, norm_forward(): lax.psum((jnp.sum(stream, axis=1), jnp.sum(stream * stream, axis=1)), ('g...  49.9 us
    all_gather x2, waiting for transfers between devices, widen(): gathered = lax.all_gather(hidden, 'gx', axis=1, tiled=True)  48.9 us
    psum x2, blocking collectives, norm_backward(): lax.psum((jnp.sum(grad_normed, axis=1), jnp.sum(grad_normed * normed, axi...  47.4 us
    unnamed x24, waiting for transfers between devices  45.8 us
    all_gather x2, waiting for transfers between devices, narrow_back(): gathered = lax.all_gather(grad_stream, 'gx', axis=1, tiled=True)  45.1 us
    unnamed x142, local copies, waits for them, and re-layouts  30.4 us
  transfers between devices with their start and end apart: 22, of which 16 were waited for; matrix products, arithmetic and copies ran while one was open for 16% of the time, Pallas kernels for 0%

commit v1 on v0

v1 whole, which is shorter than its diff:
```python
import functools

import jax
import jax.numpy as jnp
from jax import lax
from jax.experimental import pallas as pl
from jax.experimental.pallas import tpu as pltpu
from jax.sharding import PartitionSpec as P

HEAD_DIM = 72
HEAD_PAD = 80
EPSILON = 1e-06
MESH = pl.DeviceIdType.MESH
BF16 = jnp.bfloat16
F32 = jnp.float32
NN = (((1,), (0,)), ((), ()))
NT = (((1,), (1,)), ((), ()))
TN = (((0,), (0,)), ((), ()))
GELU_A = 0.044715
GELU_C = 0.7978845608028654


def mm(a, b, dims):
    return lax.dot_general(a, b, dims, preferred_element_type=F32)


def round_up(value, unit):
    return (value + unit - 1) // unit * unit


def block_kernel(
    cfg,
    len_ref,
    prm_ref,
    x_ref,
    cot_ref,
    wq_in,
    wo_in,
    wu_in,
    wd_in,
    qb_ref,
    ub_ref,
    out_ref,
    ig_ref,
    dq_out,
    do_out,
    du_out,
    dd_out,
    sm_out,
    prm_all,
    prm_col,
    x_t,
    cot_t,
    h1_t,
    h2_t,
    gb_t,
    wq,
    wo,
    wu,
    wd,
    qkv_t,
    att_t,
    gatt_t,
    act_t,
    gpre_t,
    resid,
    tsend,
    trecv,
    mrecv,
    grecv,
    dk_acc,
    dv_acc,
    fa,
    fb,
    pk,
    rows_f,
    sums_col,
    uv_send,
    uv_recv,
    sm_send,
    sm_recv,
    smz_recv,
    cq,
    co,
    cu,
    cd,
    zq,
    zo,
    zu,
    zd,
    sem_s,
    sem_r,
):
    nz, zin = cfg["nz"], cfg["zin"]
    fb_rows, tok, heads = cfg["fb"], cfg["tok"], cfg["heads"]
    half, width = 4 * fb_rows, 8 * fb_rows
    tb = tok // 4
    hp = heads * HEAD_PAD
    factor = HEAD_DIM ** (-0.5)
    z, g, c = lax.axis_index("dp"), lax.axis_index("gx"), lax.axis_index("gy")
    g_hi, g_lo = g // 2, g % 2

    def gx_of(dd):
        return ((g_hi + dd // 2) % 2) * 2 + (g_lo + dd % 2) % 2

    def row_of(dc):
        return (c + dc) % 2

    counter = [0]

    def take(count):
        first = counter[0]
        counter[0] += count
        return first

    def rcopy(src, dst, sem, dev):
        return pltpu.make_async_remote_copy(
            src_ref=src,
            dst_ref=dst,
            send_sem=sem_s.at[sem],
            recv_sem=sem_r.at[sem],
            device_id=dev,
            device_id_type=MESH,
        )

    def lcopy(src, dst, sem):
        return pltpu.make_async_copy(src, dst, sem_r.at[sem])

    others = [(dd, dc) for dd in (1, 2, 3, 0) for dc in (0, 1) if dd or dc]

    def feat(dd, dc):
        return pl.ds(pl.multiple_of(row_of(dc) * half + gx_of(dd) * fb_rows, 16), fb_rows)

    def toks(j):
        return pl.ds(pl.multiple_of(j * tb, 128), tb)

    pending = []

    barrier = pltpu.get_barrier_semaphore()
    for dd, dc in others:
        pl.semaphore_signal(barrier, inc=1, device_id=(z, gx_of(dd), row_of(dc)), device_id_type=MESH)
    for k in range(1, nz):
        pl.semaphore_signal(barrier, inc=1, device_id=((z + k) % nz, g, c), device_id_type=MESH)
    pl.semaphore_wait(barrier, 7 + nz - 1)

    own_feat = feat(0, 0)

    p0 = take(8)
    xs0 = take(8)
    cs0 = take(8)
    me = c * 4 + g

    def exchange(first, src_of, dst, start=True):
        copies = {}
        for dd, dc in others:
            cp = rcopy(src_of(dd, dc), dst, first + dd * 2 + dc, (z, gx_of(dd), row_of(dc)))
            cp.start()
            copies[(dd, dc)] = cp
            pending.append(cp)
        return copies

    cp_prm = exchange(p0, lambda dd, dc: prm_ref, prm_all.at[me])

    def row_tok(dc):
        return pl.ds(pl.multiple_of(row_of(dc) * tok, 128), tok)

    exchange(xs0, lambda dd, dc: x_ref.at[:, row_tok(dc)], x_t.at[own_feat, :])
    own_x = lcopy(x_ref.at[:, row_tok(0)], x_t.at[own_feat, :], xs0)
    own_x.start()
    own_prm = lcopy(prm_ref, prm_all.at[me], p0)
    own_prm.start()

    weights = ((wq_in, wq), (wo_in, wo), (wu_in, wu), (wd_in, wd))
    wz0 = take(4 * nz)
    wc0 = take(4 * nz)

    def zrows(zz, core):
        return pl.ds(pl.multiple_of(core * half + zz * fb_rows, 16), fb_rows)

    partner = (z, g, 1 - c)
    if zin:
        for i, (src, dst) in enumerate(weights):
            for k in range(1, nz):
                cp = rcopy(src, dst.at[zrows(z, c), :], wz0 + i * nz + k, ((z + k) % nz, g, c))
                cp.start()
                pending.append(cp)
            lcopy(src, dst.at[zrows(z, c), :], wz0 + i * nz).start()
            cp = rcopy(src, dst.at[zrows(z, c), :], wc0 + i * nz, partner)
            cp.start()
            pending.append(cp)
    else:
        for i, (src, dst) in enumerate(weights):
            lcopy(src, dst, wz0 + i * nz).start()

    passed = [[], [], [], []]

    def weight_passed(i):
        for cp in passed[i]:
            cp.wait_send()

    def weight_ready(i):
        src, dst = weights[i]
        if not zin:
            lcopy(src, dst, wz0 + i * nz).wait()
            return
        for k in range(1, nz):
            zz = (z + nz - k) % nz
            rows = dst.at[zrows(zz, c), :]
            rcopy(src, rows, wz0 + i * nz + k, partner).wait_recv()
            cp = rcopy(rows, rows, wc0 + i * nz + k, partner)
            cp.start()
            passed[i].append(cp)
        lcopy(src, dst.at[zrows(z, c), :], wz0 + i * nz).wait()
        for k in range(nz):
            zz = (z + nz - k) % nz
            rcopy(src, dst.at[zrows(zz, 1 - c), :], wc0 + i * nz + k, partner).wait_recv()

    exchange(cs0, lambda dd, dc: cot_ref.at[:, row_tok(dc)], cot_t.at[own_feat, :])
    own_cot = lcopy(cot_ref.at[:, row_tok(0)], cot_t.at[own_feat, :], cs0)
    own_cot.start()

    def wait_feat(first, src, dst, own):
        own.wait()
        for dd, dc in others:
            rcopy(src.at[:, row_tok(0)], dst.at[feat(dd, dc), :], first + dd * 2 + dc, partner).wait_recv()

    ends = []
    total = len_ref[0, 0]
    ends.append(total)
    for s in range(1, len_ref.shape[1]):
        total = total + len_ref[0, s]
        ends.append(total)

    def pictures(pos):
        picture = jnp.zeros_like(pos)
        for end in ends:
            picture = picture + jnp.where(pos >= end, 1, 0)
        return picture

    pos_col = lax.broadcasted_iota(jnp.int32, (tok, 128), 0)
    pk[...] = jnp.where(pos_col < total, pictures(pos_col), -1)
    pos_row = lax.broadcasted_iota(jnp.int32, (8, tok), 1)
    pic_row = pictures(pos_row)
    rows_f[0, :, :] = pic_row.astype(F32)
    rows_f[1, :, :] = jnp.where(pos_row < total, 1.0, 0.0)
    sums_col[...] = jnp.zeros_like(sums_col)
    att_t[...] = jnp.zeros_like(att_t)

    own_prm.wait()
    for dd, dc in others:
        rcopy(prm_ref, prm_all.at[row_of(dc) * 4 + gx_of(dd)], p0 + dd * 2 + dc, partner).wait_recv()
    for b in range(8):
        rows = jnp.concatenate([prm_all[b], jnp.zeros((120, 256), F32)], axis=0)
        prm_col[b * fb_rows : (b + 1) * fb_rows, :] = jnp.transpose(rows)[:fb_rows, :]

    def par(k):
        return prm_col[:, k : k + 1]

    wait_feat(xs0, x_ref, x_t, own_x)

    def ln1(j, carry):
        t = toks(j)
        x = x_t[:, t].astype(F32)
        m = jnp.sum(x, axis=0, keepdims=True) * (1.0 / width)
        q = jnp.sum(x * x, axis=0, keepdims=True) * (1.0 / width)
        r = lax.rsqrt(q - m * m + EPSILON)
        rows_f[2, 0:1, t] = m
        rows_f[3, 0:1, t] = r
        h1_t[:, t] = ((x - m) * r * par(0) + par(1)).astype(BF16)
        return carry

    lax.fori_loop(0, 4, ln1, 0)

    weight_ready(0)

    def project(j, carry):
        t = toks(j)
        qkv_t[:, t] = (mm(wq[...], h1_t[:, t], TN) + qb_ref[...]).astype(BF16)
        return carry

    lax.fori_loop(0, 4, project, 0)

    def head_rows(part, h):
        return pl.ds(pl.multiple_of((part * heads + h) * HEAD_PAD, 16), HEAD_PAD)

    def kept_of(h, t):
        scores = mm(qkv_t[head_rows(1, h), :], qkv_t[head_rows(0, h), t], TN) * factor
        key_pic = pk[...]
        query_pic = rows_f[0, 0:1, t].astype(jnp.int32)
        allowed = jnp.concatenate([key_pic] * (tb // 128), axis=1) == query_pic
        return jnp.where(allowed, jnp.exp(scores), 0.0)

    br0 = take(4)
    weight_ready(1)

    def attend(i, carry):
        dd = 3 - i
        j = gx_of(dd)
        t = toks(j)

        def head(h, inner):
            kept = kept_of(h, t)
            den = jnp.sum(kept, axis=0, keepdims=True)
            den = jnp.where(rows_f[1, 0:1, t] > 0.5, den, 1.0)
            scale = jnp.where(den > 1e30, 2.0**-40, 1.0)
            inv = 1.0 / (den * scale)
            rows_f[4 + 2 * h, 0:1, t] = scale
            rows_f[5 + 2 * h, 0:1, t] = inv
            probs = (kept * scale * inv).astype(BF16)
            att = mm(qkv_t[head_rows(2, h), :], probs, NN)
            att_t[head_rows(0, h), t] = att.astype(BF16)
            return inner

        lax.fori_loop(0, heads, head, 0)
        fa[...] = mm(wo[...], att_t[:, t], NN)
        for step in (3, 2, 1):

            @pl.when(i == 3 - step)
            def _(step=step):
                gb_t[:, t] = fa[...].astype(BF16)
                rcopy(gb_t.at[:, t], trecv.at[step - 1], br0 + step, (z, gx_of(step), c)).start()

        return carry

    lax.fori_loop(0, 4, attend, 0)

    def wait_tokens(first, step):
        rcopy(gb_t.at[:, toks(g)], trecv.at[step - 1], first + step, partner).wait_recv()

    def wait_tokens_sent(first):
        for step in (1, 2, 3):
            rcopy(gb_t.at[:, toks(gx_of(step))], trecv.at[step - 1], first + step, partner).wait_send()

    weight_ready(2)
    weight_ready(3)

    own_t = toks(g)
    for step in (3, 2, 1):
        wait_tokens(br0, step)
    residual = (
        x_t[:, own_t].astype(F32)
        + fa[...]
        + trecv[0].astype(F32)
        + trecv[1].astype(F32)
        + trecv[2].astype(F32)
        + par(2)
    )
    resid[...] = residual
    m2 = jnp.sum(residual, axis=0, keepdims=True) * (1.0 / width)
    q2 = jnp.sum(residual * residual, axis=0, keepdims=True) * (1.0 / width)
    r2 = lax.rsqrt(q2 - m2 * m2 + EPSILON)
    rows_f[2, 1:2, own_t] = m2
    rows_f[3, 1:2, own_t] = r2
    h2_t[:, own_t] = ((residual - m2) * r2 * par(3) + par(4)).astype(BF16)

    def spread(first, buf):
        copies = []
        for step in (3, 1, 2):
            cp = rcopy(buf.at[:, own_t], buf.at[:, own_t], first + step, (z, gx_of(step), c))
            cp.start()
            copies.append(cp)
        return copies

    def wait_block(first, buf, step):
        t = toks(gx_of(step))
        rcopy(buf.at[:, t], buf.at[:, t], first + step, partner).wait_recv()

    h20 = take(4)
    h2_copies = spread(h20, h2_t)
    wait_tokens_sent(br0)
    wait_feat(cs0, cot_ref, cot_t, own_cot)

    g20 = take(4)

    def mlp(i, carry):
        j = gx_of(i)
        t = toks(j)
        for step in (1, 2, 3):

            @pl.when(i == step)
            def _(step=step):
                wait_block(h20, h2_t, step)

        fa[...] = mm(wu[...], h2_t[:, t], TN) + ub_ref[...]
        fb[...] = mm(wd[...], cot_t[:, t], TN)

        def chunk(n, inner):
            rows = pl.ds(pl.multiple_of(n * 48, 16), 48)
            v = fa[rows, :]
            v2 = v * v
            th = jnp.tanh(GELU_C * (v + GELU_A * v2 * v))
            hf = 0.5 * (1.0 + th)
            act_t[rows, t] = (v * hf).astype(BF16)
            slope = hf + (0.5 * GELU_C) * v * (1.0 - th * th) * (1.0 + (3.0 * GELU_A) * v2)
            gpre_t[rows, t] = (fb[rows, :] * slope).astype(BF16)
            return inner

        lax.fori_loop(0, fa.shape[0] // 48, chunk, 0)
        fa[...] = mm(wu[...], gpre_t[:, t], NN)
        for step in (1, 2, 3):

            @pl.when(i == step)
            def _(step=step):
                tsend[step - 1] = fa[...].astype(BF16)
                rcopy(tsend.at[step - 1], trecv.at[step - 1], g20 + step, (z, gx_of(step), c)).start()

        @pl.when(i == 0)
        def _():
            gb_t[:, t] = fa[...].astype(BF16)

        return carry

    lax.fori_loop(0, 4, mlp, 0)

    lane_block = 384
    dwc0 = take(4)

    def weight_grad(i, left, right):
        weight_passed(i)
        dst = w_refs[i]
        cols = dst.shape[1]
        step_cols = lane_block if cols % lane_block == 0 else 256

        def one(n, carry):
            cs = pl.ds(pl.multiple_of(n * step_cols, 128), step_cols)
            dst[:, cs] = mm(left[...], right[pl.ds(pl.multiple_of(n * step_cols, 16), step_cols), :], NT).astype(BF16)
            return carry

        lax.fori_loop(0, cols // step_cols, one, 0)

    core_recv = (cq, co, cu, cd)
    z_recv = (zq, zo, zu, zd)
    w_refs = (wq, wo, wu, wd)
    dw_outs = (dq_out, do_out, du_out, dd_out)

    def core_half(core):
        return pl.ds(pl.multiple_of(core * half, 16), half)

    def send_core(i):
        if zin:
            cp = rcopy(w_refs[i].at[core_half(1 - c), :], core_recv[i], dwc0 + i, partner)
            cp.start()
            pending.append(cp)
        else:
            cp = lcopy(w_refs[i], dw_outs[i], dwc0 + i)
            cp.start()

    dwz0 = take(4 * nz)
    do0 = take(16)
    slots = [0]
    leaving = []

    def sum_core(i):
        if not zin:
            return
        rcopy(w_refs[i].at[core_half(c), :], core_recv[i], dwc0 + i, partner).wait_recv()
        w = w_refs[i]
        for zz in range(nz):
            rows = pl.ds(pl.multiple_of(c * half + zz * fb_rows, 16), fb_rows)
            w[rows, :] = (
                w[rows, :].astype(F32) + core_recv[i][zz * fb_rows : (zz + 1) * fb_rows, :].astype(F32)
            ).astype(BF16)
        for k in range(1, nz):
            zz = (z + k) % nz
            cp = rcopy(w.at[zrows(zz, c), :], z_recv[i].at[k - 1], dwz0 + i * nz + k, (zz, g, c))
            cp.start()
            pending.append(cp)

    def sum_z(i):
        if not zin:
            lcopy(w_refs[i], dw_outs[i], dwc0 + i).wait()
            return
        for k in range(1, nz):
            rcopy(
                w_refs[i].at[zrows(z, c), :], z_recv[i].at[k - 1], dwz0 + i * nz + k, partner
            ).wait_recv()
        cols = w_refs[i].shape[1]
        for n in range(0, cols, tb):
            size = min(tb, cols - n)
            part = w_refs[i][zrows(z, c), n : n + size].astype(F32)
            for k in range(1, nz):
                part = part + z_recv[i][k - 1, :, n : n + size].astype(F32)
            slot = slots[0]
            slots[0] += 1
            stage = (fa, fb)[slot // 8].at[(slot % 8) * fb_rows : (slot % 8 + 1) * fb_rows, 0:size]
            stage[...] = part
            cp = lcopy(stage, dw_outs[i].at[:, n : n + size], do0 + slot)
            cp.start()
            leaving.append(cp)

    weight_grad(2, h2_t, gpre_t)
    send_core(2)
    ones = jnp.ones((tok, 128), BF16)
    sums_col[0 : act_t.shape[0], 6:7] = mm(gpre_t[...], ones, NN)[:, 0:1]

    for step in (1, 2, 3):
        wait_tokens(g20, step)
    gh2 = (
        gb_t[:, own_t].astype(F32)
        + trecv[0].astype(F32)
        + trecv[1].astype(F32)
        + trecv[2].astype(F32)
    )
    m2 = rows_f[2, 1:2, own_t]
    r2 = rows_f[3, 1:2, own_t]
    normed2 = (resid[...] - m2) * r2
    gn = gh2 * par(3)
    s1 = jnp.sum(gn, axis=0, keepdims=True) * (1.0 / width)
    s2 = jnp.sum(gn * normed2, axis=0, keepdims=True) * (1.0 / width)
    cot_own = cot_t[:, own_t].astype(F32)
    g_res = cot_own + r2 * (gn - s1 - normed2 * s2)
    fb[...] = g_res
    g_low = g_res.astype(BF16)
    for cp in h2_copies:
        cp.wait_send()
    wait_tokens_sent(g20)
    gb_t[:, own_t] = g_low
    gb0 = take(4)
    gb_copies = spread(gb0, gb_t)
    sums_col[0:width, 2:3] = jnp.sum(g_low.astype(F32), axis=1, keepdims=True)
    sums_col[0:width, 3:4] = jnp.sum(gh2 * normed2, axis=1, keepdims=True)
    sums_col[0:width, 4:5] = jnp.sum(gh2, axis=1, keepdims=True)
    sums_col[0:width, 5:6] = jnp.sum(cot_own, axis=1, keepdims=True)

    def lower(j, carry):
        t = toks(j)
        h2_t[:, t] = mm(wd[...], act_t[:, t], NN).astype(BF16)
        return carry

    lax.fori_loop(0, 4, lower, 0)
    h2_t[:, own_t] = (mm(wd[...], act_t[:, own_t], NN) + resid[...] + par(5)).astype(BF16)
    resid[...] = fb[...]
    ml0 = take(8)
    gh0 = take(8)
    uv0 = take(8)

    def scatter(first, recv):
        copies = []
        for dd, dc in others:
            cp = rcopy(
                h2_t.at[feat(dd, dc), :], recv.at[dd * 2 + dc], first + dd * 2 + dc, (z, gx_of(dd), row_of(dc))
            )
            cp.start()
            copies.append(cp)
        return copies

    ml_copies = scatter(ml0, mrecv)
    keep_own = lcopy(h2_t.at[own_feat, :], mrecv.at[0], ml0)
    keep_own.start()
    sum_core(2)

    weight_grad(3, cot_t, act_t)
    send_core(3)

    dk_acc[...] = jnp.zeros_like(dk_acc)
    dv_acc[...] = jnp.zeros_like(dv_acc)

    def attend_back(i, carry):
        j = gx_of(i)
        t = toks(j)
        for step in (1, 2, 3):

            @pl.when(i == step)
            def _(step=step):
                wait_block(gb0, gb_t, step)

        gatt_t[...] = mm(wo[...], gb_t[:, t], TN)[0:hp, :].astype(BF16)

        def head(h, inner):
            kept = kept_of(h, t)
            probs = kept * rows_f[4 + 2 * h, 0:1, t] * rows_f[5 + 2 * h, 0:1, t]
            q_rows = head_rows(0, h)
            grad = gatt_t[q_rows, :]
            grad_probs = mm(qkv_t[head_rows(2, h), :], grad, TN)
            weighted = probs * grad_probs
            delta = jnp.sum(weighted, axis=0, keepdims=True)
            grad_scores = (weighted - probs * delta).astype(BF16)
            act_t[q_rows, t] = (mm(qkv_t[head_rows(1, h), :], grad_scores, NN) * factor).astype(BF16)
            dk_acc[q_rows, :] += mm(qkv_t[q_rows, t], grad_scores, NT)
            dv_acc[q_rows, :] += mm(grad, probs.astype(BF16), NT)
            return inner

        lax.fori_loop(0, heads, head, 0)
        return carry

    lax.fori_loop(0, 4, attend_back, 0)
    act_t[hp : 2 * hp, :] = (dk_acc[...] * factor).astype(BF16)
    act_t[2 * hp : 3 * hp, :] = dv_acc[...].astype(BF16)
    kq = wq.shape[1]
    act_t[3 * hp : kq, :] = jnp.zeros((kq - 3 * hp, tok), BF16)
    sums_col[0:kq, 7:8] = mm(act_t[0:kq, :], ones, NN)[:, 0:1]
    for cp in ml_copies:
        cp.wait_send()
    keep_own.wait()
    sum_core(3)

    def back1(j, carry):
        t = toks(j)
        gh1 = mm(wq[...], act_t[0:kq, t], NN)
        m = rows_f[2, 0:1, t]
        r = rows_f[3, 0:1, t]
        normed = (x_t[:, t].astype(F32) - m) * r
        gn1 = gh1 * par(0)
        prod = gh1 * normed
        sums_col[0:width, 0:1] += jnp.sum(prod, axis=1, keepdims=True)
        sums_col[0:width, 1:2] += jnp.sum(gh1, axis=1, keepdims=True)
        a1 = jnp.sum(gn1, axis=0, keepdims=True) * (1.0 / width)
        a2 = jnp.sum(gn1 * normed, axis=0, keepdims=True) * (1.0 / width)
        v = r * r * a2
        uv_send[0:1, t] = r * a1 - m * v
        uv_send[1:2, t] = v
        fa[...] = r * gn1

        @pl.when(j == g)
        def _():
            fa[...] += resid[...]

        h2_t[:, t] = fa[...].astype(BF16)
        return carry

    lax.fori_loop(0, 4, back1, 0)
    gh_copies = scatter(gh0, grecv)
    keep_grad = lcopy(h2_t.at[own_feat, :], grecv.at[0], gh0)
    keep_grad.start()
    exchange(uv0, lambda dd, dc: uv_send, uv_recv.at[me])
    keep_uv = lcopy(uv_send, uv_recv.at[me], uv0)
    keep_uv.start()

    weight_grad(0, h1_t, act_t)
    send_core(0)
    weight_grad(1, gb_t, att_t)
    send_core(1)

    sm0 = take(8)
    sz0 = take(nz)
    for n in range(0, sm_send.shape[1], 128):
        sm_send[:, n : n + 128] = jnp.transpose(sums_col[n : n + 128, :])[0:8, :]
    exchange(sm0, lambda dd, dc: sm_send, sm_recv.at[me])
    sum_core(0)
    sum_core(1)

    total_sm = sm_send[...]
    row8 = lax.broadcasted_iota(jnp.int32, total_sm.shape, 0)
    for dd, dc in others:
        rcopy(sm_send, sm_recv.at[row_of(dc) * 4 + gx_of(dd)], sm0 + dd * 2 + dc, partner).wait_recv()
        part = sm_recv[row_of(dc) * 4 + gx_of(dd)]
        total_sm = total_sm + (part if dd == 0 else jnp.where(row8 < 6, part, 0.0))
    smz_recv[0] = total_sm
    for k in range(1, nz):
        cp = rcopy(smz_recv.at[0], smz_recv.at[k], sz0 + k, ((z + k) % nz, g, c))
        cp.start()
        pending.append(cp)

    for dd, dc in others:
        rcopy(h2_t.at[own_feat, :], mrecv.at[dd * 2 + dc], ml0 + dd * 2 + dc, partner).wait_recv()
    for dc in (0, 1):
        acc = mrecv[dc].astype(F32)
        for dd in (1, 2, 3):
            acc = acc + mrecv[dd * 2 + dc].astype(F32)
        out_ref[:, row_tok(dc)] = acc.astype(BF16)

    sum_z(2)
    sum_z(3)

    keep_grad.wait()
    keep_uv.wait()
    for dd, dc in others:
        rcopy(h2_t.at[own_feat, :], grecv.at[dd * 2 + dc], gh0 + dd * 2 + dc, partner).wait_recv()
        rcopy(uv_send, uv_recv.at[row_of(dc) * 4 + gx_of(dd)], uv0 + dd * 2 + dc, partner).wait_recv()
    for dc in (0, 1):
        acc = grecv[dc].astype(F32)
        uv = uv_recv[row_of(dc) * 4 + g]
        for dd in (1, 2, 3):
            acc = acc + grecv[dd * 2 + dc].astype(F32)
            uv = uv + uv_recv[row_of(dc) * 4 + gx_of(dd)]
        x_own = x_ref[:, row_tok(dc)].astype(F32)
        ig_ref[:, row_tok(dc)] = acc - uv[0:1, :] - x_own * uv[1:2, :]

    total_z = smz_recv[0]
    for k in range(1, nz):
        rcopy(smz_recv.at[0], smz_recv.at[k], sz0 + k, partner).wait_recv()
        total_z = total_z + smz_recv[k]
    sm_out[...] = total_z
    sum_z(0)
    sum_z(1)

    for cp in leaving:
        cp.wait()
    for cp in pending + gb_copies + gh_copies:
        cp.wait_send()


def local(
    block_input,
    lengths,
    ln1_gain,
    ln1_bias,
    w_qkv,
    qv_bias,
    w_out,
    out_bias,
    ln2_gain,
    ln2_bias,
    w_up,
    up_bias,
    w_down,
    down_bias,
    cotangent,
):
    nz = lax.axis_size("dp")
    fb_rows, tok2 = block_input.shape[1], block_input.shape[2]
    tok = tok2 // 2
    width = 8 * fb_rows
    heads = w_qkv.shape[3] // HEAD_DIM
    hp = heads * HEAD_PAD
    kq, ko = round_up(3 * hp, 128), round_up(hp, 128)
    hid = w_up.shape[2]
    kh = round_up(hid, 384)
    zrow = w_qkv.shape[1]
    zin = zrow == fb_rows and nz == 4

    def pad_heads(a):
        parts = a.shape[-1] // HEAD_DIM
        a = a.reshape(a.shape[:-1] + (parts, HEAD_DIM))
        a = jnp.pad(a, [(0, 0)] * (a.ndim - 1) + [(0, HEAD_PAD - HEAD_DIM)])
        return a.reshape(a.shape[:-2] + (parts * HEAD_PAD,))

    def widen(a, cols):
        return jnp.pad(a, ((0, 0), (0, cols - a.shape[1])))

    prm = jnp.concatenate([ln1_gain, ln1_bias, out_bias, ln2_gain, ln2_bias, down_bias], axis=0)
    prm = jnp.pad(prm, ((0, 2), (0, 256 - fb_rows)))
    wq = widen(pad_heads(w_qkv[0].reshape(zrow, -1)), kq)
    wo = widen(pad_heads(jnp.transpose(w_out[:, 0, :])), ko)
    wu = widen(w_up[0], kh)
    wd = widen(jnp.transpose(w_down[:, 0, :]), kh)
    qb = jnp.concatenate([qv_bias[0:1], jnp.zeros_like(qv_bias[0:1]), qv_bias[1:2]], axis=1)
    qb = widen(pad_heads(qb), kq).reshape(kq, 1)
    ub = jnp.pad(up_bias, (0, kh - hid)).reshape(kh, 1)
    if not zin:
        wq, wo, wu, wd = (
            lax.all_gather(lax.all_gather(w, "dp", axis=0, tiled=True), "gy", axis=0, tiled=True)
            for w in (wq, wo, wu, wd)
        )

    cfg = dict(nz=nz, zin=zin, fb=fb_rows, tok=tok, heads=heads)
    tb = tok // 4
    half = width // 2
    vm = pltpu.VMEM
    n_sems = 8 * 3 + 8 * nz + 4 * 4 + 4 + 4 * nz + 8 * 4 + nz + 24
    dw_specs = [pl.BlockSpec(memory_space=pl.ANY)] * 4
    if zin:
        dw_shapes = tuple(jax.ShapeDtypeStruct((fb_rows, k), F32) for k in (kq, ko, kh, kh))
        core_shapes = [vm((half, k), BF16) for k in (kq, ko, kh, kh)]
        z_shapes = [vm((nz - 1, fb_rows, k), BF16) for k in (kq, ko, kh, kh)]
    else:
        dw_shapes = tuple(jax.ShapeDtypeStruct((width, k), BF16) for k in (kq, ko, kh, kh))
        core_shapes = [vm((16, 128), BF16)] * 4
        z_shapes = [vm((16, 128), BF16)] * 4
    scratch = [
        vm((8, 8, 256), F32),
        vm((width, 128), F32),
        vm((width, tok), BF16),
        vm((width, tok), BF16),
        vm((width, tok), BF16),
        vm((width, tok), BF16),
        vm((width, tok), BF16),
        vm((width, kq), BF16),
        vm((width, ko), BF16),
        vm((width, kh), BF16),
        vm((width, kh), BF16),
        vm((kq, tok), BF16),
        vm((ko, tok), BF16),
        vm((hp, tb), BF16),
        vm((kh, tok), BF16),
        vm((kh, tok), BF16),
        vm((width, tb), F32),
        vm((3, width, tb), BF16),
        vm((3, width, tb), BF16),
        vm((8, fb_rows, tok), BF16),
        vm((8, fb_rows, tok), BF16),
        vm((hp, tok), F32),
        vm((hp, tok), F32),
        vm((max(width, kh), tb), F32),
        vm((max(width, kh), tb), F32),
        vm((tok, 128), jnp.int32),
        vm((4 + 2 * heads, 8, tok), F32),
        vm((max(width, kh), 128), F32),
        vm((8, tok), F32),
        vm((8, 8, tok), F32),
        vm((8, max(width, kh)), F32),
        vm((8, 8, max(width, kh)), F32),
        vm((nz, 8, max(width, kh)), F32),
        *core_shapes,
        *z_shapes,
        pltpu.SemaphoreType.DMA((n_sems,)),
        pltpu.SemaphoreType.DMA((n_sems,)),
    ]
    any_spec = pl.BlockSpec(memory_space=pl.ANY)
    vmem_spec = pl.BlockSpec(memory_space=pltpu.VMEM)
    out, ig, dq, do, du, dd, sm = pl.pallas_call(
        functools.partial(block_kernel, cfg),
        out_shape=(
            jax.ShapeDtypeStruct((fb_rows, tok2), BF16),
            jax.ShapeDtypeStruct((fb_rows, tok2), F32),
            *dw_shapes,
            jax.ShapeDtypeStruct((8, max(width, kh)), F32),
        ),
        in_specs=[
            pl.BlockSpec(memory_space=pltpu.SMEM),
            vmem_spec,
            vmem_spec,
            any_spec,
            any_spec,
            any_spec,
            any_spec,
            any_spec,
            vmem_spec,
            vmem_spec,
        ],
        out_specs=(vmem_spec, vmem_spec, *dw_specs, vmem_spec),
        scratch_shapes=scratch,
        compiler_params=pltpu.CompilerParams(
            collective_id=0, has_side_effects=True, vmem_limit_bytes=67043328
        ),
        name="encoder_block",
    )(lengths, prm, block_input[0], cotangent[0], wq, wo, wu, wd, qb, ub)

    if not zin:

        def reduce(a):
            a = lax.psum_scatter(a, "gy", scatter_dimension=0, tiled=True)
            return lax.optimization_barrier(lax.psum_scatter(a, "dp", scatter_dimension=0, tiled=True)).astype(F32)

        dq, do, du, dd = reduce(dq), reduce(do), reduce(du), reduce(dd)

    def cut_heads(a):
        parts = a.shape[-1] // HEAD_PAD
        a = a.reshape(a.shape[:-1] + (parts, HEAD_PAD))[..., :HEAD_DIM]
        return a.reshape(a.shape[:-2] + (parts * HEAD_DIM,))

    mine = lax.axis_index("gy") * (width // 2) + lax.axis_index("gx") * fb_rows
    feats = lax.dynamic_slice(sm, (0, mine), (6, fb_rows))
    qkv_sum = cut_heads(sm[7:8, : 3 * hp]).reshape(3, -1)
    return (
        out[None],
        ig[None],
        feats[0:1],
        feats[1:2],
        cut_heads(dq[:, : 3 * hp]).reshape(1, zrow, 3, -1),
        jnp.stack([qkv_sum[0], qkv_sum[2]]),
        jnp.transpose(cut_heads(do[:, :hp]))[:, None, :],
        feats[2:3],
        feats[3:4],
        feats[4:5],
        du[None, :, :hid],
        sm[6, :hid],
        jnp.transpose(dd[:, :hid])[:, None, :],
        feats[5:6],
    )


def solution(mesh):
    in_specs = (
        P("gy", "gx", "dp"),
        P(("dp", "gy"), None),
        P("gy", "gx"),
        P("gy", "gx"),
        P("gy", "dp", None, "gx"),
        P(None, "gx"),
        P("gx", "gy", "dp"),
        P("gy", "gx"),
        P("gy", "gx"),
        P("gy", "gx"),
        P("gy", "dp", "gx"),
        P("gx"),
        P("gx", "gy", "dp"),
        P("gy", "gx"),
        P("gy", "gx", "dp"),
    )
    out_specs = (
        P("gy", "gx", "dp"),
        P("gy", "gx", "dp"),
        P("gy", "gx"),
        P("gy", "gx"),
        P("gy", "dp", None, "gx"),
        P(None, "gx"),
        P("gx", "gy", "dp"),
        P("gy", "gx"),
        P("gy", "gx"),
        P("gy", "gx"),
        P("gy", "dp", "gx"),
        P("gx"),
        P("gx", "gy", "dp"),
        P("gy", "gx"),
    )
    return jax.shard_map(local, mesh=mesh, in_specs=in_specs, out_specs=out_specs, check_vma=False)
```

time: 766 us -> 312 us (0.41)
  waiting for transfers between devices: 393 us -> 0 us
  Pallas kernels: 0 us -> 285 us
  blocking collectives: 158 us -> 0 us
  matrix products: 107 us -> 0 us
  other arithmetic: 47.4 us -> 0.68 us
  local copies, waits for them, and re-layouts: 38.2 us -> 20 us
  between operations: 17.2 us -> 0.81 us
    pallas_call x0 -> x1, Pallas kernels: none -> 285 us  [local(): pl.pallas_call(functools.partial(block_kernel, cfg), out_shape=(jax.Shape...]
    reduce_scatter x10 -> x0, waiting for transfers between devices: 212 us -> none  [the longest x2 112 us: widen_back(): lax.psum_scatter(product, 'gx', scatter_dimension=1, tiled=True)]
    all_gather x10 -> x0, waiting for transfers between devices: 134 us -> none  [the longest x2 48.9 us: widen(): gathered = lax.all_gather(hidden, 'gx', axis=1, tiled=True)]
    psum x5 -> x0, blocking collectives: 117 us -> none  [the longest x2 49.9 us: norm_forward(): lax.psum((jnp.sum(stream, axis=1), jnp.sum(stream * stream, axis=1)), ('g...]
    dot_general x60 -> x0, matrix products: 107 us -> none  [the longest x2 15.7 us: widen(): jnp.dot(gathered, weight, preferred_element_type=jnp.float32)]
    unnamed x24 -> x0, waiting for transfers between devices: 45.8 us -> none
    all_gather x2 -> x0, blocking collectives: 41.1 us -> none  [the longest x1 25.7 us: local(): lax.all_gather(w_qkv, 'dp', axis=1, tiled=True)]
    unnamed x142 -> x24, local copies, waits for them, and re-layouts: 30.4 us -> 4.24 us
  transfers between devices with their start and end apart: 22 -> 0, of which waited for: 16 -> 0; matrix products, arithmetic and copies ran while one was open for 16% -> 0% of each run, Pallas kernels for 0% -> 0%
where the time goes in v1:
time: 312 us; the launch traced here: 307 us
  Pallas kernels  285 us (91%)
  local copies, waits for them, and re-layouts  20 us (6%)
    pallas_call x1, Pallas kernels, local(): pl.pallas_call(functools.partial(block_kernel, cfg), out_shape=(jax.Shape...  285 us

profile of v1, /device:TPU:0, one launch (start us, length us, event | category | flops | bytes accessed | tf_op | source)
XLA Modules:
  0.0 306.7 jit_solution(8828776490625656552)
XLA Ops:
  0.6 0.8 concatenate.6
  1.4 0.6 pad.39.prm_ref
  2.0 1.2 copy.29
  3.3 0.2 copy.35
  3.5 0.7 pad.41.wq_in
  4.5 0.1 reshape.65
  4.6 0.7 pad.43.wo_in
  5.3 0.8 pad.44.wu_in
  6.1 0.8 pad.45.wd_in
  7.2 1.0 copy.31.qb_ref
  8.2 1.0 reshape.74.ub_ref
  9.3 285.2 %encoder_block.1 = (bf16[144,2048]{1,0:T(8,128)(2,1)}, f32[144,2048]{1,0:T(8,128)}, f32[144,1024]{1,0:T(8,128)}, f32[144,384]{1,0:T(8,128)}, f32[144,1152]{1,0:T...) custom-call(s32[1,6]{1,0:T(1,128)} %len_ref.1, f32[8,256]{1,0:T(8,128)} %pad.39.prm_ref, bf16[144,2048]{1,0:T(8,128)(2,1)} %bitcast.37, ...), custom_call_target="tpu_custom_call" | custom-call | tf_op jit(solution)/shard_map/encoder_block/pallas_call | solution.py:801
  294.5 1.6 fusion.2
  296.1 1.7 reshape.70
  297.8 0.5 copy.33
  298.3 1.2 copy.34
  299.5 0.8 slice_reduce_fusion.1
  300.5 0.6 pad_maximum_fusion
  301.1 0.2 reshape.72
  301.4 0.9 reshape.73
  302.2 1.1 slice_bitcast_fusion
  303.4 1.5 slice_reduce_fusion
  304.9 0.8 copy.38
  305.7 1.0 copy.39
  (36 shorter events, 0.9 us)
Async XLA Ops:
  3.2 1.0 copy-start.7
  3.3 2.0 copy-start.4
  3.5 2.6 copy-start.5
  4.3 2.6 copy-start.9
  4.5 3.7 %copy-start.8 = (f32[1076]{0:T(1024)S(1)}, f32[1076]{0:T(1024)}, u32[]{:S(2)}) copy-start(f32[1076]{0:T(1024)} %param.26) | copy-start | bytes 12916
  298.3 2.8 copy-start.6
  298.3 3.9 %copy-start.1 = (f32[144,1152]{1,0:T(8,128)S(1)}, f32[144,1152]{1,0:T(8,128)}, u32[]{:S(2)}) copy-start(f32[144,1152]{1,0:T(8,128)} %get-tuple-element.26) | copy-start | bytes 1990660
  298.3 3.9 %copy-start.2 = (f32[144,1152]{1,0:T(8,128)S(1)}, f32[144,1152]{1,0:T(8,128)}, u32[]{:S(2)}) copy-start(f32[144,1152]{1,0:T(8,128)} %get-tuple-element.27) | copy-start | bytes 1990660
  302.2 2.6 copy-start.3
  303.4 2.3 copy-start

commit v2 on v1

--- a/solution.py
+++ b/solution.py
@@ -127,6 +127,10 @@
         return pltpu.make_async_copy(src, dst, sem_r.at[sem])
 
     others = [(dd, dc) for dd in (1, 2, 3, 0) for dc in (0, 1) if dd or dc]
+    near = [(dd, dc) for dd, dc in others if dd < 3]
+
+    def dev(dd, dc):
+        return (z, gx_of(dd), row_of(dc))
 
     def feat(dd, dc):
         return pl.ds(pl.multiple_of(row_of(dc) * half + gx_of(dd) * fb_rows, 16), fb_rows)
@@ -134,95 +138,149 @@
     def toks(j):
         return pl.ds(pl.multiple_of(j * tb, 128), tb)
 
+    def row_tok(dc):
+        return pl.ds(pl.multiple_of(row_of(dc) * tok, 128), tok)
+
     pending = []
 
     barrier = pltpu.get_barrier_semaphore()
     for dd, dc in others:
-        pl.semaphore_signal(barrier, inc=1, device_id=(z, gx_of(dd), row_of(dc)), device_id_type=MESH)
+        pl.semaphore_signal(barrier, inc=1, device_id=dev(dd, dc), device_id_type=MESH)
     for k in range(1, nz):
         pl.semaphore_signal(barrier, inc=1, device_id=((z + k) % nz, g, c), device_id_type=MESH)
     pl.semaphore_wait(barrier, 7 + nz - 1)
 
     own_feat = feat(0, 0)
-
-    p0 = take(8)
-    xs0 = take(8)
-    cs0 = take(8)
+    own_t = toks(g)
+    partner = (z, g, 1 - c)
     me = c * 4 + g
-
-    def exchange(first, src_of, dst, start=True):
-        copies = {}
+    th = tok // 2
+
+    def exchange(first, src, dst):
         for dd, dc in others:
-            cp = rcopy(src_of(dd, dc), dst, first + dd * 2 + dc, (z, gx_of(dd), row_of(dc)))
-            cp.start()
-            copies[(dd, dc)] = cp
-            pending.append(cp)
-        return copies
-
-    cp_prm = exchange(p0, lambda dd, dc: prm_ref, prm_all.at[me])
-
-    def row_tok(dc):
-        return pl.ds(pl.multiple_of(row_of(dc) * tok, 128), tok)
-
-    exchange(xs0, lambda dd, dc: x_ref.at[:, row_tok(dc)], x_t.at[own_feat, :])
-    own_x = lcopy(x_ref.at[:, row_tok(0)], x_t.at[own_feat, :], xs0)
-    own_x.start()
-    own_prm = lcopy(prm_ref, prm_all.at[me], p0)
-    own_prm.start()
+            rcopy(src, dst, first + dd * 2 + dc, dev(dd, dc)).start()
+            pending.append(lambda dd=dd, dc=dc: rcopy(src, dst, first + dd * 2 + dc, dev(dd, dc)).wait_send())
+
+    def gather_start(first, src, dst):
+        for dd, dc in near:
+            rcopy(src.at[:, row_tok(dc)], dst.at[own_feat, :], first + dd * 2 + dc, dev(dd, dc)).start()
+            pending.append(
+                lambda dd=dd, dc=dc: rcopy(
+                    src.at[:, row_tok(dc)], dst.at[own_feat, :], first + dd * 2 + dc, dev(dd, dc)
+                ).wait_send()
+            )
+        lcopy(src.at[:, row_tok(0)], dst.at[own_feat, :], first).start()
+
+    def relay_ref(dst, dd, dc):
+        return dst.at[feat(dd, dc), (dd - 1) * th : dd * th]
+
+    def gather_relay(first, src, dst):
+        for dd in (1, 2):
+            for dc in (0, 1):
+                rcopy(src.at[:, row_tok(0)], dst.at[feat(dd, dc), :], first + dd * 2 + dc, partner).wait_recv()
+                part = relay_ref(dst, dd, dc)
+                rcopy(part, part, first + 6 + dd * 2 + dc, dev(3 - dd, 0)).start()
+
+    def gather_done(first, src, dst):
+        lcopy(src.at[:, row_tok(0)], dst.at[own_feat, :], first).wait()
+        rcopy(src.at[:, row_tok(0)], dst.at[feat(0, 1), :], first + 1, partner).wait_recv()
+        for dd in (1, 2):
+            for dc in (0, 1):
+                part = dst.at[feat(3, dc), (dd - 1) * th : dd * th]
+                rcopy(part, part, first + 6 + dd * 2 + dc, partner).wait_recv()
+
+    def gather_sent(first, dst):
+        for dd in (1, 2):
+            for dc in (0, 1):
+                part = relay_ref(dst, dd, dc)
+                rcopy(part, part, first + 6 + dd * 2 + dc, partner).wait_send()
 
     weights = ((wq_in, wq), (wo_in, wo), (wu_in, wu), (wd_in, wd))
-    wz0 = take(4 * nz)
-    wc0 = take(4 * nz)
+    steps = nz - 1
+    nw = nz if zin else 1
+    wz0 = take(4 * 2 * nw)
+    wc0 = take(4 * 2 * nw)
 
     def zrows(zz, core):
         return pl.ds(pl.multiple_of(core * half + zz * fb_rows, 16), fb_rows)
 
-    partner = (z, g, 1 - c)
-    if zin:
-        for i, (src, dst) in enumerate(weights):
-            for k in range(1, nz):
-                cp = rcopy(src, dst.at[zrows(z, c), :], wz0 + i * nz + k, ((z + k) % nz, g, c))
-                cp.start()
-                pending.append(cp)
-            lcopy(src, dst.at[zrows(z, c), :], wz0 + i * nz).start()
-            cp = rcopy(src, dst.at[zrows(z, c), :], wc0 + i * nz, partner)
-            cp.start()
-            pending.append(cp)
-    else:
-        for i, (src, dst) in enumerate(weights):
-            lcopy(src, dst, wz0 + i * nz).start()
-
-    passed = [[], [], [], []]
+    def w_rows(i, zz, core):
+        return weights[i][1].at[zrows(zz, core), :]
+
+    def hop(i, s, d):
+        origin = z - (s - 1) if d == 0 else z + (s - 1)
+        here = jnp.logical_and(z >= s - 1, z < nz - 1) if d == 0 else jnp.logical_and(z < nz - s + 1, z > 0)
+        to = z + 1 if d == 0 else z - 1
+        src = weights[i][0] if s == 1 else w_rows(i, origin, c)
+        return here, lambda: rcopy(src, w_rows(i, origin, c), wz0 + i * 2 * nw + s * 2 + d, (to, g, c))
+
+    def arrival(s, d):
+        return (z >= s, z - s) if d == 0 else (z < nz - s, z + s)
+
+    def z_send(i, s):
+        if not zin:
+            if s == 1:
+                lcopy(weights[i][0], weights[i][1], wz0 + i * 2 * nw).start()
+            return
+        for d in (0, 1):
+            here, make = hop(i, s, d)
+            pl.when(here)(lambda make=make: make().start())
+        if s == 1:
+            lcopy(weights[i][0], w_rows(i, z, c), wz0 + i * 2 * nw).start()
+            rcopy(weights[i][0], w_rows(i, z, c), wc0 + i * 2 * nw, partner).start()
+
+    def z_recv(i, s):
+        if not zin:
+            return
+        for d in (0, 1):
+            here, origin = arrival(s, d)
+
+            @pl.when(here)
+            def _(s=s, d=d, origin=origin):
+                rows = w_rows(i, origin, c)
+                rcopy(rows, rows, wz0 + i * 2 * nw + s * 2 + d, partner).wait_recv()
+                rcopy(rows, rows, wc0 + i * 2 * nw + s * 2 + d, partner).start()
+
+        if s < steps:
+            z_send(i, s + 1)
+
+    def weight_ready(i):
+        if not zin:
+            lcopy(weights[i][0], weights[i][1], wz0 + i * 2 * nw).wait()
+            return
+        lcopy(weights[i][0], w_rows(i, z, c), wz0 + i * 2 * nw).wait()
+        rcopy(weights[i][0], w_rows(i, z, 1 - c), wc0 + i * 2 * nw, partner).wait_recv()
+        for s in range(1, nz):
+            for d in (0, 1):
+                here, origin = arrival(s, d)
+
+                @pl.when(here)
+                def _(s=s, d=d, origin=origin):
+                    rows = w_rows(i, origin, 1 - c)
+                    rcopy(rows, rows, wc0 + i * 2 * nw + s * 2 + d, partner).wait_recv()
 
     def weight_passed(i):
-        for cp in passed[i]:
-            cp.wait_send()
-
-    def weight_ready(i):
-        src, dst = weights[i]
         if not zin:
-            lcopy(src, dst, wz0 + i * nz).wait()
             return
-        for k in range(1, nz):
-            zz = (z + nz - k) % nz
-            rows = dst.at[zrows(zz, c), :]
-            rcopy(src, rows, wz0 + i * nz + k, partner).wait_recv()
-            cp = rcopy(rows, rows, wc0 + i * nz + k, partner)
-            cp.start()
-            passed[i].append(cp)
-        lcopy(src, dst.at[zrows(z, c), :], wz0 + i * nz).wait()
-        for k in range(nz):
-            zz = (z + nz - k) % nz
-            rcopy(src, dst.at[zrows(zz, 1 - c), :], wc0 + i * nz + k, partner).wait_recv()
-
-    exchange(cs0, lambda dd, dc: cot_ref.at[:, row_tok(dc)], cot_t.at[own_feat, :])
-    own_cot = lcopy(cot_ref.at[:, row_tok(0)], cot_t.at[own_feat, :], cs0)
-    own_cot.start()
-
-    def wait_feat(first, src, dst, own):
-        own.wait()
-        for dd, dc in others:
-            rcopy(src.at[:, row_tok(0)], dst.at[feat(dd, dc), :], first + dd * 2 + dc, partner).wait_recv()
+        rcopy(weights[i][0], w_rows(i, z, c), wc0 + i * 2 * nw, partner).wait_send()
+        for s in range(1, nz):
+            for d in (0, 1):
+                here, make = hop(i, s, d)
+                pl.when(here)(lambda make=make: make().wait_send())
+                here, origin = arrival(s, d)
+
+                @pl.when(here)
+                def _(s=s, d=d, origin=origin):
+                    rows = w_rows(i, origin, c)
+                    rcopy(rows, rows, wc0 + i * 2 * nw + s * 2 + d, partner).wait_send()
+
+    p0 = take(8)
+    xs0 = take(12)
+    cs0 = take(12)
+    exchange(p0, prm_ref, prm_all.at[me])
+    lcopy(prm_ref, prm_all.at[me], p0).start()
+    gather_start(xs0, x_ref, x_t)
+    z_send(0, 1)
 
     ends = []
     total = len_ref[0, 0]
@@ -246,7 +304,7 @@
     sums_col[...] = jnp.zeros_like(sums_col)
     att_t[...] = jnp.zeros_like(att_t)
 
-    own_prm.wait()
+    lcopy(prm_ref, prm_all.at[me], p0).wait()
     for dd, dc in others:
         rcopy(prm_ref, prm_all.at[row_of(dc) * 4 + gx_of(dd)], p0 + dd * 2 + dc, partner).wait_recv()
     for b in range(8):
@@ -256,7 +314,15 @@
     def par(k):
         return prm_col[:, k : k + 1]
 
-    wait_feat(xs0, x_ref, x_t, own_x)
+    z_recv(0, 1)
+    z_send(1, 1)
+    gather_relay(xs0, x_ref, x_t)
+    gather_start(cs0, cot_ref, cot_t)
+    if steps > 1:
+        z_recv(0, 2)
+    z_recv(1, 1)
+    z_send(2, 1)
+    gather_done(xs0, x_ref, x_t)
 
     def ln1(j, carry):
         t = toks(j)
@@ -271,6 +337,10 @@
 
     lax.fori_loop(0, 4, ln1, 0)
 
+    for s in range(3, nz):
+        z_recv(0, s)
+    if steps > 1:
+        z_recv(1, 2)
     weight_ready(0)
 
     def project(j, carry):
@@ -279,6 +349,9 @@
         return carry
 
     lax.fori_loop(0, 4, project, 0)
+    z_recv(2, 1)
+    for s in range(3, nz):
+        z_recv(1, s)
 
     def head_rows(part, h):
         return pl.ds(pl.multiple_of((part * heads + h) * HEAD_PAD, 16), HEAD_PAD)
@@ -291,7 +364,6 @@
         return jnp.where(allowed, jnp.exp(scores), 0.0)
 
     br0 = take(4)
-    weight_ready(1)
 
     def attend(i, carry):
         dd = 3 - i
@@ -312,6 +384,11 @@
             return inner
 
         lax.fori_loop(0, heads, head, 0)
+
+        @pl.when(i == 0)
+        def _():
+            weight_ready(1)
+
         fa[...] = mm(wo[...], att_t[:, t], NN)
         for step in (3, 2, 1):
 
@@ -320,21 +397,28 @@
                 gb_t[:, t] = fa[...].astype(BF16)
                 rcopy(gb_t.at[:, t], trecv.at[step - 1], br0 + step, (z, gx_of(step), c)).start()
 
+        @pl.when(i == 1)
+        def _():
+            if steps > 1:
+                z_recv(2, 2)
+            z_send(3, 1)
+            gather_relay(cs0, cot_ref, cot_t)
+
         return carry
 
     lax.fori_loop(0, 4, attend, 0)
 
     def wait_tokens(first, step):
-        rcopy(gb_t.at[:, toks(g)], trecv.at[step - 1], first + step, partner).wait_recv()
+        rcopy(gb_t.at[:, own_t], trecv.at[step - 1], first + step, partner).wait_recv()
 
     def wait_tokens_sent(first):
         for step in (1, 2, 3):
             rcopy(gb_t.at[:, toks(gx_of(step))], trecv.at[step - 1], first + step, partner).wait_send()
 
-    weight_ready(2)
-    weight_ready(3)
-
-    own_t = toks(g)
+    for s in range(3, nz):
+        z_recv(2, s)
+    z_recv(3, 1)
+
     for step in (3, 2, 1):
         wait_tokens(br0, step)
     residual = (
@@ -354,32 +438,54 @@
     h2_t[:, own_t] = ((residual - m2) * r2 * par(3) + par(4)).astype(BF16)
 
     def spread(first, buf):
-        copies = []
-        for step in (3, 1, 2):
-            cp = rcopy(buf.at[:, own_t], buf.at[:, own_t], first + step, (z, gx_of(step), c))
-            cp.start()
-            copies.append(cp)
-        return copies
-
-    def wait_block(first, buf, step):
-        t = toks(gx_of(step))
-        rcopy(buf.at[:, t], buf.at[:, t], first + step, partner).wait_recv()
-
-    h20 = take(4)
-    h2_copies = spread(h20, h2_t)
+        for step in (1, 2):
+            rcopy(buf.at[:, own_t], buf.at[:, own_t], first + step, (z, gx_of(step), c)).start()
+
+    def halves(buf, step, k):
+        return buf.at[(k - 1) * half : k * half, toks(gx_of(step))]
+
+    def spread_relay(first, buf):
+        for step in (1, 2):
+            block = buf.at[:, toks(gx_of(step))]
+            rcopy(block, block, first + step, partner).wait_recv()
+            part = halves(buf, step, step)
+            rcopy(part, part, first + 2 + step, (z, gx_of(3 - step), c)).start()
+
+    def spread_done(first, buf):
+        for k in (1, 2):
+            part = halves(buf, 3, k)
+            rcopy(part, part, first + 2 + k, partner).wait_recv()
+
+    def spread_sent(first, buf):
+        for step in (1, 2):
+            rcopy(buf.at[:, own_t], buf.at[:, own_t], first + step, partner).wait_send()
+            part = halves(buf, step, step)
+            rcopy(part, part, first + 2 + step, partner).wait_send()
+
+    h20 = take(5)
+    spread(h20, h2_t)
     wait_tokens_sent(br0)
-    wait_feat(cs0, cot_ref, cot_t, own_cot)
+    weight_ready(2)
+    if steps > 1:
+        z_recv(3, 2)
+    gather_done(cs0, cot_ref, cot_t)
 
     g20 = take(4)
 
     def mlp(i, carry):
-        j = gx_of(i)
-        t = toks(j)
-        for step in (1, 2, 3):
-
-            @pl.when(i == step)
-            def _(step=step):
-                wait_block(h20, h2_t, step)
+        dd = (i + 1) % 4
+        t = toks(gx_of(dd))
+
+        @pl.when(i == 0)
+        def _():
+            spread_relay(h20, h2_t)
+            for s in range(3, nz):
+                z_recv(3, s)
+            weight_ready(3)
+
+        @pl.when(i == 2)
+        def _():
+            spread_done(h20, h2_t)
 
         fa[...] = mm(wu[...], h2_t[:, t], TN) + ub_ref[...]
         fb[...] = mm(wd[...], cot_t[:, t], TN)
@@ -388,10 +494,10 @@
             rows = pl.ds(pl.multiple_of(n * 48, 16), 48)
             v = fa[rows, :]
             v2 = v * v
-            th = jnp.tanh(GELU_C * (v + GELU_A * v2 * v))
-            hf = 0.5 * (1.0 + th)
+            thv = jnp.tanh(GELU_C * (v + GELU_A * v2 * v))
+            hf = 0.5 * (1.0 + thv)
             act_t[rows, t] = (v * hf).astype(BF16)
-            slope = hf + (0.5 * GELU_C) * v * (1.0 - th * th) * (1.0 + (3.0 * GELU_A) * v2)
+            slope = hf + (0.5 * GELU_C) * v * (1.0 - thv * thv) * (1.0 + (3.0 * GELU_A) * v2)
             gpre_t[rows, t] = (fb[rows, :] * slope).astype(BF16)
             return inner
 
@@ -399,27 +505,30 @@
         fa[...] = mm(wu[...], gpre_t[:, t], NN)
         for step in (1, 2, 3):
 
-            @pl.when(i == step)
+            @pl.when(i == step - 1)
             def _(step=step):
                 tsend[step - 1] = fa[...].astype(BF16)
                 rcopy(tsend.at[step - 1], trecv.at[step - 1], g20 + step, (z, gx_of(step), c)).start()
 
-        @pl.when(i == 0)
-        def _():
-            gb_t[:, t] = fa[...].astype(BF16)
-
         return carry
 
     lax.fori_loop(0, 4, mlp, 0)
 
-    lane_block = 384
     dwc0 = take(4)
+    dwz0 = take(4 * nw)
+    do0 = take(16)
+    core_recv = (cq, co, cu, cd)
+    z_recvs = (zq, zo, zu, zd)
+    dw_refs = (gpre_t, wo, wu, wd)
+    dw_cols = (wq.shape[1], wo.shape[1], wu.shape[1], wd.shape[1])
+    dw_outs = (dq_out, do_out, du_out, dd_out)
+    slots = [0]
+    leaving = []
 
     def weight_grad(i, left, right):
         weight_passed(i)
-        dst = w_refs[i]
-        cols = dst.shape[1]
-        step_cols = lane_block if cols % lane_block == 0 else 256
+        dst, cols = dw_refs[i], dw_cols[i]
+        step_cols = 384 if cols % 384 == 0 else 256
 
         def one(n, carry):
             cs = pl.ds(pl.multiple_of(n * step_cols, 128), step_cols)
@@ -428,58 +537,47 @@
 
         lax.fori_loop(0, cols // step_cols, one, 0)
 
-    core_recv = (cq, co, cu, cd)
-    z_recv = (zq, zo, zu, zd)
-    w_refs = (wq, wo, wu, wd)
-    dw_outs = (dq_out, do_out, du_out, dd_out)
-
-    def core_half(core):
-        return pl.ds(pl.multiple_of(core * half, 16), half)
+    def core_half(i, core):
+        return dw_refs[i].at[pl.ds(pl.multiple_of(core * half, 16), half), :]
 
     def send_core(i):
         if zin:
-            cp = rcopy(w_refs[i].at[core_half(1 - c), :], core_recv[i], dwc0 + i, partner)
-            cp.start()
-            pending.append(cp)
+            rcopy(core_half(i, 1 - c), core_recv[i], dwc0 + i, partner).start()
+            pending.append(lambda: rcopy(core_half(i, 1 - c), core_recv[i], dwc0 + i, partner).wait_send())
         else:
-            cp = lcopy(w_refs[i], dw_outs[i], dwc0 + i)
-            cp.start()
-
-    dwz0 = take(4 * nz)
-    do0 = take(16)
-    slots = [0]
-    leaving = []
+            lcopy(dw_refs[i], dw_outs[i], dwc0 + i).start()
 
     def sum_core(i):
         if not zin:
             return
-        rcopy(w_refs[i].at[core_half(c), :], core_recv[i], dwc0 + i, partner).wait_recv()
-        w = w_refs[i]
+        rcopy(core_half(i, c), core_recv[i], dwc0 + i, partner).wait_recv()
+        w = dw_refs[i]
         for zz in range(nz):
             rows = pl.ds(pl.multiple_of(c * half + zz * fb_rows, 16), fb_rows)
             w[rows, :] = (
                 w[rows, :].astype(F32) + core_recv[i][zz * fb_rows : (zz + 1) * fb_rows, :].astype(F32)
             ).astype(BF16)
         for k in range(1, nz):
-            zz = (z + k) % nz
-            cp = rcopy(w.at[zrows(zz, c), :], z_recv[i].at[k - 1], dwz0 + i * nz + k, (zz, g, c))
-            cp.start()
-            pending.append(cp)
+
+            def make(k=k):
+                zz = (z + k) % nz
+                return rcopy(w.at[zrows(zz, c), :], z_recvs[i].at[k - 1], dwz0 + i * nz + k, (zz, g, c))
+
+            make().start()
+            pending.append(lambda make=make: make().wait_send())
 
     def sum_z(i):
         if not zin:
-            lcopy(w_refs[i], dw_outs[i], dwc0 + i).wait()
+            lcopy(dw_refs[i], dw_outs[i], dwc0 + i).wait()
             return
         for k in range(1, nz):
-            rcopy(
-                w_refs[i].at[zrows(z, c), :], z_recv[i].at[k - 1], dwz0 + i * nz + k, partner
-            ).wait_recv()
-        cols = w_refs[i].shape[1]
+            rcopy(dw_refs[i].at[zrows(z, c), :], z_recvs[i].at[k - 1], dwz0 + i * nz + k, partner).wait_recv()
+        cols = dw_cols[i]
         for n in range(0, cols, tb):
             size = min(tb, cols - n)
-            part = w_refs[i][zrows(z, c), n : n + size].astype(F32)
+            part = dw_refs[i][zrows(z, c), n : n + size].astype(F32)
             for k in range(1, nz):
-                part = part + z_recv[i][k - 1, :, n : n + size].astype(F32)
+                part = part + z_recvs[i][k - 1, :, n : n + size].astype(F32)
             slot = slots[0]
             slots[0] += 1
             stage = (fa, fb)[slot // 8].at[(slot % 8) * fb_rows : (slot % 8 + 1) * fb_rows, 0:size]
@@ -488,19 +586,38 @@
             cp.start()
             leaving.append(cp)
 
+    ml0 = take(8)
+    gh0 = take(4 * 8)
+    uv0 = take(8)
+    sm0 = take(8)
+    sz0 = take(nz)
+
+    def scatter(first, recv, start):
+        for dd, dc in others:
+            cp = rcopy(h2_t.at[feat(dd, dc), :], recv.at[dd * 2 + dc], first + dd * 2 + dc, dev(dd, dc))
+            cp.start() if start else cp.wait_send()
+        cp = lcopy(h2_t.at[own_feat, :], recv.at[0], first)
+        cp.start() if start else cp.wait()
+
     weight_grad(2, h2_t, gpre_t)
     send_core(2)
+
+    spread_sent(h20, h2_t)
+
+    def lower(j, carry):
+        t = toks(j)
+        h2_t[:, t] = mm(wd[...], act_t[:, t], NN).astype(BF16)
+        return carry
+
+    lax.fori_loop(0, 4, lower, 0)
+    h2_t[:, own_t] = (mm(wd[...], act_t[:, own_t], NN) + resid[...] + par(5)).astype(BF16)
+    sum_core(2)
     ones = jnp.ones((tok, 128), BF16)
     sums_col[0 : act_t.shape[0], 6:7] = mm(gpre_t[...], ones, NN)[:, 0:1]
 
     for step in (1, 2, 3):
         wait_tokens(g20, step)
-    gh2 = (
-        gb_t[:, own_t].astype(F32)
-        + trecv[0].astype(F32)
-        + trecv[1].astype(F32)
-        + trecv[2].astype(F32)
-    )
+    gh2 = fa[...] + trecv[0].astype(F32) + trecv[1].astype(F32) + trecv[2].astype(F32)
     m2 = rows_f[2, 1:2, own_t]
     r2 = rows_f[3, 1:2, own_t]
     normed2 = (resid[...] - m2) * r2
@@ -509,46 +626,17 @@
     s2 = jnp.sum(gn * normed2, axis=0, keepdims=True) * (1.0 / width)
     cot_own = cot_t[:, own_t].astype(F32)
     g_res = cot_own + r2 * (gn - s1 - normed2 * s2)
-    fb[...] = g_res
     g_low = g_res.astype(BF16)
-    for cp in h2_copies:
-        cp.wait_send()
-    wait_tokens_sent(g20)
     gb_t[:, own_t] = g_low
-    gb0 = take(4)
-    gb_copies = spread(gb0, gb_t)
+    gb0 = take(5)
+    spread(gb0, gb_t)
+    resid[...] = g_res
     sums_col[0:width, 2:3] = jnp.sum(g_low.astype(F32), axis=1, keepdims=True)
     sums_col[0:width, 3:4] = jnp.sum(gh2 * normed2, axis=1, keepdims=True)
     sums_col[0:width, 4:5] = jnp.sum(gh2, axis=1, keepdims=True)
     sums_col[0:width, 5:6] = jnp.sum(cot_own, axis=1, keepdims=True)
-
-    def lower(j, carry):
-        t = toks(j)
-        h2_t[:, t] = mm(wd[...], act_t[:, t], NN).astype(BF16)
-        return carry
-
-    lax.fori_loop(0, 4, lower, 0)
-    h2_t[:, own_t] = (mm(wd[...], act_t[:, own_t], NN) + resid[...] + par(5)).astype(BF16)
-    resid[...] = fb[...]
-    ml0 = take(8)
-    gh0 = take(8)
-    uv0 = take(8)
-
-    def scatter(first, recv):
-        copies = []
-        for dd, dc in others:
-            cp = rcopy(
-                h2_t.at[feat(dd, dc), :], recv.at[dd * 2 + dc], first + dd * 2 + dc, (z, gx_of(dd), row_of(dc))
-            )
-            cp.start()
-            copies.append(cp)
-        return copies
-
-    ml_copies = scatter(ml0, mrecv)
-    keep_own = lcopy(h2_t.at[own_feat, :], mrecv.at[0], ml0)
-    keep_own.start()
-    sum_core(2)
-
+    for step in (1, 2, 3):
+        rcopy(tsend.at[step - 1], trecv.at[step - 1], g20 + step, partner).wait_send()
     weight_grad(3, cot_t, act_t)
     send_core(3)
 
@@ -556,15 +644,27 @@
     dv_acc[...] = jnp.zeros_like(dv_acc)
 
     def attend_back(i, carry):
-        j = gx_of(i)
-        t = toks(j)
-        for step in (1, 2, 3):
-
-            @pl.when(i == step)
-            def _(step=step):
-                wait_block(gb0, gb_t, step)
+        t = toks(gx_of(i))
+
+        @pl.when(i == 1)
+        def _():
+            spread_relay(gb0, gb_t)
+            scatter(ml0, mrecv, True)
+
+        @pl.when(i == 3)
+        def _():
+            spread_done(gb0, gb_t)
 
         gatt_t[...] = mm(wo[...], gb_t[:, t], TN)[0:hp, :].astype(BF16)
+
+        @pl.when(i == 1)
+        def _():
+            sum_core(3)
+
+        @pl.when(i == 3)
+        def _():
+            weight_grad(1, gb_t, att_t)
+            send_core(1)
 
         def head(h, inner):
             kept = kept_of(h, t)
@@ -584,15 +684,25 @@
         return carry
 
     lax.fori_loop(0, 4, attend_back, 0)
+    kq = wq.shape[1]
     act_t[hp : 2 * hp, :] = (dk_acc[...] * factor).astype(BF16)
     act_t[2 * hp : 3 * hp, :] = dv_acc[...].astype(BF16)
-    kq = wq.shape[1]
     act_t[3 * hp : kq, :] = jnp.zeros((kq - 3 * hp, tok), BF16)
+    weight_grad(0, h1_t, act_t)
+    send_core(0)
+    sum_core(1)
     sums_col[0:kq, 7:8] = mm(act_t[0:kq, :], ones, NN)[:, 0:1]
-    for cp in ml_copies:
-        cp.wait_send()
-    keep_own.wait()
-    sum_core(3)
+    sum_core(0)
+    scatter(ml0, mrecv, False)
+
+    def gh_pieces(j, start):
+        t = toks(j)
+        for dd, dc in others:
+            slot = dd * 2 + dc
+            cp = rcopy(h2_t.at[feat(dd, dc), t], grecv.at[slot, :, t], gh0 + j * 8 + slot, dev(dd, dc))
+            cp.start() if start else cp.wait_send()
+        cp = lcopy(h2_t.at[own_feat, t], grecv.at[0, :, t], gh0 + j * 8)
+        cp.start() if start else cp.wait()
 
     def back1(j, carry):
         t = toks(j)
@@ -616,28 +726,32 @@
             fa[...] += resid[...]
 
         h2_t[:, t] = fa[...].astype(BF16)
+
+        @pl.when(j < 3)
+        def _():
+            gh_pieces(j, True)
+
         return carry
 
     lax.fori_loop(0, 4, back1, 0)
-    gh_copies = scatter(gh0, grecv)
-    keep_grad = lcopy(h2_t.at[own_feat, :], grecv.at[0], gh0)
-    keep_grad.start()
-    exchange(uv0, lambda dd, dc: uv_send, uv_recv.at[me])
-    keep_uv = lcopy(uv_send, uv_recv.at[me], uv0)
-    keep_uv.start()
-
-    weight_grad(0, h1_t, act_t)
-    send_core(0)
-    weight_grad(1, gb_t, att_t)
-    send_core(1)
-
-    sm0 = take(8)
-    sz0 = take(nz)
+
     for n in range(0, sm_send.shape[1], 128):
         sm_send[:, n : n + 128] = jnp.transpose(sums_col[n : n + 128, :])[0:8, :]
-    exchange(sm0, lambda dd, dc: sm_send, sm_recv.at[me])
-    sum_core(0)
-    sum_core(1)
+    exchange(sm0, sm_send, sm_recv.at[me])
+    exchange(uv0, uv_send, uv_recv.at[me])
+    lcopy(uv_send, uv_recv.at[me], uv0).start()
+    gh_pieces(3, True)
+
+    for dd, dc in others:
+        rcopy(h2_t.at[own_feat, :], mrecv.at[dd * 2 + dc], ml0 + dd * 2 + dc, partner).wait_recv()
+    for dc in (0, 1):
+        acc = mrecv[dc].astype(F32)
+        for dd in (1, 2, 3):
+            acc = acc + mrecv[dd * 2 + dc].astype(F32)
+        out_ref[:, row_tok(dc)] = acc.astype(BF16)
+
+    sum_z(2)
+    sum_z(3)
 
     total_sm = sm_send[...]
     row8 = lax.broadcasted_iota(jnp.int32, total_sm.shape, 0)
@@ -647,26 +761,24 @@
         total_sm = total_sm + (part if dd == 0 else jnp.where(row8 < 6, part, 0.0))
     smz_recv[0] = total_sm
     for k in range(1, nz):
-        cp = rcopy(smz_recv.at[0], smz_recv.at[k], sz0 + k, ((z + k) % nz, g, c))
-        cp.start()
-        pending.append(cp)
-
+
+        def make(k=k):
+            return rcopy(smz_recv.at[0], smz_recv.at[k], sz0 + k, ((z + k) % nz, g, c))
+
+        make().start()
+        pending.append(lambda make=make: make().wait_send())
+
+    sum_z(1)
+
+    lcopy(uv_send, uv_recv.at[me], uv0).wait()
     for dd, dc in others:
-        rcopy(h2_t.at[own_feat, :], mrecv.at[dd * 2 + dc], ml0 + dd * 2 + dc, partner).wait_recv()
-    for dc in (0, 1):
-        acc = mrecv[dc].astype(F32)
-        for dd in (1, 2, 3):
-            acc = acc + mrecv[dd * 2 + dc].astype(F32)
-        out_ref[:, row_tok(dc)] = acc.astype(BF16)
-
-    sum_z(2)
-    sum_z(3)
-
-    keep_grad.wait()
-    keep_uv.wait()
-    for dd, dc in others:
-        rcopy(h2_t.at[own_feat, :], grecv.at[dd * 2 + dc], gh0 + dd * 2 + dc, partner).wait_recv()
-        rcopy(uv_send, uv_recv.at[row_of(dc) * 4 + gx_of(dd)], uv0 + dd * 2 + dc, partner).wait_recv()
+        slot = dd * 2 + dc
+        rcopy(uv_send, uv_recv.at[row_of(dc) * 4 + gx_of(dd)], uv0 + slot, partner).wait_recv()
+        for j in range(4):
+            t = toks(j)
+            rcopy(h2_t.at[own_feat, t], grecv.at[slot, :, t], gh0 + j * 8 + slot, partner).wait_recv()
+    for j in range(4):
+        gh_pieces(j, False)
     for dc in (0, 1):
         acc = grecv[dc].astype(F32)
         uv = uv_recv[row_of(dc) * 4 + g]
@@ -676,18 +788,20 @@
         x_own = x_ref[:, row_tok(dc)].astype(F32)
         ig_ref[:, row_tok(dc)] = acc - uv[0:1, :] - x_own * uv[1:2, :]
 
+    sum_z(0)
     total_z = smz_recv[0]
     for k in range(1, nz):
         rcopy(smz_recv.at[0], smz_recv.at[k], sz0 + k, partner).wait_recv()
         total_z = total_z + smz_recv[k]
     sm_out[...] = total_z
-    sum_z(0)
-    sum_z(1)
 
     for cp in leaving:
         cp.wait()
-    for cp in pending + gb_copies + gh_copies:
-        cp.wait_send()
+    for wait in pending:
+        wait()
+    gather_sent(xs0, x_t)
+    gather_sent(cs0, cot_t)
+    spread_sent(gb0, gb_t)
 
 
 def local(
@@ -747,7 +861,7 @@
     tb = tok // 4
     half = width // 2
     vm = pltpu.VMEM
-    n_sems = 8 * 3 + 8 * nz + 4 * 4 + 4 + 4 * nz + 8 * 4 + nz + 24
+    n_sems = 130 + nz + (20 * nz if zin else 20)
     dw_specs = [pl.BlockSpec(memory_space=pl.ANY)] * 4
     if zin:
         dw_shapes = tuple(jax.ShapeDtypeStruct((fb_rows, k), F32) for k in (kq, ko, kh, kh))

time: 312 us -> 244 us (0.78); the launches traced: 307 us -> 243 us
  Pallas kernels: 285 us -> 222 us
    pallas_call x1, Pallas kernels: 285 us -> 222 us  [local(): pl.pallas_call(functools.partial(block_kernel, cfg), out_shape=(jax.Shape...]
where the time goes in v2:
time: 244 us; the launch traced here: 243 us
  Pallas kernels  222 us (91%)
  local copies, waits for them, and re-layouts  20 us (8%)
    pallas_call x1, Pallas kernels, local(): pl.pallas_call(functools.partial(block_kernel, cfg), out_shape=(jax.Shape...  222 us

profile of v2, /device:TPU:0, one launch (start us, length us, event | category | flops | bytes accessed | tf_op | source)
XLA Modules:
  0.0 243.5 jit_solution(16461915784282880346)
XLA Ops:
  0.6 0.8 concatenate.6
  1.4 0.6 pad.39.prm_ref
  2.0 1.2 copy.29
  3.3 0.2 copy.35
  3.5 0.7 pad.41.wq_in
  4.5 0.1 reshape.65
  4.6 0.7 pad.43.wo_in
  5.3 0.8 pad.44.wu_in
  6.1 0.8 pad.45.wd_in
  7.2 1.0 copy.31.qb_ref
  8.2 1.0 reshape.74.ub_ref
  9.3 222.0 %encoder_block.1 = (bf16[144,2048]{1,0:T(8,128)(2,1)}, f32[144,2048]{1,0:T(8,128)}, f32[144,1024]{1,0:T(8,128)}, f32[144,384]{1,0:T(8,128)}, f32[144,1152]{1,0:T...) custom-call(s32[1,6]{1,0:T(1,128)} %len_ref.1, f32[8,256]{1,0:T(8,128)} %pad.39.prm_ref, bf16[144,2048]{1,0:T(8,128)(2,1)} %bitcast.37, ...), custom_call_target="tpu_custom_call" | custom-call | tf_op jit(solution)/shard_map/encoder_block/pallas_call | solution.py:915
  231.3 1.6 fusion.2
  232.9 1.7 reshape.70
  234.6 0.5 copy.33
  235.1 1.2 copy.34
  236.3 0.8 slice_reduce_fusion.1
  237.3 0.6 pad_maximum_fusion
  237.9 0.2 reshape.72
  238.1 0.9 reshape.73
  239.0 1.1 slice_bitcast_fusion
  240.1 1.5 slice_reduce_fusion
  241.6 0.8 copy.38
  242.4 1.0 copy.39
  (36 shorter events, 0.9 us)
Async XLA Ops:
  3.2 1.0 copy-start.7
  3.3 2.0 copy-start.4
  3.5 2.6 %copy-start.5 = (bf16[1076,1,144]{0,2,1:T(8,128)(2,1)S(1)}, bf16[1076,1,144]{0,2,1:T(8,128)(2,1)}, u32[]{:S(2)}) copy-start(bf16[1076,1,144]{0,2,1:T(8,128)(2,1)} %param.27) | copy-start | bytes 929668
  4.3 2.6 %copy-start.9 = (f32[2,288]{1,0:T(2,128)S(1)}, f32[2,288]{1,0:T(2,128)}, u32[]{:S(2)}) copy-start(f32[2,288]{1,0:T(2,128)} %param.20) | copy-start | bytes 6916
  4.5 3.7 %copy-start.8 = (f32[1076]{0:T(1024)S(1)}, f32[1076]{0:T(1024)}, u32[]{:S(2)}) copy-start(f32[1076]{0:T(1024)} %param.26) | copy-start | bytes 12916
  235.1 2.8 %copy-start.6 = (f32[144,384]{1,0:T(8,128)S(1)}, f32[144,384]{1,0:T(8,128)}, u32[]{:S(2)}) copy-start(f32[144,384]{1,0:T(8,128)} %get-tuple-element.25) | copy-start | bytes 663556
  235.1 3.9 %copy-start.1 = (f32[144,1152]{1,0:T(8,128)S(1)}, f32[144,1152]{1,0:T(8,128)}, u32[]{:S(2)}) copy-start(f32[144,1152]{1,0:T(8,128)} %get-tuple-element.26) | copy-start | bytes 1990660
  235.1 3.9 %copy-start.2 = (f32[144,1152]{1,0:T(8,128)S(1)}, f32[144,1152]{1,0:T(8,128)}, u32[]{:S(2)}) copy-start(f32[144,1152]{1,0:T(8,128)} %get-tuple-element.27) | copy-start | bytes 1990660
  239.0 2.6 %copy-start.3 = (bf16[144,2048]{1,0:T(8,128)(2,1)S(1)}, bf16[144,2048]{1,0:T(8,128)(2,1)}, u32[]{:S(2)}) copy-start(bf16[144,2048]{1,0:T(8,128)(2,1)} %get-tuple-element.21) | copy-start | bytes 1769476
  240.1 2.3 copy-start

commit v3 on v2

--- a/solution.py
+++ b/solution.py
@@ -31,15 +31,20 @@
 def block_kernel(
     cfg,
     len_ref,
-    prm_ref,
+    g1_ref,
+    b1_ref,
+    ob_ref,
+    g2_ref,
+    b2_ref,
+    db_ref,
     x_ref,
     cot_ref,
     wq_in,
     wo_in,
     wu_in,
     wd_in,
-    qb_ref,
-    ub_ref,
+    qv_ref,
+    up_ref,
     out_ref,
     ig_ref,
     dq_out,
@@ -47,6 +52,7 @@
     du_out,
     dd_out,
     sm_out,
+    prm_send,
     prm_all,
     prm_col,
     x_t,
@@ -60,16 +66,17 @@
     wd,
     qkv_t,
     att_t,
+    wo_n,
     gatt_t,
     act_t,
     gpre_t,
     resid,
-    tsend,
     trecv,
     mrecv,
     grecv,
-    dk_acc,
-    dv_acc,
+    mrelay,
+    grelay,
+    dqf,
     fa,
     fb,
     pk,
@@ -91,11 +98,13 @@
     sem_s,
     sem_r,
 ):
+    prm_refs = (g1_ref, b1_ref, ob_ref, g2_ref, b2_ref, db_ref)
     nz, zin = cfg["nz"], cfg["zin"]
     fb_rows, tok, heads = cfg["fb"], cfg["tok"], cfg["heads"]
     half, width = 4 * fb_rows, 8 * fb_rows
     tb = tok // 4
-    hp = heads * HEAD_PAD
+    hd = heads * HEAD_DIM
+    hw = cfg["hw"]
     factor = HEAD_DIM ** (-0.5)
     z, g, c = lax.axis_index("dp"), lax.axis_index("gx"), lax.axis_index("gy")
     g_hi, g_lo = g // 2, g % 2
@@ -148,6 +157,39 @@
         pl.semaphore_signal(barrier, inc=1, device_id=dev(dd, dc), device_id_type=MESH)
     for k in range(1, nz):
         pl.semaphore_signal(barrier, inc=1, device_id=((z + k) % nz, g, c), device_id_type=MESH)
+    ends = []
+    total = len_ref[0, 0]
+    ends.append(total)
+    for s in range(1, len_ref.shape[1]):
+        total = total + len_ref[0, s]
+        ends.append(total)
+
+    def pictures(pos):
+        picture = jnp.zeros_like(pos)
+        for end in ends:
+            picture = picture + jnp.where(pos >= end, 1, 0)
+        return picture
+
+    pos_col = lax.broadcasted_iota(jnp.int32, (tok, 128), 0)
+    pk[...] = jnp.where(pos_col < total, pictures(pos_col), -1)
+    pos_row = lax.broadcasted_iota(jnp.int32, (8, tok), 1)
+    pic_row = pictures(pos_row)
+    rows_f[0, :, :] = pic_row.astype(F32)
+    rows_f[1, :, :] = jnp.where(pos_row < total, 1.0, 0.0)
+    sums_col[...] = jnp.zeros_like(sums_col)
+    qkv_t[...] = jnp.zeros_like(qkv_t)
+    gatt_t[...] = jnp.zeros_like(gatt_t)
+
+    prm_send[...] = jnp.zeros_like(prm_send)
+    for k, ref in enumerate(prm_refs):
+        prm_send[k : k + 1, 0:fb_rows] = ref[...]
+    sm_send[...] = jnp.zeros_like(sm_send)
+    sm_send[0:1, 0 : up_ref.shape[1]] = up_ref[...]
+    sm_send[1:2, 0:hd] = qv_ref[0:1, :]
+    sm_send[1:2, 2 * hw : 2 * hw + hd] = qv_ref[1:2, :]
+    for n in range(0, sm_send.shape[1], 128):
+        rows = jnp.concatenate([sm_send[:, n : n + 128], jnp.zeros((120, 128), F32)], axis=0)
+        prm_col[n : n + 128, 8:16] = jnp.transpose(rows)[:, 0:8]
     pl.semaphore_wait(barrier, 7 + nz - 1)
 
     own_feat = feat(0, 0)
@@ -195,11 +237,14 @@
                 part = relay_ref(dst, dd, dc)
                 rcopy(part, part, first + 6 + dd * 2 + dc, partner).wait_send()
 
-    weights = ((wq_in, wq), (wo_in, wo), (wu_in, wu), (wd_in, wd))
+    weights = tuple((wq_in.at[p], wq.at[:, p * hw : (p + 1) * hw]) for p in range(3))
+    weights += ((wo_in, wo), (wu_in, wu), (wd_in, wd))
+    n_w = len(weights)
+    all_s = range(1, nz)
     steps = nz - 1
     nw = nz if zin else 1
-    wz0 = take(4 * 2 * nw)
-    wc0 = take(4 * 2 * nw)
+    wz0 = take(n_w * 2 * nw)
+    wc0 = take(n_w * 2 * nw)
 
     def zrows(zz, core):
         return pl.ds(pl.multiple_of(core * half + zz * fb_rows, 16), fb_rows)
@@ -277,51 +322,35 @@
     p0 = take(8)
     xs0 = take(12)
     cs0 = take(12)
-    exchange(p0, prm_ref, prm_all.at[me])
-    lcopy(prm_ref, prm_all.at[me], p0).start()
+    exchange(p0, prm_send, prm_all.at[me])
+    lcopy(prm_send, prm_all.at[me], p0).start()
     gather_start(xs0, x_ref, x_t)
-    z_send(0, 1)
-
-    ends = []
-    total = len_ref[0, 0]
-    ends.append(total)
-    for s in range(1, len_ref.shape[1]):
-        total = total + len_ref[0, s]
-        ends.append(total)
-
-    def pictures(pos):
-        picture = jnp.zeros_like(pos)
-        for end in ends:
-            picture = picture + jnp.where(pos >= end, 1, 0)
-        return picture
-
-    pos_col = lax.broadcasted_iota(jnp.int32, (tok, 128), 0)
-    pk[...] = jnp.where(pos_col < total, pictures(pos_col), -1)
-    pos_row = lax.broadcasted_iota(jnp.int32, (8, tok), 1)
-    pic_row = pictures(pos_row)
-    rows_f[0, :, :] = pic_row.astype(F32)
-    rows_f[1, :, :] = jnp.where(pos_row < total, 1.0, 0.0)
-    sums_col[...] = jnp.zeros_like(sums_col)
-    att_t[...] = jnp.zeros_like(att_t)
-
-    lcopy(prm_ref, prm_all.at[me], p0).wait()
+    for i in range(3):
+        z_send(i, 1)
+
+    lcopy(prm_send, prm_all.at[me], p0).wait()
     for dd, dc in others:
-        rcopy(prm_ref, prm_all.at[row_of(dc) * 4 + gx_of(dd)], p0 + dd * 2 + dc, partner).wait_recv()
+        rcopy(prm_send, prm_all.at[row_of(dc) * 4 + gx_of(dd)], p0 + dd * 2 + dc, partner).wait_recv()
     for b in range(8):
         rows = jnp.concatenate([prm_all[b], jnp.zeros((120, 256), F32)], axis=0)
-        prm_col[b * fb_rows : (b + 1) * fb_rows, :] = jnp.transpose(rows)[:fb_rows, :]
+        prm_col[b * fb_rows : (b + 1) * fb_rows, 0:8] = jnp.transpose(rows)[:fb_rows, 0:8]
 
     def par(k):
         return prm_col[:, k : k + 1]
 
-    z_recv(0, 1)
-    z_send(1, 1)
+    def z_recv_all(pairs):
+        for i, step in pairs:
+            if step < nz:
+                z_recv(i, step)
+
+    z_recv_all(((0, 1), (1, 1), (0, 2), (2, 1), (1, 2), (0, 3)))
     gather_relay(xs0, x_ref, x_t)
     gather_start(cs0, cot_ref, cot_t)
-    if steps > 1:
-        z_recv(0, 2)
-    z_recv(1, 1)
-    z_send(2, 1)
+    z_recv_all(((2, 2), (1, 3)))
+    z_send(3, 1)
+    z_recv_all(((2, 3),))
+    for i in range(3):
+        z_recv_all((i, step) for step in range(4, nz))
     gather_done(xs0, x_ref, x_t)
 
     def ln1(j, carry):
@@ -337,24 +366,27 @@
 
     lax.fori_loop(0, 4, ln1, 0)
 
-    for s in range(3, nz):
-        z_recv(0, s)
-    if steps > 1:
-        z_recv(1, 2)
-    weight_ready(0)
+    z_recv_all(((3, 1),))
+    z_send(4, 1)
+    for i in range(3):
+        weight_ready(i)
+
+    def head_rows(part, h):
+        return pl.ds(pl.multiple_of((part * heads + h) * HEAD_PAD, 16), HEAD_PAD)
 
     def project(j, carry):
         t = toks(j)
-        qkv_t[:, t] = (mm(wq[...], h1_t[:, t], TN) + qb_ref[...]).astype(BF16)
+        for p in range(3):
+            part = mm(wq[:, p * hw : (p + 1) * hw], h1_t[:, t], TN)
+            if p != 1:
+                part = part + prm_col[p * hw : (p + 1) * hw, 9:10]
+            for h in range(heads):
+                first = (p * heads + h) * HEAD_PAD
+                qkv_t[first : first + HEAD_DIM, t] = part[h * HEAD_DIM : (h + 1) * HEAD_DIM, :].astype(BF16)
         return carry
 
     lax.fori_loop(0, 4, project, 0)
-    z_recv(2, 1)
-    for s in range(3, nz):
-        z_recv(1, s)
-
-    def head_rows(part, h):
-        return pl.ds(pl.multiple_of((part * heads + h) * HEAD_PAD, 16), HEAD_PAD)
+    z_recv_all(((3, 2),))
 
     def kept_of(h, t):
         scores = mm(qkv_t[head_rows(1, h), :], qkv_t[head_rows(0, h), t], TN) * factor
@@ -363,11 +395,77 @@
         allowed = jnp.concatenate([key_pic] * (tb // 128), axis=1) == query_pic
         return jnp.where(allowed, jnp.exp(scores), 0.0)
 
-    br0 = take(4)
-
-    def attend(i, carry):
-        dd = 3 - i
-        j = gx_of(dd)
+    wn0 = take(8)
+
+    def wo_part(gx, core, first=0, last=None):
+        rows = (fb_rows if last is None else last) - first
+        return wo_n.at[pl.ds(pl.multiple_of(gx * hd + core * fb_rows + first, 16), rows), :]
+
+    cut = fb_rows // 32 * 16 + 16
+
+    def wo_copy(n):
+        if n < 2:
+            own = wo_part(g, c)
+            return rcopy(own, own, wn0 + n + 1, (z, gx_of(n + 1), c))
+        if n < 4:
+            got = wo_part(gx_of(n - 1), c)
+            return rcopy(got, got, wn0 + n + 1, partner)
+        if n < 6:
+            on = wo_part(gx_of(1), c, 0, cut) if n == 4 else wo_part(gx_of(2), c, cut)
+            return rcopy(on, on, wn0 + n + 1, (z, gx_of(6 - n), c))
+        far = wo_part(gx_of(3), c)
+        return rcopy(far, far, wn0 + 7, partner)
+
+    def wo_first():
+        turned = jnp.transpose(wo[...])
+        wo_n[pl.ds(pl.multiple_of(g * hd, 16), hd), :] = turned[0:hd, :]
+        for n in (0, 1):
+            wo_copy(n).start()
+
+    def wo_second():
+        for step in (1, 2):
+            got = wo_part(gx_of(step), c)
+            rcopy(got, got, wn0 + step, partner).wait_recv()
+        for n in (4, 5, 2, 3):
+            wo_copy(n).start()
+
+    def wo_third():
+        for step, on in ((1, wo_part(gx_of(3), c, 0, cut)), (2, wo_part(gx_of(3), c, cut))):
+            rcopy(on, on, wn0 + 4 + step, partner).wait_recv()
+        wo_copy(6).start()
+
+    def wo_ready():
+        for step in (1, 2):
+            got = wo_part(gx_of(step), 1 - c)
+            rcopy(got, got, wn0 + 2 + step, partner).wait_recv()
+        far = wo_part(gx_of(3), 1 - c)
+        rcopy(far, far, wn0 + 7, partner).wait_recv()
+
+    at0 = take(4 * 3)
+    own_heads = pl.ds(pl.multiple_of(g * hd, 16), hd)
+
+    def att_piece(dd, j):
+        return att_t.at[pl.ds(pl.multiple_of(gx_of(dd) * hd, 16), hd), toks(j)]
+
+    def att_send(j, start):
+        for step in (1, 2):
+            piece = att_piece(0, j)
+            cp = rcopy(piece, piece, at0 + j * 3 + step - 1, (z, gx_of(step), c))
+            cp.start() if start else cp.wait_send()
+
+    def att_relay(j):
+        for step in (1, 2):
+            piece = att_piece(step, j)
+            rcopy(piece, piece, at0 + j * 3 + step - 1, partner).wait_recv()
+        step = 1 if j < 2 else 2
+        piece = att_piece(step, j)
+        rcopy(piece, piece, at0 + j * 3 + 2, (z, gx_of(3 - step), c)).start()
+
+    def att_relayed(j):
+        piece = att_piece(1 if j < 2 else 2, j)
+        rcopy(piece, piece, at0 + j * 3 + 2, partner).wait_send()
+
+    def attend(j, carry):
         t = toks(j)
 
         def head(h, inner):
@@ -380,62 +478,74 @@
             rows_f[5 + 2 * h, 0:1, t] = inv
             probs = (kept * scale * inv).astype(BF16)
             att = mm(qkv_t[head_rows(2, h), :], probs, NN)
-            att_t[head_rows(0, h), t] = att.astype(BF16)
+            dqf[pl.ds(pl.multiple_of(h * HEAD_DIM, 8), HEAD_DIM), :] = att[0:HEAD_DIM, :]
             return inner
 
         lax.fori_loop(0, heads, head, 0)
-
-        @pl.when(i == 0)
-        def _():
-            weight_ready(1)
-
-        fa[...] = mm(wo[...], att_t[:, t], NN)
-        for step in (3, 2, 1):
-
-            @pl.when(i == 3 - step)
-            def _(step=step):
-                gb_t[:, t] = fa[...].astype(BF16)
-                rcopy(gb_t.at[:, t], trecv.at[step - 1], br0 + step, (z, gx_of(step), c)).start()
-
-        @pl.when(i == 1)
-        def _():
-            if steps > 1:
-                z_recv(2, 2)
-            z_send(3, 1)
+        att_t[own_heads, t] = dqf[...].astype(BF16)
+
+        @pl.when(j == 0)
+        def _():
+            z_recv_all((3, step) for step in range(3, nz))
+            weight_ready(3)
+            wo_first()
+
+        att_send(j, True)
+
+        @pl.when(j == 0)
+        def _():
+            z_recv_all(((4, 1),))
             gather_relay(cs0, cot_ref, cot_t)
 
+        @pl.when(j == 2)
+        def _():
+            wo_second()
+            z_recv_all(((4, 2),))
+            z_send(5, 1)
+            att_relay(0)
+
         return carry
 
     lax.fori_loop(0, 4, attend, 0)
-
-    def wait_tokens(first, step):
-        rcopy(gb_t.at[:, own_t], trecv.at[step - 1], first + step, partner).wait_recv()
-
-    def wait_tokens_sent(first):
-        for step in (1, 2, 3):
-            rcopy(gb_t.at[:, toks(gx_of(step))], trecv.at[step - 1], first + step, partner).wait_send()
-
-    for s in range(3, nz):
-        z_recv(2, s)
-    z_recv(3, 1)
-
-    for step in (3, 2, 1):
-        wait_tokens(br0, step)
-    residual = (
-        x_t[:, own_t].astype(F32)
-        + fa[...]
-        + trecv[0].astype(F32)
-        + trecv[1].astype(F32)
-        + trecv[2].astype(F32)
-        + par(2)
-    )
-    resid[...] = residual
-    m2 = jnp.sum(residual, axis=0, keepdims=True) * (1.0 / width)
-    q2 = jnp.sum(residual * residual, axis=0, keepdims=True) * (1.0 / width)
-    r2 = lax.rsqrt(q2 - m2 * m2 + EPSILON)
-    rows_f[2, 1:2, own_t] = m2
-    rows_f[3, 1:2, own_t] = r2
-    h2_t[:, own_t] = ((residual - m2) * r2 * par(3) + par(4)).astype(BF16)
+    att_relay(1)
+    wo_third()
+    z_recv_all((4, step) for step in range(3, nz))
+
+    def project_out(j, carry):
+        t = toks(j)
+
+        @pl.when(j == 0)
+        def _():
+            att_relay(2)
+            wo_ready()
+
+        @pl.when(j == 1)
+        def _():
+            att_relay(3)
+            z_recv_all(((5, 1),))
+
+        far = att_piece(3, j)
+        rcopy(far, far, at0 + j * 3 + 2, partner).wait_recv()
+        residual = mm(wo_n[...], att_t[:, t], TN) + x_t[:, t].astype(F32) + par(2)
+        m2 = jnp.sum(residual, axis=0, keepdims=True) * (1.0 / width)
+        q2 = jnp.sum(residual * residual, axis=0, keepdims=True) * (1.0 / width)
+        r2 = lax.rsqrt(q2 - m2 * m2 + EPSILON)
+        rows_f[2, 1:2, t] = m2
+        rows_f[3, 1:2, t] = r2
+        h2_t[:, t] = ((residual - m2) * r2 * par(3) + par(4)).astype(BF16)
+
+        @pl.when(j == g)
+        def _():
+            resid[...] = residual
+
+        return carry
+
+    lax.fori_loop(0, 4, project_out, 0)
+    weight_ready(4)
+    z_recv_all(((5, 2),))
+    gather_done(cs0, cot_ref, cot_t)
+    for n in range(7):
+        wo_copy(n).wait_send()
 
     def spread(first, buf):
         for step in (1, 2):
@@ -462,32 +572,20 @@
             part = halves(buf, step, step)
             rcopy(part, part, first + 2 + step, partner).wait_send()
 
-    h20 = take(5)
-    spread(h20, h2_t)
-    wait_tokens_sent(br0)
-    weight_ready(2)
-    if steps > 1:
-        z_recv(3, 2)
-    gather_done(cs0, cot_ref, cot_t)
-
     g20 = take(4)
 
+    def tsend(step):
+        return wo_n.at[:, (step - 1) * tb : step * tb]
+
     def mlp(i, carry):
-        dd = (i + 1) % 4
-        t = toks(gx_of(dd))
+        t = toks(gx_of(3 - i))
+        fa[...] = mm(wu[...], h2_t[:, t], TN) + prm_col[:, 8:9]
 
         @pl.when(i == 0)
         def _():
-            spread_relay(h20, h2_t)
-            for s in range(3, nz):
-                z_recv(3, s)
-            weight_ready(3)
-
-        @pl.when(i == 2)
-        def _():
-            spread_done(h20, h2_t)
-
-        fa[...] = mm(wu[...], h2_t[:, t], TN) + ub_ref[...]
+            z_recv_all((5, step) for step in range(3, nz))
+            weight_ready(5)
+
         fb[...] = mm(wd[...], cot_t[:, t], TN)
 
         def chunk(n, inner):
@@ -505,30 +603,33 @@
         fa[...] = mm(wu[...], gpre_t[:, t], NN)
         for step in (1, 2, 3):
 
-            @pl.when(i == step - 1)
+            @pl.when(i == 3 - step)
             def _(step=step):
-                tsend[step - 1] = fa[...].astype(BF16)
-                rcopy(tsend.at[step - 1], trecv.at[step - 1], g20 + step, (z, gx_of(step), c)).start()
+                tsend(step)[...] = fa[...].astype(BF16)
+                rcopy(tsend(step), trecv.at[step - 1], g20 + step, (z, gx_of(step), c)).start()
 
         return carry
 
     lax.fori_loop(0, 4, mlp, 0)
 
     dwc0 = take(4)
-    dwz0 = take(4 * nw)
+    dwz0 = take(4 * 8)
     do0 = take(16)
+    gath = ((0, 1, 2), (3,), (4,), (5,))
     core_recv = (cq, co, cu, cd)
     z_recvs = (zq, zo, zu, zd)
-    dw_refs = (gpre_t, wo, wu, wd)
-    dw_cols = (wq.shape[1], wo.shape[1], wu.shape[1], wd.shape[1])
+    dw_refs = (wo_n, wo, wu, wd)
+    kp = cfg["kp"]
+    dw_cols = (kp, wo.shape[1], wu.shape[1], wd.shape[1])
     dw_outs = (dq_out, do_out, du_out, dd_out)
     slots = [0]
     leaving = []
 
     def weight_grad(i, left, right):
-        weight_passed(i)
+        for n in gath[i]:
+            weight_passed(n)
         dst, cols = dw_refs[i], dw_cols[i]
-        step_cols = 384 if cols % 384 == 0 else 256
+        step_cols = 384
 
         def one(n, carry):
             cs = pl.ds(pl.multiple_of(n * step_cols, 128), step_cols)
@@ -536,16 +637,19 @@
             return carry
 
         lax.fori_loop(0, cols // step_cols, one, 0)
+        rest = cols // step_cols * step_cols
+        if rest < cols:
+            dst[:, rest:cols] = mm(left[...], right[rest:cols, :], NT).astype(BF16)
 
     def core_half(i, core):
-        return dw_refs[i].at[pl.ds(pl.multiple_of(core * half, 16), half), :]
+        return dw_refs[i].at[pl.ds(pl.multiple_of(core * half, 16), half), 0 : dw_cols[i]]
 
     def send_core(i):
         if zin:
             rcopy(core_half(i, 1 - c), core_recv[i], dwc0 + i, partner).start()
             pending.append(lambda: rcopy(core_half(i, 1 - c), core_recv[i], dwc0 + i, partner).wait_send())
         else:
-            lcopy(dw_refs[i], dw_outs[i], dwc0 + i).start()
+            lcopy(dw_refs[i].at[:, 0 : dw_cols[i]], dw_outs[i], dwc0 + i).start()
 
     def sum_core(i):
         if not zin:
@@ -554,55 +658,161 @@
         w = dw_refs[i]
         for zz in range(nz):
             rows = pl.ds(pl.multiple_of(c * half + zz * fb_rows, 16), fb_rows)
-            w[rows, :] = (
-                w[rows, :].astype(F32) + core_recv[i][zz * fb_rows : (zz + 1) * fb_rows, :].astype(F32)
+            cols = dw_cols[i]
+            w[rows, 0:cols] = (
+                w[rows, 0:cols].astype(F32) + core_recv[i][zz * fb_rows : (zz + 1) * fb_rows, :].astype(F32)
             ).astype(BF16)
-        for k in range(1, nz):
-
-            def make(k=k):
-                zz = (z + k) % nz
-                return rcopy(w.at[zrows(zz, c), :], z_recvs[i].at[k - 1], dwz0 + i * nz + k, (zz, g, c))
-
-            make().start()
-            pending.append(lambda make=make: make().wait_send())
+
+        @pl.when(leaf)
+        def _():
+            for slot, zz in enumerate((far_end, far_inner, inner)):
+                z_piece(i, slot, zz, slot, inner).start()
+
+        @pl.when(jnp.logical_not(leaf))
+        def _():
+            z_piece(i, 3, end, 0, end).start()
+
+    leaf = z % 3 == 0
+    low = z < 2
+    end, inner = jnp.where(low, 0, 3), jnp.where(low, 1, 2)
+    far_end, far_inner = 3 - end, 3 - inner
+
+    def z_piece(i, sem, zz, slot, to):
+        rows = dw_refs[i].at[zrows(zz, c), 0 : dw_cols[i]]
+        return rcopy(rows, z_recvs[i].at[slot], dwz0 + i * 8 + sem, (to, g, c))
+
+    def z_land(i, slot):
+        rows = dw_refs[i].at[zrows(z, c), 0 : dw_cols[i]]
+        return rcopy(rows, z_recvs[i].at[min(slot, 3) if slot != 3 else 0], dwz0 + i * 8 + slot, partner)
+
+    def relay_z(i, slot):
+        if not zin:
+            return
+
+        @pl.when(jnp.logical_not(leaf))
+        def _():
+            z_land(i, slot).wait_recv()
+            zz = far_end if slot == 0 else far_inner
+            w, cols = dw_refs[i], dw_cols[i]
+            rows = zrows(zz, c)
+            w[rows, 0:cols] = (w[rows, 0:cols].astype(F32) + z_recvs[i][slot].astype(F32)).astype(BF16)
+            z_piece(i, 4 + slot, zz, 3, zz).start()
+
+    def z_sent(i):
+        if not zin:
+            return
+
+        @pl.when(leaf)
+        def _():
+            for slot, zz in enumerate((far_end, far_inner, inner)):
+                z_piece(i, slot, zz, slot, inner).wait_send()
+
+        @pl.when(jnp.logical_not(leaf))
+        def _():
+            z_piece(i, 3, end, 0, end).wait_send()
+            z_piece(i, 4, far_end, 3, far_end).wait_send()
+            z_piece(i, 5, far_inner, 3, far_inner).wait_send()
 
     def sum_z(i):
         if not zin:
-            lcopy(dw_refs[i], dw_outs[i], dwc0 + i).wait()
+            lcopy(dw_refs[i].at[:, 0 : dw_cols[i]], dw_outs[i], dwc0 + i).wait()
             return
-        for k in range(1, nz):
-            rcopy(dw_refs[i].at[zrows(z, c), :], z_recvs[i].at[k - 1], dwz0 + i * nz + k, partner).wait_recv()
+
+        @pl.when(leaf)
+        def _():
+            z_land(i, 3).wait_recv()
+            z_land(i, 4).wait_recv()
+
+        @pl.when(jnp.logical_not(leaf))
+        def _():
+            z_land(i, 2).wait_recv()
+            z_land(i, 5).wait_recv()
+
+        near_slot = jnp.where(leaf, 0, 2)
         cols = dw_cols[i]
-        for n in range(0, cols, tb):
-            size = min(tb, cols - n)
+
+        def total_of(n, size):
             part = dw_refs[i][zrows(z, c), n : n + size].astype(F32)
-            for k in range(1, nz):
-                part = part + z_recvs[i][k - 1, :, n : n + size].astype(F32)
-            slot = slots[0]
+            return part + z_recvs[i][near_slot, :, n : n + size].astype(F32) + z_recvs[i][3, :, n : n + size].astype(F32)
+
+        if i == 0:
+            whole = total_of(0, cols)
+            gap = jnp.zeros((fb_rows, hw - hd), F32)
+            pieces = []
+            for p in range(3):
+                part = jnp.concatenate([whole[:, p * hd : (p + 1) * hd], gap], axis=1)
+                for n in range(0, hw, tb):
+                    size = min(tb, hw - n)
+                    pieces.append((part[:, n : n + size], dq_out.at[p, :, n : n + size]))
+        else:
+            pieces = []
+            for n in range(0, cols, tb):
+                size = min(tb, cols - n)
+                pieces.append((total_of(n, size), dw_outs[i].at[:, n : n + size]))
+        for part, goes in pieces:
+            size = part.shape[1]
+            slot = slots[0] % 16
+            if slots[0] >= 16:
+                leaving[slot].wait()
             slots[0] += 1
             stage = (fa, fb)[slot // 8].at[(slot % 8) * fb_rows : (slot % 8 + 1) * fb_rows, 0:size]
             stage[...] = part
-            cp = lcopy(stage, dw_outs[i].at[:, n : n + size], do0 + slot)
+            cp = lcopy(stage, goes, do0 + slot)
             cp.start()
-            leaving.append(cp)
-
-    ml0 = take(8)
-    gh0 = take(4 * 8)
+            if len(leaving) > slot:
+                leaving[slot] = cp
+            else:
+                leaving.append(cp)
+
+    ml0 = take(16)
+    gh0 = take(16)
     uv0 = take(8)
     sm0 = take(8)
     sz0 = take(nz)
 
-    def scatter(first, recv, start):
-        for dd, dc in others:
-            cp = rcopy(h2_t.at[feat(dd, dc), :], recv.at[dd * 2 + dc], first + dd * 2 + dc, dev(dd, dc))
-            cp.start() if start else cp.wait_send()
-        cp = lcopy(h2_t.at[own_feat, :], recv.at[0], first)
-        cp.start() if start else cp.wait()
+    direct, added = ((1, 0), (2, 1), (0, 1)), ((1, 1), (2, 0))
+
+    def hand(buf, relay, first, j, n):
+        part = relay.at[n, :, toks(j)]
+        return rcopy(buf.at[feat(3, n), toks(j)], part, first + 8 + j * 2 + n, (z, gx_of(n + 1), c))
+
+    def block_copy(buf, recv, first, dd, dc):
+        slot = dd * 2 + dc
+        return rcopy(buf.at[feat(dd, dc), :], recv.at[slot], first + slot, dev(dd, dc))
+
+    def add_relayed(buf, relay, recv, first):
+        for n, (dd, dc) in ((0, (2, 0)), (1, (1, 1))):
+            for j in range(4):
+                hand(buf, relay, first, j, n).wait_recv()
+            rows = feat(dd, dc)
+            buf[rows, :] = (buf[rows, :].astype(F32) + relay[n].astype(F32)).astype(BF16)
+            block_copy(buf, recv, first, dd, dc).start()
+
+    def scatter_sent(buf, relay, recv, first):
+        for dd, dc in direct + added:
+            block_copy(buf, recv, first, dd, dc).wait_send()
+        for n in (0, 1):
+            for j in range(4):
+                hand(buf, relay, first, j, n).wait_send()
+
+    def scatter_start(buf, recv, first):
+        for dd, dc in direct:
+            block_copy(buf, recv, first, dd, dc).start()
+        lcopy(buf.at[own_feat, :], recv.at[0], first).start()
+
+    def scatter_sum(buf, recv, first, dc):
+        if dc == 0:
+            lcopy(buf.at[own_feat, :], recv.at[0], first).wait()
+        acc = 0.0
+        for dd in (0, 1, 2):
+            if dd or dc:
+                block_copy(buf, recv, first, dd, dc).wait_recv()
+            acc = acc + recv[dd * 2 + dc].astype(F32)
+        return acc
 
     weight_grad(2, h2_t, gpre_t)
     send_core(2)
 
-    spread_sent(h20, h2_t)
 
     def lower(j, carry):
         t = toks(j)
@@ -616,7 +826,7 @@
     sums_col[0 : act_t.shape[0], 6:7] = mm(gpre_t[...], ones, NN)[:, 0:1]
 
     for step in (1, 2, 3):
-        wait_tokens(g20, step)
+        rcopy(tsend(step), trecv.at[step - 1], g20 + step, partner).wait_recv()
     gh2 = fa[...] + trecv[0].astype(F32) + trecv[1].astype(F32) + trecv[2].astype(F32)
     m2 = rows_f[2, 1:2, own_t]
     r2 = rows_f[3, 1:2, own_t]
@@ -636,12 +846,16 @@
     sums_col[0:width, 4:5] = jnp.sum(gh2, axis=1, keepdims=True)
     sums_col[0:width, 5:6] = jnp.sum(cot_own, axis=1, keepdims=True)
     for step in (1, 2, 3):
-        rcopy(tsend.at[step - 1], trecv.at[step - 1], g20 + step, partner).wait_send()
+        rcopy(tsend(step), trecv.at[step - 1], g20 + step, partner).wait_send()
     weight_grad(3, cot_t, act_t)
     send_core(3)
-
-    dk_acc[...] = jnp.zeros_like(dk_acc)
-    dv_acc[...] = jnp.zeros_like(dv_acc)
+    relay_z(2, 0)
+
+    fa[...] = jnp.zeros_like(fa)
+    fb[...] = jnp.zeros_like(fb)
+    for p in range(3):
+        act_t[p * hw + hd : (p + 1) * hw, :] = jnp.zeros((hw - hd, tok), BF16)
+    gpre_t[3 * hd : kp, :] = jnp.zeros((kp - 3 * hd, tok), BF16)
 
     def attend_back(i, carry):
         t = toks(gx_of(i))
@@ -649,21 +863,32 @@
         @pl.when(i == 1)
         def _():
             spread_relay(gb0, gb_t)
-            scatter(ml0, mrecv, True)
+            for n in (0, 1):
+                for k in range(4):
+                    hand(h2_t, mrelay, ml0, k, n).start()
+            scatter_start(h2_t, mrecv, ml0)
 
         @pl.when(i == 3)
         def _():
             spread_done(gb0, gb_t)
 
-        gatt_t[...] = mm(wo[...], gb_t[:, t], TN)[0:hp, :].astype(BF16)
+        gatt = mm(wo[...], gb_t[:, t], TN)
+        for h in range(heads):
+            gatt_t[h * HEAD_PAD : h * HEAD_PAD + HEAD_DIM, :] = gatt[h * HEAD_DIM : (h + 1) * HEAD_DIM, :].astype(BF16)
 
         @pl.when(i == 1)
         def _():
             sum_core(3)
 
+        @pl.when(i == 2)
+        def _():
+            relay_z(2, 1)
+
         @pl.when(i == 3)
         def _():
-            weight_grad(1, gb_t, att_t)
+            add_relayed(h2_t, mrelay, mrecv, ml0)
+            weight_passed(3)
+            wo[:, 0:hd] = mm(gb_t[...], att_t[own_heads, :], NT).astype(BF16)
             send_core(1)
 
         def head(h, inner):
@@ -675,34 +900,37 @@
             weighted = probs * grad_probs
             delta = jnp.sum(weighted, axis=0, keepdims=True)
             grad_scores = (weighted - probs * delta).astype(BF16)
-            act_t[q_rows, t] = (mm(qkv_t[head_rows(1, h), :], grad_scores, NN) * factor).astype(BF16)
-            dk_acc[q_rows, :] += mm(qkv_t[q_rows, t], grad_scores, NT)
-            dv_acc[q_rows, :] += mm(grad, probs.astype(BF16), NT)
+            dq = mm(qkv_t[head_rows(1, h), :], grad_scores, NN) * factor
+            dqf[pl.ds(pl.multiple_of(h * HEAD_DIM, 8), HEAD_DIM), :] = dq[0:HEAD_DIM, :]
+            dk = mm(qkv_t[q_rows, t], grad_scores, NT)
+            dv = mm(grad, probs.astype(BF16), NT)
+            for kb in range(4):
+                rows = pl.ds(pl.multiple_of(kb * hd + h * HEAD_DIM, 8), HEAD_DIM)
+                fa[rows, :] += dk[0:HEAD_DIM, kb * tb : (kb + 1) * tb]
+                fb[rows, :] += dv[0:HEAD_DIM, kb * tb : (kb + 1) * tb]
             return inner
 
         lax.fori_loop(0, heads, head, 0)
+        act_t[0:hd, t] = dqf[...].astype(BF16)
+        gpre_t[0:hd, t] = dqf[...].astype(BF16)
         return carry
 
     lax.fori_loop(0, 4, attend_back, 0)
     kq = wq.shape[1]
-    act_t[hp : 2 * hp, :] = (dk_acc[...] * factor).astype(BF16)
-    act_t[2 * hp : 3 * hp, :] = dv_acc[...].astype(BF16)
-    act_t[3 * hp : kq, :] = jnp.zeros((kq - 3 * hp, tok), BF16)
-    weight_grad(0, h1_t, act_t)
+    for kb in range(4):
+        cols, rows = slice(kb * tb, (kb + 1) * tb), slice(kb * hd, (kb + 1) * hd)
+        dk_low, dv_low = (fa[rows, :] * factor).astype(BF16), fb[rows, :].astype(BF16)
+        act_t[hw : hw + hd, cols] = dk_low
+        act_t[2 * hw : 2 * hw + hd, cols] = dv_low
+        gpre_t[hd : 2 * hd, cols] = dk_low
+        gpre_t[2 * hd : 3 * hd, cols] = dv_low
+    weight_grad(0, h1_t, gpre_t)
     send_core(0)
     sum_core(1)
+    relay_z(3, 0)
     sums_col[0:kq, 7:8] = mm(act_t[0:kq, :], ones, NN)[:, 0:1]
     sum_core(0)
-    scatter(ml0, mrecv, False)
-
-    def gh_pieces(j, start):
-        t = toks(j)
-        for dd, dc in others:
-            slot = dd * 2 + dc
-            cp = rcopy(h2_t.at[feat(dd, dc), t], grecv.at[slot, :, t], gh0 + j * 8 + slot, dev(dd, dc))
-            cp.start() if start else cp.wait_send()
-        cp = lcopy(h2_t.at[own_feat, t], grecv.at[0, :, t], gh0 + j * 8)
-        cp.start() if start else cp.wait()
+    gather_sent(cs0, cot_t)
 
     def back1(j, carry):
         t = toks(j)
@@ -717,38 +945,39 @@
         a1 = jnp.sum(gn1, axis=0, keepdims=True) * (1.0 / width)
         a2 = jnp.sum(gn1 * normed, axis=0, keepdims=True) * (1.0 / width)
         v = r * r * a2
-        uv_send[0:1, t] = r * a1 - m * v
-        uv_send[1:2, t] = v
+        u = r * a1 - m * v
+        for n in range(tb // 128):
+            row = j * (tb // 128) + n
+            uv_send[pl.ds(row, 1), :] = u[:, n * 128 : (n + 1) * 128]
+            uv_send[pl.ds(tok // 128 + row, 1), :] = v[:, n * 128 : (n + 1) * 128]
         fa[...] = r * gn1
 
         @pl.when(j == g)
         def _():
             fa[...] += resid[...]
 
-        h2_t[:, t] = fa[...].astype(BF16)
-
-        @pl.when(j < 3)
-        def _():
-            gh_pieces(j, True)
-
+        cot_t[:, t] = fa[...].astype(BF16)
+        for n in (0, 1):
+            hand(cot_t, grelay, gh0, j, n).start()
         return carry
 
     lax.fori_loop(0, 4, back1, 0)
+
+    relay_z(3, 1)
+    relay_z(1, 0)
+    relay_z(1, 1)
 
     for n in range(0, sm_send.shape[1], 128):
         sm_send[:, n : n + 128] = jnp.transpose(sums_col[n : n + 128, :])[0:8, :]
     exchange(sm0, sm_send, sm_recv.at[me])
     exchange(uv0, uv_send, uv_recv.at[me])
     lcopy(uv_send, uv_recv.at[me], uv0).start()
-    gh_pieces(3, True)
-
-    for dd, dc in others:
-        rcopy(h2_t.at[own_feat, :], mrecv.at[dd * 2 + dc], ml0 + dd * 2 + dc, partner).wait_recv()
+    scatter_start(cot_t, grecv, gh0)
+    add_relayed(cot_t, grelay, grecv, gh0)
+    relay_z(0, 0)
+
     for dc in (0, 1):
-        acc = mrecv[dc].astype(F32)
-        for dd in (1, 2, 3):
-            acc = acc + mrecv[dd * 2 + dc].astype(F32)
-        out_ref[:, row_tok(dc)] = acc.astype(BF16)
+        out_ref[:, row_tok(dc)] = scatter_sum(h2_t, mrecv, ml0, dc).astype(BF16)
 
     sum_z(2)
     sum_z(3)
@@ -768,25 +997,22 @@
         make().start()
         pending.append(lambda make=make: make().wait_send())
 
+    relay_z(0, 1)
     sum_z(1)
 
     lcopy(uv_send, uv_recv.at[me], uv0).wait()
     for dd, dc in others:
-        slot = dd * 2 + dc
-        rcopy(uv_send, uv_recv.at[row_of(dc) * 4 + gx_of(dd)], uv0 + slot, partner).wait_recv()
-        for j in range(4):
-            t = toks(j)
-            rcopy(h2_t.at[own_feat, t], grecv.at[slot, :, t], gh0 + j * 8 + slot, partner).wait_recv()
-    for j in range(4):
-        gh_pieces(j, False)
+        rcopy(uv_send, uv_recv.at[row_of(dc) * 4 + gx_of(dd)], uv0 + dd * 2 + dc, partner).wait_recv()
     for dc in (0, 1):
-        acc = grecv[dc].astype(F32)
+        acc = scatter_sum(cot_t, grecv, gh0, dc)
         uv = uv_recv[row_of(dc) * 4 + g]
         for dd in (1, 2, 3):
-            acc = acc + grecv[dd * 2 + dc].astype(F32)
             uv = uv + uv_recv[row_of(dc) * 4 + gx_of(dd)]
+        n_rows = tok // 128
+        u_row = jnp.concatenate([uv[n : n + 1, :] for n in range(n_rows)], axis=1)
+        v_row = jnp.concatenate([uv[n_rows + n : n_rows + n + 1, :] for n in range(n_rows)], axis=1)
         x_own = x_ref[:, row_tok(dc)].astype(F32)
-        ig_ref[:, row_tok(dc)] = acc - uv[0:1, :] - x_own * uv[1:2, :]
+        ig_ref[:, row_tok(dc)] = acc - u_row - x_own * v_row
 
     sum_z(0)
     total_z = smz_recv[0]
@@ -800,7 +1026,13 @@
     for wait in pending:
         wait()
     gather_sent(xs0, x_t)
-    gather_sent(cs0, cot_t)
+    for j in range(4):
+        att_send(j, False)
+        att_relayed(j)
+    scatter_sent(h2_t, mrelay, mrecv, ml0)
+    scatter_sent(cot_t, grelay, grecv, gh0)
+    for i in range(4):
+        z_sent(i)
     spread_sent(gb0, gb_t)
 
 
@@ -826,52 +1058,48 @@
     tok = tok2 // 2
     width = 8 * fb_rows
     heads = w_qkv.shape[3] // HEAD_DIM
+    hd = heads * HEAD_DIM
+    hw = round_up(hd, 128)
     hp = heads * HEAD_PAD
-    kq, ko = round_up(3 * hp, 128), round_up(hp, 128)
     hid = w_up.shape[2]
     kh = round_up(hid, 384)
+    kq = 3 * hw
+    kp = round_up(3 * hd, 128)
     zrow = w_qkv.shape[1]
     zin = zrow == fb_rows and nz == 4
 
-    def pad_heads(a):
-        parts = a.shape[-1] // HEAD_DIM
-        a = a.reshape(a.shape[:-1] + (parts, HEAD_DIM))
-        a = jnp.pad(a, [(0, 0)] * (a.ndim - 1) + [(0, HEAD_PAD - HEAD_DIM)])
-        return a.reshape(a.shape[:-2] + (parts * HEAD_PAD,))
-
     def widen(a, cols):
-        return jnp.pad(a, ((0, 0), (0, cols - a.shape[1])))
-
-    prm = jnp.concatenate([ln1_gain, ln1_bias, out_bias, ln2_gain, ln2_bias, down_bias], axis=0)
-    prm = jnp.pad(prm, ((0, 2), (0, 256 - fb_rows)))
-    wq = widen(pad_heads(w_qkv[0].reshape(zrow, -1)), kq)
-    wo = widen(pad_heads(jnp.transpose(w_out[:, 0, :])), ko)
+        return jnp.pad(a, [(0, 0)] * (a.ndim - 1) + [(0, cols - a.shape[-1])])
+
+    wq = widen(jnp.transpose(w_qkv[0], (1, 0, 2)), hw)
+    wo = widen(jnp.transpose(w_out[:, 0, :]), hw)
     wu = widen(w_up[0], kh)
     wd = widen(jnp.transpose(w_down[:, 0, :]), kh)
-    qb = jnp.concatenate([qv_bias[0:1], jnp.zeros_like(qv_bias[0:1]), qv_bias[1:2]], axis=1)
-    qb = widen(pad_heads(qb), kq).reshape(kq, 1)
-    ub = jnp.pad(up_bias, (0, kh - hid)).reshape(kh, 1)
     if not zin:
-        wq, wo, wu, wd = (
-            lax.all_gather(lax.all_gather(w, "dp", axis=0, tiled=True), "gy", axis=0, tiled=True)
-            for w in (wq, wo, wu, wd)
-        )
-
-    cfg = dict(nz=nz, zin=zin, fb=fb_rows, tok=tok, heads=heads)
+
+        def gather(w):
+            axis = w.ndim - 2
+            return lax.all_gather(lax.all_gather(w, "dp", axis=axis, tiled=True), "gy", axis=axis, tiled=True)
+
+        wq, wo, wu, wd = gather(wq), gather(wo), gather(wu), gather(wd)
+
+    cfg = dict(nz=nz, zin=zin, fb=fb_rows, tok=tok, heads=heads, hw=hw, kp=kp)
     tb = tok // 4
     half = width // 2
     vm = pltpu.VMEM
-    n_sems = 130 + nz + (20 * nz if zin else 20)
+    n_sems = 160 + nz + (28 * nz if zin else 30)
     dw_specs = [pl.BlockSpec(memory_space=pl.ANY)] * 4
     if zin:
-        dw_shapes = tuple(jax.ShapeDtypeStruct((fb_rows, k), F32) for k in (kq, ko, kh, kh))
-        core_shapes = [vm((half, k), BF16) for k in (kq, ko, kh, kh)]
-        z_shapes = [vm((nz - 1, fb_rows, k), BF16) for k in (kq, ko, kh, kh)]
+        dw_shapes = (jax.ShapeDtypeStruct((3, fb_rows, hw), F32),)
+        dw_shapes += tuple(jax.ShapeDtypeStruct((fb_rows, k), F32) for k in (hw, kh, kh))
+        core_shapes = [vm((half, k), BF16) for k in (kp, hw, kh, kh)]
+        z_shapes = [vm((4, fb_rows, k), BF16) for k in (kp, hw, kh, kh)]
     else:
-        dw_shapes = tuple(jax.ShapeDtypeStruct((width, k), BF16) for k in (kq, ko, kh, kh))
+        dw_shapes = tuple(jax.ShapeDtypeStruct((width, k), BF16) for k in (kp, hw, kh, kh))
         core_shapes = [vm((16, 128), BF16)] * 4
         z_shapes = [vm((16, 128), BF16)] * 4
     scratch = [
+        vm((8, 256), F32),
         vm((8, 8, 256), F32),
         vm((width, 128), F32),
         vm((width, tok), BF16),
@@ -880,28 +1108,29 @@
         vm((width, tok), BF16),
         vm((width, tok), BF16),
         vm((width, kq), BF16),
-        vm((width, ko), BF16),
+        vm((width, hw), BF16),
         vm((width, kh), BF16),
         vm((width, kh), BF16),
-        vm((kq, tok), BF16),
-        vm((ko, tok), BF16),
+        vm((3 * hp, tok), BF16),
+        vm((4 * hd, tok), BF16),
+        vm((4 * hd, width), BF16),
         vm((hp, tb), BF16),
         vm((kh, tok), BF16),
         vm((kh, tok), BF16),
         vm((width, tb), F32),
         vm((3, width, tb), BF16),
-        vm((3, width, tb), BF16),
-        vm((8, fb_rows, tok), BF16),
-        vm((8, fb_rows, tok), BF16),
-        vm((hp, tok), F32),
-        vm((hp, tok), F32),
+        vm((6, fb_rows, tok), BF16),
+        vm((6, fb_rows, tok), BF16),
+        vm((2, fb_rows, tok), BF16),
+        vm((2, fb_rows, tok), BF16),
+        vm((hd, tb), F32),
         vm((max(width, kh), tb), F32),
         vm((max(width, kh), tb), F32),
         vm((tok, 128), jnp.int32),
         vm((4 + 2 * heads, 8, tok), F32),
         vm((max(width, kh), 128), F32),
-        vm((8, tok), F32),
-        vm((8, 8, tok), F32),
+        vm((tok // 64, 128), F32),
+        vm((8, tok // 64, 128), F32),
         vm((8, max(width, kh)), F32),
         vm((8, 8, max(width, kh)), F32),
         vm((nz, 8, max(width, kh)), F32),
@@ -920,25 +1149,30 @@
             *dw_shapes,
             jax.ShapeDtypeStruct((8, max(width, kh)), F32),
         ),
-        in_specs=[
-            pl.BlockSpec(memory_space=pltpu.SMEM),
-            vmem_spec,
-            vmem_spec,
-            any_spec,
-            any_spec,
-            any_spec,
-            any_spec,
-            any_spec,
-            vmem_spec,
-            vmem_spec,
-        ],
+        in_specs=[pl.BlockSpec(memory_space=pltpu.SMEM)] + [vmem_spec] * 7 + [any_spec] * 5 + [vmem_spec] * 2,
         out_specs=(vmem_spec, vmem_spec, *dw_specs, vmem_spec),
         scratch_shapes=scratch,
         compiler_params=pltpu.CompilerParams(
             collective_id=0, has_side_effects=True, vmem_limit_bytes=67043328
         ),
         name="encoder_block",
-    )(lengths, prm, block_input[0], cotangent[0], wq, wo, wu, wd, qb, ub)
+    )(
+        lengths,
+        ln1_gain,
+        ln1_bias,
+        out_bias,
+        ln2_gain,
+        ln2_bias,
+        down_bias,
+        block_input[0],
+        cotangent[0],
+        wq,
+        wo,
+        wu,
+        wd,
+        qv_bias,
+        up_bias.reshape(1, hid),
+    )
 
     if not zin:
 
@@ -947,23 +1181,18 @@
             return lax.optimization_barrier(lax.psum_scatter(a, "dp", scatter_dimension=0, tiled=True)).astype(F32)
 
         dq, do, du, dd = reduce(dq), reduce(do), reduce(du), reduce(dd)
-
-    def cut_heads(a):
-        parts = a.shape[-1] // HEAD_PAD
-        a = a.reshape(a.shape[:-1] + (parts, HEAD_PAD))[..., :HEAD_DIM]
-        return a.reshape(a.shape[:-2] + (parts * HEAD_DIM,))
+        dq = jnp.transpose(dq[:, : 3 * hd].reshape(zrow, 3, hd), (1, 0, 2))
 
     mine = lax.axis_index("gy") * (width // 2) + lax.axis_index("gx") * fb_rows
     feats = lax.dynamic_slice(sm, (0, mine), (6, fb_rows))
-    qkv_sum = cut_heads(sm[7:8, : 3 * hp]).reshape(3, -1)
     return (
         out[None],
         ig[None],
         feats[0:1],
         feats[1:2],
-        cut_heads(dq[:, : 3 * hp]).reshape(1, zrow, 3, -1),
-        jnp.stack([qkv_sum[0], qkv_sum[2]]),
-        jnp.transpose(cut_heads(do[:, :hp]))[:, None, :],
+        jnp.transpose(dq[:, :, :hd], (1, 0, 2))[None],
+        jnp.concatenate([sm[7:8, :hd], sm[7:8, 2 * hw : 2 * hw + hd]], axis=0),
+        jnp.transpose(do[:, :hd])[:, None, :],
         feats[2:3],
         feats[3:4],
         feats[4:5],

time: 244 us -> 225 us (0.922)
  Pallas kernels: 222 us -> 204 us
  local copies, waits for them, and re-layouts: 20 us -> 17.2 us
    pallas_call x1, Pallas kernels: 222 us -> 204 us  [local(): pl.pallas_call(functools.partial(block_kernel, cfg), out_shape=(jax.Shape...]
    reshape x12 -> x1, local copies, waits for them, and re-layouts: 5.51 us -> 1.36 us  [local(): up_bias.reshape(1, hid)]
    broadcast_in_dim x1 -> x2, local copies, waits for them, and re-layouts: 0.01 us -> 3.6 us  [the longest x1 1.97 us: local(): jnp.transpose(dq[:, :, :hd], (1, 0, 2))[None]]
where the time goes in v3:
time: 225 us; the launch traced here: 222 us
  Pallas kernels  204 us (91%)
  local copies, waits for them, and re-layouts  17.2 us (8%)
    pallas_call x1, Pallas kernels, local(): pl.pallas_call(functools.partial(block_kernel, cfg), out_shape=(jax.Shape...  204 us
    pad x4, local copies, waits for them, and re-layouts, widen(): return jnp.pad(a, [(0, 0)] * (a.ndim - 1) + [(0, cols - a.shape[-1])])  4.8 us

profile of v3, /device:TPU:0, one launch (start us, length us, event | category | flops | bytes accessed | tf_op | source)
XLA Modules:
  0.0 222.0 jit_solution(4554685644739882833)
XLA Ops:
  0.6 0.0 copy-start.5
  0.7 0.0 copy-start.4
  0.7 1.4 reshape.31.up_ref
  2.0 1.6 pad.16.wo_in
  3.6 1.7 pad.15.wq_in
  5.3 0.0 copy-done.4
  5.3 0.8 pad.17.wu_in
  6.1 0.0 copy-done.5
  6.1 0.8 pad.18.wd_in
  6.8 203.6 %encoder_block.1 = (bf16[144,2048]{1,0:T(8,128)(2,1)}, f32[144,2048]{1,0:T(8,128)}, f32[3,144,384]{2,1,0:T(8,128)}, f32[144,384]{1,0:T(8,128)}, f32[144,1152]{1,...) custom-call(s32[1,6]{1,0:T(1,128)} %len_ref.1, f32[1,144]{1,0:T(1,128)} %g1_ref.1, f32[1,144]{1,0:T(1,128)} %b1_ref.1, ...), custom_call_target="tpu_custom_call" | custom-call | tf_op jit(solution)/shard_map/encoder_block/pallas_call | solution.py:1144
  210.4 0.0 copy-start.1
  210.4 0.0 copy-start.2
  210.5 1.6 fusion
  212.1 0.7 fusion.1
  212.8 1.4 slice_reduce_fusion
  214.2 0.6 pad_maximum_fusion
  214.8 1.6 slice_bitcast_fusion.3
  216.4 2.0 slice_bitcast_fusion.2
  218.4 0.0 copy-done.2
  218.4 1.1 slice_bitcast_fusion
  219.5 0.1 copy-done.3
  219.6 0.8 copy.31
  220.4 0.6 copy-done
  221.0 1.0 copy.32
  (3 shorter events, 0.0 us)
Async XLA Ops:
  0.6 5.4 %copy-start.5 = (bf16[1076,1,144]{0,2,1:T(8,128)(2,1)S(1)}, bf16[1076,1,144]{0,2,1:T(8,128)(2,1)}, u32[]{:S(2)}) copy-start(bf16[1076,1,144]{0,2,1:T(8,128)(2,1)} %param.27) | copy-start | bytes 929668
  0.7 4.7 %copy-start.4 = (bf16[1,144,1076]{2,1,0:T(8,128)(2,1)S(1)}, bf16[1,144,1076]{2,1,0:T(8,128)(2,1)}, u32[]{:S(2)}) copy-start(bf16[1,144,1076]{2,1,0:T(8,128)(2,1)} %param.25) | copy-start | bytes 929668
  210.4 7.9 %copy-start.1 = (f32[144,1152]{1,0:T(8,128)S(1)}, f32[144,1152]{1,0:T(8,128)}, u32[]{:S(2)}) copy-start(f32[144,1152]{1,0:T(8,128)} %get-tuple-element.26) | copy-start | bytes 1990660
  210.4 7.9 %copy-start.2 = (f32[144,1152]{1,0:T(8,128)S(1)}, f32[144,1152]{1,0:T(8,128)}, u32[]{:S(2)}) copy-start(f32[144,1152]{1,0:T(8,128)} %get-tuple-element.27) | copy-start | bytes 1990660
  218.4 1.2 copy-start.3
  219.5 1.5 copy-start

commit v4 on v3

--- a/solution.py
+++ b/solution.py
@@ -104,7 +104,7 @@
     half, width = 4 * fb_rows, 8 * fb_rows
     tb = tok // 4
     hd = heads * HEAD_DIM
-    hw = cfg["hw"]
+    hw, kp = cfg["hw"], cfg["kp"]
     factor = HEAD_DIM ** (-0.5)
     z, g, c = lax.axis_index("dp"), lax.axis_index("gx"), lax.axis_index("gy")
     g_hi, g_lo = g // 2, g % 2
@@ -122,11 +122,11 @@
         counter[0] += count
         return first
 
-    def rcopy(src, dst, sem, dev):
+    def rcopy(src, dst, sem, dev, send=None):
         return pltpu.make_async_remote_copy(
             src_ref=src,
             dst_ref=dst,
-            send_sem=sem_s.at[sem],
+            send_sem=sem_s.at[sem if send is None else send],
             recv_sem=sem_r.at[sem],
             device_id=dev,
             device_id_type=MESH,
@@ -184,12 +184,19 @@
     for k, ref in enumerate(prm_refs):
         prm_send[k : k + 1, 0:fb_rows] = ref[...]
     sm_send[...] = jnp.zeros_like(sm_send)
-    sm_send[0:1, 0 : up_ref.shape[1]] = up_ref[...]
+    sm_send[0:1, 0 : up_ref.shape[0]] = up_ref[...].reshape(1, up_ref.shape[0])
     sm_send[1:2, 0:hd] = qv_ref[0:1, :]
-    sm_send[1:2, 2 * hw : 2 * hw + hd] = qv_ref[1:2, :]
+    sm_send[1:2, 2 * hd : 3 * hd] = qv_ref[1:2, :]
     for n in range(0, sm_send.shape[1], 128):
         rows = jnp.concatenate([sm_send[:, n : n + 128], jnp.zeros((120, 128), F32)], axis=0)
         prm_col[n : n + 128, 8:16] = jnp.transpose(rows)[:, 0:8]
+    if zin:
+        rows = pl.ds(pl.multiple_of(c * half + z * fb_rows, 16), fb_rows)
+        gap = jnp.zeros((fb_rows, kp - 3 * hd), BF16)
+        wq[rows, :] = jnp.concatenate([wq_in[0], wq_in[1], wq_in[2], gap], axis=1)
+        for src, dst in ((wo_in, wo), (wu_in, wu), (wd_in, wd)):
+            gap = jnp.zeros((fb_rows, dst.shape[1] - src.shape[1]), BF16)
+            dst[rows, :] = jnp.concatenate([src[...], gap], axis=1)
     pl.semaphore_wait(barrier, 7 + nz - 1)
 
     own_feat = feat(0, 0)
@@ -203,76 +210,91 @@
             rcopy(src, dst, first + dd * 2 + dc, dev(dd, dc)).start()
             pending.append(lambda dd=dd, dc=dc: rcopy(src, dst, first + dd * 2 + dc, dev(dd, dc)).wait_send())
 
-    def gather_start(first, src, dst):
+    passing = ((0, 1, 0), (1, 2, 1))
+
+    def gather_copy(first, src, dst, n, size, dd, dc):
+        tokens = pl.ds(pl.multiple_of(row_of(dc) * tok + n * size, 128), size)
+        part = dst.at[own_feat, n * size : (n + 1) * size]
+        return rcopy(src.at[:, tokens], part, first + n * 8 + dd * 2 + dc, dev(dd, dc))
+
+    def gather_land(first, dst, n, size, dd, dc, sem):
+        part = dst.at[feat(dd, dc), n * size : (n + 1) * size]
+        return rcopy(part, part, first + n * 8 + sem, partner)
+
+    def gather_pass(first, dst, n, size, k, dd, dc):
+        part = dst.at[feat(dd, dc), n * size : (n + 1) * size]
+        return rcopy(part, part, first + n * 8 + 6 + k, dev(3 - dd, 0))
+
+    def gather_own(first, src, dst, n, size):
+        tokens = pl.ds(pl.multiple_of(row_of(0) * tok + n * size, 128), size)
+        return lcopy(src.at[:, tokens], dst.at[own_feat, n * size : (n + 1) * size], first + n * 8)
+
+    def gather_start(first, src, dst, n, size):
         for dd, dc in near:
-            rcopy(src.at[:, row_tok(dc)], dst.at[own_feat, :], first + dd * 2 + dc, dev(dd, dc)).start()
-            pending.append(
-                lambda dd=dd, dc=dc: rcopy(
-                    src.at[:, row_tok(dc)], dst.at[own_feat, :], first + dd * 2 + dc, dev(dd, dc)
-                ).wait_send()
-            )
-        lcopy(src.at[:, row_tok(0)], dst.at[own_feat, :], first).start()
-
-    def relay_ref(dst, dd, dc):
-        return dst.at[feat(dd, dc), (dd - 1) * th : dd * th]
-
-    def gather_relay(first, src, dst):
-        for dd in (1, 2):
-            for dc in (0, 1):
-                rcopy(src.at[:, row_tok(0)], dst.at[feat(dd, dc), :], first + dd * 2 + dc, partner).wait_recv()
-                part = relay_ref(dst, dd, dc)
-                rcopy(part, part, first + 6 + dd * 2 + dc, dev(3 - dd, 0)).start()
-
-    def gather_done(first, src, dst):
-        lcopy(src.at[:, row_tok(0)], dst.at[own_feat, :], first).wait()
-        rcopy(src.at[:, row_tok(0)], dst.at[feat(0, 1), :], first + 1, partner).wait_recv()
-        for dd in (1, 2):
-            for dc in (0, 1):
-                part = dst.at[feat(3, dc), (dd - 1) * th : dd * th]
-                rcopy(part, part, first + 6 + dd * 2 + dc, partner).wait_recv()
-
-    def gather_sent(first, dst):
-        for dd in (1, 2):
-            for dc in (0, 1):
-                part = relay_ref(dst, dd, dc)
-                rcopy(part, part, first + 6 + dd * 2 + dc, partner).wait_send()
-
-    weights = tuple((wq_in.at[p], wq.at[:, p * hw : (p + 1) * hw]) for p in range(3))
-    weights += ((wo_in, wo), (wu_in, wu), (wd_in, wd))
+            gather_copy(first, src, dst, n, size, dd, dc).start()
+        gather_own(first, src, dst, n, size).start()
+
+    def gather_relay(first, dst, n, size):
+        for k, dd, dc in passing:
+            gather_land(first, dst, n, size, dd, dc, dd * 2 + dc).wait_recv()
+            gather_pass(first, dst, n, size, k, dd, dc).start()
+
+    def gather_done(first, src, dst, n, size):
+        gather_own(first, src, dst, n, size).wait()
+        for dd, dc in ((0, 1), (1, 1), (2, 0)):
+            gather_land(first, dst, n, size, dd, dc, dd * 2 + dc).wait_recv()
+        for k in (0, 1):
+            gather_land(first, dst, n, size, 3, k, 6 + k).wait_recv()
+
+    def gather_sent(first, src, dst, n, size):
+        for dd, dc in near:
+            gather_copy(first, src, dst, n, size, dd, dc).wait_send()
+        for k, dd, dc in passing:
+            gather_pass(first, dst, n, size, k, dd, dc).wait_send()
+
+    q_cuts = (0, 256, 512, kp)
+    weights = tuple(wq.at[:, q_cuts[p] : q_cuts[p + 1]] for p in range(3)) + (wo, wu, wd)
+    inputs = (wq_in, None, None, wo_in, wu_in, wd_in)
+    whole = (wq, wq, wq, wo, wu, wd)
     n_w = len(weights)
-    all_s = range(1, nz)
     steps = nz - 1
     nw = nz if zin else 1
-    wz0 = take(n_w * 2 * nw)
-    wc0 = take(n_w * 2 * nw)
+    wz0 = take((n_w + 2) * nw)
+    wc0 = take(4 * nw)
 
     def zrows(zz, core):
         return pl.ds(pl.multiple_of(core * half + zz * fb_rows, 16), fb_rows)
 
     def w_rows(i, zz, core):
-        return weights[i][1].at[zrows(zz, core), :]
+        return weights[i].at[zrows(zz, core), :]
+
+    def whole_rows(i, zz, core):
+        return whole[i].at[zrows(zz, core), :]
 
     def hop(i, s, d):
         origin = z - (s - 1) if d == 0 else z + (s - 1)
         here = jnp.logical_and(z >= s - 1, z < nz - 1) if d == 0 else jnp.logical_and(z < nz - s + 1, z > 0)
         to = z + 1 if d == 0 else z - 1
-        src = weights[i][0] if s == 1 else w_rows(i, origin, c)
-        return here, lambda: rcopy(src, w_rows(i, origin, c), wz0 + i * 2 * nw + s * 2 + d, (to, g, c))
+        send = wz0 + n_w * nw + i if s == 1 and d == 1 else None
+        return here, lambda: rcopy(w_rows(i, origin, c), w_rows(i, origin, c), wz0 + i * nw + origin, (to, g, c), send)
 
     def arrival(s, d):
         return (z >= s, z - s) if d == 0 else (z < nz - s, z + s)
 
+    def pass_on(i, zz):
+        first = max(i - 2, 0)
+        return rcopy(whole_rows(i, zz, c), whole_rows(i, zz, c), wc0 + first * nw + zz, partner)
+
     def z_send(i, s):
         if not zin:
-            if s == 1:
-                lcopy(weights[i][0], weights[i][1], wz0 + i * 2 * nw).start()
+            if s == 1 and inputs[i] is not None:
+                lcopy(inputs[i], whole[i], wz0 + i * nw).start()
             return
         for d in (0, 1):
             here, make = hop(i, s, d)
             pl.when(here)(lambda make=make: make().start())
-        if s == 1:
-            lcopy(weights[i][0], w_rows(i, z, c), wz0 + i * 2 * nw).start()
-            rcopy(weights[i][0], w_rows(i, z, c), wc0 + i * 2 * nw, partner).start()
+        if s == 1 and i >= 2:
+            pass_on(i, z).start()
 
     def z_recv(i, s):
         if not zin:
@@ -283,57 +305,43 @@
             @pl.when(here)
             def _(s=s, d=d, origin=origin):
                 rows = w_rows(i, origin, c)
-                rcopy(rows, rows, wz0 + i * 2 * nw + s * 2 + d, partner).wait_recv()
-                rcopy(rows, rows, wc0 + i * 2 * nw + s * 2 + d, partner).start()
+                rcopy(rows, rows, wz0 + i * nw + origin, partner).wait_recv()
+                if i >= 2:
+                    pass_on(i, origin).start()
 
         if s < steps:
             z_send(i, s + 1)
 
     def weight_ready(i):
         if not zin:
-            lcopy(weights[i][0], weights[i][1], wz0 + i * 2 * nw).wait()
+            if inputs[i] is not None:
+                lcopy(inputs[i], whole[i], wz0 + i * nw).wait()
             return
-        lcopy(weights[i][0], w_rows(i, z, c), wz0 + i * 2 * nw).wait()
-        rcopy(weights[i][0], w_rows(i, z, 1 - c), wc0 + i * 2 * nw, partner).wait_recv()
-        for s in range(1, nz):
-            for d in (0, 1):
-                here, origin = arrival(s, d)
-
-                @pl.when(here)
-                def _(s=s, d=d, origin=origin):
-                    rows = w_rows(i, origin, 1 - c)
-                    rcopy(rows, rows, wc0 + i * 2 * nw + s * 2 + d, partner).wait_recv()
+        if i >= 2:
+            for zz in range(nz):
+                rows = whole_rows(i, zz, 1 - c)
+                rcopy(rows, rows, wc0 + (i - 2) * nw + zz, partner).wait_recv()
 
     def weight_passed(i):
         if not zin:
             return
-        rcopy(weights[i][0], w_rows(i, z, c), wc0 + i * 2 * nw, partner).wait_send()
         for s in range(1, nz):
             for d in (0, 1):
                 here, make = hop(i, s, d)
                 pl.when(here)(lambda make=make: make().wait_send())
-                here, origin = arrival(s, d)
-
-                @pl.when(here)
-                def _(s=s, d=d, origin=origin):
-                    rows = w_rows(i, origin, c)
-                    rcopy(rows, rows, wc0 + i * 2 * nw + s * 2 + d, partner).wait_send()
+        if i >= 2:
+            for zz in range(nz):
+                pass_on(i, zz).wait_send()
 
     p0 = take(8)
-    xs0 = take(12)
-    cs0 = take(12)
+    xs0 = take(16)
+    cs0 = take(16)
     exchange(p0, prm_send, prm_all.at[me])
     lcopy(prm_send, prm_all.at[me], p0).start()
-    gather_start(xs0, x_ref, x_t)
+    for n in (0, 1):
+        gather_start(xs0, x_ref, x_t, n, th)
     for i in range(3):
         z_send(i, 1)
-
-    lcopy(prm_send, prm_all.at[me], p0).wait()
-    for dd, dc in others:
-        rcopy(prm_send, prm_all.at[row_of(dc) * 4 + gx_of(dd)], p0 + dd * 2 + dc, partner).wait_recv()
-    for b in range(8):
-        rows = jnp.concatenate([prm_all[b], jnp.zeros((120, 256), F32)], axis=0)
-        prm_col[b * fb_rows : (b + 1) * fb_rows, 0:8] = jnp.transpose(rows)[:fb_rows, 0:8]
 
     def par(k):
         return prm_col[:, k : k + 1]
@@ -343,17 +351,10 @@
             if step < nz:
                 z_recv(i, step)
 
-    z_recv_all(((0, 1), (1, 1), (0, 2), (2, 1), (1, 2), (0, 3)))
-    gather_relay(xs0, x_ref, x_t)
-    gather_start(cs0, cot_ref, cot_t)
-    z_recv_all(((2, 2), (1, 3)))
-    z_send(3, 1)
-    z_recv_all(((2, 3),))
-    for i in range(3):
-        z_recv_all((i, step) for step in range(4, nz))
-    gather_done(xs0, x_ref, x_t)
-
-    def ln1(j, carry):
+    def head_rows(part, h):
+        return pl.ds(pl.multiple_of((part * heads + h) * HEAD_PAD, 16), HEAD_PAD)
+
+    def project(j, carry):
         t = toks(j)
         x = x_t[:, t].astype(F32)
         m = jnp.sum(x, axis=0, keepdims=True) * (1.0 / width)
@@ -362,31 +363,41 @@
         rows_f[2, 0:1, t] = m
         rows_f[3, 0:1, t] = r
         h1_t[:, t] = ((x - m) * r * par(0) + par(1)).astype(BF16)
+        part = mm(wq[...], h1_t[:, t], TN) + prm_col[0:kp, 9:10]
+        for p in range(3):
+            for h in range(heads):
+                first, row = (p * heads + h) * HEAD_PAD, p * hd + h * HEAD_DIM
+                qkv_t[first : first + HEAD_DIM, t] = part[row : row + HEAD_DIM, :].astype(BF16)
         return carry
 
-    lax.fori_loop(0, 4, ln1, 0)
-
+    z_recv_all(((0, 1), (1, 1), (2, 1)))
+    z_send(3, 1)
+    gather_relay(xs0, x_t, 0, th)
+    z_recv_all(((0, 2), (1, 2), (2, 2)))
+    gather_relay(xs0, x_t, 1, th)
     z_recv_all(((3, 1),))
-    z_send(4, 1)
+
+    lcopy(prm_send, prm_all.at[me], p0).wait()
+    for dd, dc in others:
+        rcopy(prm_send, prm_all.at[row_of(dc) * 4 + gx_of(dd)], p0 + dd * 2 + dc, partner).wait_recv()
+    for b in range(8):
+        rows = jnp.concatenate([prm_all[b], jnp.zeros((120, 256), F32)], axis=0)
+        prm_col[b * fb_rows : (b + 1) * fb_rows, 0:8] = jnp.transpose(rows)[:fb_rows, 0:8]
+
+    for step in range(3, nz):
+        z_recv_all((i, step) for i in range(3))
     for i in range(3):
         weight_ready(i)
-
-    def head_rows(part, h):
-        return pl.ds(pl.multiple_of((part * heads + h) * HEAD_PAD, 16), HEAD_PAD)
-
-    def project(j, carry):
-        t = toks(j)
-        for p in range(3):
-            part = mm(wq[:, p * hw : (p + 1) * hw], h1_t[:, t], TN)
-            if p != 1:
-                part = part + prm_col[p * hw : (p + 1) * hw, 9:10]
-            for h in range(heads):
-                first = (p * heads + h) * HEAD_PAD
-                qkv_t[first : first + HEAD_DIM, t] = part[h * HEAD_DIM : (h + 1) * HEAD_DIM, :].astype(BF16)
-        return carry
-
-    lax.fori_loop(0, 4, project, 0)
+    gather_done(xs0, x_ref, x_t, 0, th)
+    gather_start(cs0, cot_ref, cot_t, 0, th)
+    lax.fori_loop(0, 2, project, 0)
     z_recv_all(((3, 2),))
+    z_send(4, 1)
+    gather_done(xs0, x_ref, x_t, 1, th)
+    lax.fori_loop(2, 4, project, 0)
+    z_recv_all((3, step) for step in range(3, nz))
+    z_send(5, 1)
+    weight_ready(3)
 
     def kept_of(h, t):
         scores = mm(qkv_t[head_rows(1, h), :], qkv_t[head_rows(0, h), t], TN) * factor
@@ -484,32 +495,24 @@
         lax.fori_loop(0, heads, head, 0)
         att_t[own_heads, t] = dqf[...].astype(BF16)
 
-        @pl.when(j == 0)
-        def _():
-            z_recv_all((3, step) for step in range(3, nz))
-            weight_ready(3)
-            wo_first()
-
         att_send(j, True)
 
-        @pl.when(j == 0)
-        def _():
+        @pl.when(j == 1)
+        def _():
+            wo_second()
             z_recv_all(((4, 1),))
-            gather_relay(cs0, cot_ref, cot_t)
 
         @pl.when(j == 2)
         def _():
-            wo_second()
-            z_recv_all(((4, 2),))
-            z_send(5, 1)
             att_relay(0)
 
         return carry
 
+    wo_first()
     lax.fori_loop(0, 4, attend, 0)
+    wo_third()
     att_relay(1)
-    wo_third()
-    z_recv_all((4, step) for step in range(3, nz))
+    z_recv_all(((4, 2),))
 
     def project_out(j, carry):
         t = toks(j)
@@ -522,6 +525,8 @@
         @pl.when(j == 1)
         def _():
             att_relay(3)
+            gather_relay(cs0, cot_t, 0, th)
+            gather_start(cs0, cot_ref, cot_t, 1, th)
             z_recv_all(((5, 1),))
 
         far = att_piece(3, j)
@@ -541,9 +546,8 @@
         return carry
 
     lax.fori_loop(0, 4, project_out, 0)
+    z_recv_all((4, step) for step in range(3, nz))
     weight_ready(4)
-    z_recv_all(((5, 2),))
-    gather_done(cs0, cot_ref, cot_t)
     for n in range(7):
         wo_copy(n).wait_send()
 
@@ -572,21 +576,9 @@
             part = halves(buf, step, step)
             rcopy(part, part, first + 2 + step, partner).wait_send()
 
-    g20 = take(4)
-
-    def tsend(step):
-        return wo_n.at[:, (step - 1) * tb : step * tb]
-
-    def mlp(i, carry):
-        t = toks(gx_of(3 - i))
+    def mlp_up(i, carry):
+        t = toks(i)
         fa[...] = mm(wu[...], h2_t[:, t], TN) + prm_col[:, 8:9]
-
-        @pl.when(i == 0)
-        def _():
-            z_recv_all((5, step) for step in range(3, nz))
-            weight_ready(5)
-
-        fb[...] = mm(wd[...], cot_t[:, t], TN)
 
         def chunk(n, inner):
             rows = pl.ds(pl.multiple_of(n * 48, 16), 48)
@@ -596,30 +588,71 @@
             hf = 0.5 * (1.0 + thv)
             act_t[rows, t] = (v * hf).astype(BF16)
             slope = hf + (0.5 * GELU_C) * v * (1.0 - thv * thv) * (1.0 + (3.0 * GELU_A) * v2)
-            gpre_t[rows, t] = (fb[rows, :] * slope).astype(BF16)
+            gpre_t[rows, t] = slope.astype(BF16)
             return inner
 
         lax.fori_loop(0, fa.shape[0] // 48, chunk, 0)
+
+        @pl.when(i == 0)
+        def _():
+            z_recv_all(((5, 2),))
+
+        @pl.when(i == 1)
+        def _():
+            gather_relay(cs0, cot_t, 1, th)
+
+        return carry
+
+    lax.fori_loop(0, 4, mlp_up, 0)
+    for n in (0, 1):
+        gather_done(cs0, cot_ref, cot_t, n, th)
+    z_recv_all((5, step) for step in range(3, nz))
+    weight_ready(5)
+
+    for n in (0, 1):
+        gather_sent(xs0, x_ref, x_t, n, th)
+    g20 = xs0
+
+    def tsend(step):
+        return wo_n.at[:, (step - 1) * tb : step * tb]
+
+    def g2_copy(n):
+        top, bottom = slice(0, half), slice(half, width)
+        rows = (top, bottom, top, bottom, bottom, top)[n]
+        step = (3, 3, 1, 1, 2, 2)[n]
+        slot = (2, 2, 0, 0, 1, 1)[n]
+        to = (1, 2, 1, 1, 2, 2)[n]
+        src = wo_n.at[rows, (step - 1) * tb : step * tb]
+        return rcopy(src, trecv.at[slot, rows, :], g20 + n, (z, gx_of(to), c))
+
+    def mlp_back(i, carry):
+        t = toks(gx_of(3 - i))
+        gpre_t[:, t] = (mm(wd[...], cot_t[:, t], TN) * gpre_t[:, t].astype(F32)).astype(BF16)
         fa[...] = mm(wu[...], gpre_t[:, t], NN)
-        for step in (1, 2, 3):
+        for step, sends in ((3, (0, 1)), (2, (4,)), (1, (2,))):
 
             @pl.when(i == 3 - step)
-            def _(step=step):
+            def _(step=step, sends=sends):
                 tsend(step)[...] = fa[...].astype(BF16)
-                rcopy(tsend(step), trecv.at[step - 1], g20 + step, (z, gx_of(step), c)).start()
+                for n in sends:
+                    g2_copy(n).start()
 
         return carry
 
-    lax.fori_loop(0, 4, mlp, 0)
+    lax.fori_loop(0, 4, mlp_back, 0)
+    for n, step, rows, then in ((0, 2, slice(0, half), 5), (1, 1, slice(half, width), 3)):
+        g2_copy(n).wait_recv()
+        cols = slice((step - 1) * tb, step * tb)
+        wo_n[rows, cols] = (wo_n[rows, cols].astype(F32) + trecv[2, rows, :].astype(F32)).astype(BF16)
+        g2_copy(then).start()
 
     dwc0 = take(4)
-    dwz0 = take(4 * 8)
-    do0 = take(16)
+    dwz0 = take(4 * 6)
+    do0 = take(4)
     gath = ((0, 1, 2), (3,), (4,), (5,))
     core_recv = (cq, co, cu, cd)
     z_recvs = (zq, zo, zu, zd)
     dw_refs = (wo_n, wo, wu, wd)
-    kp = cfg["kp"]
     dw_cols = (kp, wo.shape[1], wu.shape[1], wd.shape[1])
     dw_outs = (dq_out, do_out, du_out, dd_out)
     slots = [0]
@@ -679,11 +712,11 @@
 
     def z_piece(i, sem, zz, slot, to):
         rows = dw_refs[i].at[zrows(zz, c), 0 : dw_cols[i]]
-        return rcopy(rows, z_recvs[i].at[slot], dwz0 + i * 8 + sem, (to, g, c))
+        return rcopy(rows, z_recvs[i].at[slot], dwz0 + i * 6 + sem, (to, g, c))
 
     def z_land(i, slot):
         rows = dw_refs[i].at[zrows(z, c), 0 : dw_cols[i]]
-        return rcopy(rows, z_recvs[i].at[min(slot, 3) if slot != 3 else 0], dwz0 + i * 8 + slot, partner)
+        return rcopy(rows, z_recvs[i].at[min(slot, 3) if slot != 3 else 0], dwz0 + i * 6 + slot, partner)
 
     def relay_z(i, slot):
         if not zin:
@@ -752,22 +785,24 @@
         for part, goes in pieces:
             size = part.shape[1]
             slot = slots[0] % 16
-            if slots[0] >= 16:
-                leaving[slot].wait()
+            if slots[0] >= 4:
+                leaving[slots[0] - 4].wait()
             slots[0] += 1
             stage = (fa, fb)[slot // 8].at[(slot % 8) * fb_rows : (slot % 8 + 1) * fb_rows, 0:size]
             stage[...] = part
-            cp = lcopy(stage, goes, do0 + slot)
+            cp = lcopy(stage, goes, do0 + slot % 4)
             cp.start()
-            if len(leaving) > slot:
-                leaving[slot] = cp
-            else:
-                leaving.append(cp)
-
-    ml0 = take(16)
-    gh0 = take(16)
-    uv0 = take(8)
-    sm0 = take(8)
+            leaving.append(cp)
+
+    ml0, gh0, uv0, sm0 = cs0, xs0, at0, p0
+    for n in (0, 1):
+        gather_sent(cs0, cot_ref, cot_t, n, th)
+    for j in range(4):
+        att_send(j, False)
+        att_relayed(j)
+    for wait in pending:
+        wait()
+    pending.clear()
     sz0 = take(nz)
 
     direct, added = ((1, 0), (2, 1), (0, 1)), ((1, 1), (2, 0))
@@ -825,9 +860,9 @@
     ones = jnp.ones((tok, 128), BF16)
     sums_col[0 : act_t.shape[0], 6:7] = mm(gpre_t[...], ones, NN)[:, 0:1]
 
-    for step in (1, 2, 3):
-        rcopy(tsend(step), trecv.at[step - 1], g20 + step, partner).wait_recv()
-    gh2 = fa[...] + trecv[0].astype(F32) + trecv[1].astype(F32) + trecv[2].astype(F32)
+    for n in (2, 3, 4, 5):
+        g2_copy(n).wait_recv()
+    gh2 = fa[...] + trecv[0].astype(F32) + trecv[1].astype(F32)
     m2 = rows_f[2, 1:2, own_t]
     r2 = rows_f[3, 1:2, own_t]
     normed2 = (resid[...] - m2) * r2
@@ -838,24 +873,23 @@
     g_res = cot_own + r2 * (gn - s1 - normed2 * s2)
     g_low = g_res.astype(BF16)
     gb_t[:, own_t] = g_low
-    gb0 = take(5)
+    gb0 = wn0
     spread(gb0, gb_t)
     resid[...] = g_res
     sums_col[0:width, 2:3] = jnp.sum(g_low.astype(F32), axis=1, keepdims=True)
     sums_col[0:width, 3:4] = jnp.sum(gh2 * normed2, axis=1, keepdims=True)
     sums_col[0:width, 4:5] = jnp.sum(gh2, axis=1, keepdims=True)
     sums_col[0:width, 5:6] = jnp.sum(cot_own, axis=1, keepdims=True)
-    for step in (1, 2, 3):
-        rcopy(tsend(step), trecv.at[step - 1], g20 + step, partner).wait_send()
+    for n in range(6):
+        g2_copy(n).wait_send()
     weight_grad(3, cot_t, act_t)
     send_core(3)
     relay_z(2, 0)
+    sum_core(3)
 
     fa[...] = jnp.zeros_like(fa)
     fb[...] = jnp.zeros_like(fb)
-    for p in range(3):
-        act_t[p * hw + hd : (p + 1) * hw, :] = jnp.zeros((hw - hd, tok), BF16)
-    gpre_t[3 * hd : kp, :] = jnp.zeros((kp - 3 * hd, tok), BF16)
+    act_t[3 * hd : kp, :] = jnp.zeros((kp - 3 * hd, tok), BF16)
 
     def attend_back(i, carry):
         t = toks(gx_of(i))
@@ -876,17 +910,12 @@
         for h in range(heads):
             gatt_t[h * HEAD_PAD : h * HEAD_PAD + HEAD_DIM, :] = gatt[h * HEAD_DIM : (h + 1) * HEAD_DIM, :].astype(BF16)
 
-        @pl.when(i == 1)
-        def _():
-            sum_core(3)
-
         @pl.when(i == 2)
         def _():
             relay_z(2, 1)
 
         @pl.when(i == 3)
         def _():
-            add_relayed(h2_t, mrelay, mrecv, ml0)
             weight_passed(3)
             wo[:, 0:hd] = mm(gb_t[...], att_t[own_heads, :], NT).astype(BF16)
             send_core(1)
@@ -912,29 +941,21 @@
 
         lax.fori_loop(0, heads, head, 0)
         act_t[0:hd, t] = dqf[...].astype(BF16)
-        gpre_t[0:hd, t] = dqf[...].astype(BF16)
         return carry
 
     lax.fori_loop(0, 4, attend_back, 0)
-    kq = wq.shape[1]
+
     for kb in range(4):
         cols, rows = slice(kb * tb, (kb + 1) * tb), slice(kb * hd, (kb + 1) * hd)
-        dk_low, dv_low = (fa[rows, :] * factor).astype(BF16), fb[rows, :].astype(BF16)
-        act_t[hw : hw + hd, cols] = dk_low
-        act_t[2 * hw : 2 * hw + hd, cols] = dv_low
-        gpre_t[hd : 2 * hd, cols] = dk_low
-        gpre_t[2 * hd : 3 * hd, cols] = dv_low
-    weight_grad(0, h1_t, gpre_t)
-    send_core(0)
+        act_t[hd : 2 * hd, cols] = (fa[rows, :] * factor).astype(BF16)
+        act_t[2 * hd : 3 * hd, cols] = fb[rows, :].astype(BF16)
+    add_relayed(h2_t, mrelay, mrecv, ml0)
     sum_core(1)
     relay_z(3, 0)
-    sums_col[0:kq, 7:8] = mm(act_t[0:kq, :], ones, NN)[:, 0:1]
-    sum_core(0)
-    gather_sent(cs0, cot_t)
 
     def back1(j, carry):
         t = toks(j)
-        gh1 = mm(wq[...], act_t[0:kq, t], NN)
+        gh1 = mm(wq[...], act_t[0:kp, t], NN)
         m = rows_f[2, 0:1, t]
         r = rows_f[3, 0:1, t]
         normed = (x_t[:, t].astype(F32) - m) * r
@@ -963,16 +984,20 @@
 
     lax.fori_loop(0, 4, back1, 0)
 
+    scatter_start(cot_t, grecv, gh0)
+    weight_grad(0, h1_t, act_t)
+    send_core(0)
+    sums_col[0:kp, 7:8] = mm(act_t[0:kp, :], ones, NN)[:, 0:1]
     relay_z(3, 1)
     relay_z(1, 0)
     relay_z(1, 1)
+    sum_core(0)
 
     for n in range(0, sm_send.shape[1], 128):
         sm_send[:, n : n + 128] = jnp.transpose(sums_col[n : n + 128, :])[0:8, :]
     exchange(sm0, sm_send, sm_recv.at[me])
     exchange(uv0, uv_send, uv_recv.at[me])
     lcopy(uv_send, uv_recv.at[me], uv0).start()
-    scatter_start(cot_t, grecv, gh0)
     add_relayed(cot_t, grelay, grecv, gh0)
     relay_z(0, 0)
 
@@ -1021,14 +1046,10 @@
         total_z = total_z + smz_recv[k]
     sm_out[...] = total_z
 
-    for cp in leaving:
+    for cp in leaving[-4:]:
         cp.wait()
     for wait in pending:
         wait()
-    gather_sent(xs0, x_t)
-    for j in range(4):
-        att_send(j, False)
-        att_relayed(j)
     scatter_sent(h2_t, mrelay, mrecv, ml0)
     scatter_sent(cot_t, grelay, grecv, gh0)
     for i in range(4):
@@ -1063,31 +1084,26 @@
     hp = heads * HEAD_PAD
     hid = w_up.shape[2]
     kh = round_up(hid, 384)
-    kq = 3 * hw
     kp = round_up(3 * hd, 128)
     zrow = w_qkv.shape[1]
     zin = zrow == fb_rows and nz == 4
 
-    def widen(a, cols):
-        return jnp.pad(a, [(0, 0)] * (a.ndim - 1) + [(0, cols - a.shape[-1])])
-
-    wq = widen(jnp.transpose(w_qkv[0], (1, 0, 2)), hw)
-    wo = widen(jnp.transpose(w_out[:, 0, :]), hw)
-    wu = widen(w_up[0], kh)
-    wd = widen(jnp.transpose(w_down[:, 0, :]), kh)
+    wq, wo = jnp.transpose(w_qkv[0], (1, 0, 2)), jnp.transpose(w_out[:, 0, :])
+    wu, wd = w_up[0], jnp.transpose(w_down[:, 0, :])
     if not zin:
 
-        def gather(w):
-            axis = w.ndim - 2
-            return lax.all_gather(lax.all_gather(w, "dp", axis=axis, tiled=True), "gy", axis=axis, tiled=True)
-
-        wq, wo, wu, wd = gather(wq), gather(wo), gather(wu), gather(wd)
+        def gather(w, cols):
+            w = jnp.pad(w, ((0, 0), (0, cols - w.shape[1])))
+            return lax.all_gather(lax.all_gather(w, "dp", axis=0, tiled=True), "gy", axis=0, tiled=True)
+
+        wq = gather(w_qkv[0].reshape(zrow, 3 * hd), kp)
+        wo, wu, wd = gather(wo, hw), gather(wu, kh), gather(wd, kh)
 
     cfg = dict(nz=nz, zin=zin, fb=fb_rows, tok=tok, heads=heads, hw=hw, kp=kp)
     tb = tok // 4
     half = width // 2
     vm = pltpu.VMEM
-    n_sems = 160 + nz + (28 * nz if zin else 30)
+    n_sems = 92 + nz + (12 * nz if zin else 12)
     dw_specs = [pl.BlockSpec(memory_space=pl.ANY)] * 4
     if zin:
         dw_shapes = (jax.ShapeDtypeStruct((3, fb_rows, hw), F32),)
@@ -1107,7 +1123,7 @@
         vm((width, tok), BF16),
         vm((width, tok), BF16),
         vm((width, tok), BF16),
-        vm((width, kq), BF16),
+        vm((width, kp), BF16),
         vm((width, hw), BF16),
         vm((width, kh), BF16),
         vm((width, kh), BF16),
@@ -1141,6 +1157,7 @@
     ]
     any_spec = pl.BlockSpec(memory_space=pl.ANY)
     vmem_spec = pl.BlockSpec(memory_space=pltpu.VMEM)
+    w_spec = vmem_spec if zin else any_spec
     out, ig, dq, do, du, dd, sm = pl.pallas_call(
         functools.partial(block_kernel, cfg),
         out_shape=(
@@ -1149,7 +1166,7 @@
             *dw_shapes,
             jax.ShapeDtypeStruct((8, max(width, kh)), F32),
         ),
-        in_specs=[pl.BlockSpec(memory_space=pltpu.SMEM)] + [vmem_spec] * 7 + [any_spec] * 5 + [vmem_spec] * 2,
+        in_specs=[pl.BlockSpec(memory_space=pltpu.SMEM)] + [vmem_spec] * 7 + [any_spec] + [w_spec] * 4 + [vmem_spec] * 2,
         out_specs=(vmem_spec, vmem_spec, *dw_specs, vmem_spec),
         scratch_shapes=scratch,
         compiler_params=pltpu.CompilerParams(
@@ -1171,7 +1188,7 @@
         wu,
         wd,
         qv_bias,
-        up_bias.reshape(1, hid),
+        up_bias,
     )
 
     if not zin:
@@ -1191,7 +1208,7 @@
         feats[0:1],
         feats[1:2],
         jnp.transpose(dq[:, :, :hd], (1, 0, 2))[None],
-        jnp.concatenate([sm[7:8, :hd], sm[7:8, 2 * hw : 2 * hw + hd]], axis=0),
+        jnp.concatenate([sm[7:8, :hd], sm[7:8, 2 * hd : 3 * hd]], axis=0),
         jnp.transpose(do[:, :hd])[:, None, :],
         feats[2:3],
         feats[3:4],

time: 225 us -> 197 us (0.88)
  Pallas kernels: 204 us -> 183 us
  local copies, waits for them, and re-layouts: 17.2 us -> 11.1 us
    pallas_call x1, Pallas kernels: 204 us -> 183 us  [local(): pl.pallas_call(functools.partial(block_kernel, cfg), out_shape=(jax.Shape...]
    pad x4 -> x0, local copies, waits for them, and re-layouts: 4.8 us -> none  [widen(): return jnp.pad(a, [(0, 0)] * (a.ndim - 1) + [(0, cols - a.shape[-1])])]
where the time goes in v4:
time: 197 us; the launch traced here: 195 us
  Pallas kernels  183 us (93%)
  local copies, waits for them, and re-layouts  11.1 us (6%)
    pallas_call x1, Pallas kernels, local(): pl.pallas_call(functools.partial(block_kernel, cfg), out_shape=(jax.Shape...  183 us

profile of v4, /device:TPU:0, one launch (start us, length us, event | category | flops | bytes accessed | tf_op | source)
XLA Modules:
  0.0 194.9 jit_solution(8219140606613625000)
XLA Ops:
  0.7 182.6 %encoder_block.1 = (bf16[144,2048]{1,0:T(8,128)(2,1)}, f32[144,2048]{1,0:T(8,128)}, f32[3,144,384]{2,1,0:T(8,128)}, f32[144,384]{1,0:T(8,128)}, f32[144,1152]{1,...) custom-call(s32[1,6]{1,0:T(1,128)} %len_ref.1, f32[1,144]{1,0:T(1,128)} %g1_ref.1, f32[1,144]{1,0:T(1,128)} %b1_ref.1, ...), custom_call_target="tpu_custom_call" | custom-call | tf_op jit(solution)/shard_map/encoder_block/pallas_call | solution.py:1161
  183.3 0.0 copy-start.1
  183.3 0.0 copy-start.2
  183.3 1.6 fusion
  184.9 0.8 fusion.1
  185.7 1.4 slice_reduce_fusion
  187.1 0.6 pad_maximum_fusion
  187.7 1.6 slice_bitcast_fusion.3
  189.3 2.0 %slice_bitcast_fusion.2 = f32[1,144,3,288]{3,1,2,0:T(8,128)} fusion(f32[3,144,384]{2,1,0:T(8,128)} %get-tuple-element.24), kind=kLoop, calls=%fused_computation.2 | loop fusion | bytes 995328 | tf_op jit(solution)/shard_map/broadcast_in_dim | solution.py:1210
  191.3 0.0 copy-done.1
  191.3 0.0 copy-done.2
  191.3 0.0 copy-start.3
  191.3 1.1 slice_bitcast_fusion
  192.4 0.0 copy-start
  192.4 0.1 copy-done.3
  192.5 0.8 copy.31
  193.3 0.6 copy-done
  193.9 1.0 copy.32
Async XLA Ops:
  183.3 8.0 %copy-start.1 = (f32[144,1152]{1,0:T(8,128)S(1)}, f32[144,1152]{1,0:T(8,128)}, u32[]{:S(2)}) copy-start(f32[144,1152]{1,0:T(8,128)} %get-tuple-element.26) | copy-start | bytes 1990660
  183.3 8.0 %copy-start.2 = (f32[144,1152]{1,0:T(8,128)S(1)}, f32[144,1152]{1,0:T(8,128)}, u32[]{:S(2)}) copy-start(f32[144,1152]{1,0:T(8,128)} %get-tuple-element.27) | copy-start | bytes 1990660
  191.3 1.2 copy-start.3
  192.4 1.5 copy-start

commit v5 on v4

--- a/solution.py
+++ b/solution.py
@@ -85,7 +85,9 @@
     uv_send,
     uv_recv,
     sm_send,
-    sm_recv,
+    sm_part,
+    sm_chip,
+    sm_win,
     smz_recv,
     cq,
     co,
@@ -335,12 +337,12 @@
 
     p0 = take(8)
     xs0 = take(16)
-    cs0 = take(16)
+    cs0 = take(32)
     exchange(p0, prm_send, prm_all.at[me])
     lcopy(prm_send, prm_all.at[me], p0).start()
     for n in (0, 1):
         gather_start(xs0, x_ref, x_t, n, th)
-    for i in range(3):
+    for i in (0, 1, 2):
         z_send(i, 1)
 
     def par(k):
@@ -350,6 +352,52 @@
         for i, step in pairs:
             if step < nz:
                 z_recv(i, step)
+
+    wn0 = take(8)
+
+    def wo_part(gx, core, first=0, last=None):
+        rows = (fb_rows if last is None else last) - first
+        return wo_n.at[pl.ds(pl.multiple_of(gx * hd + core * fb_rows + first, 16), rows), :]
+
+    cut = fb_rows // 32 * 16 + 16
+
+    def wo_copy(n):
+        if n < 2:
+            own = wo_part(g, c)
+            return rcopy(own, own, wn0 + n + 1, (z, gx_of(n + 1), c))
+        if n < 4:
+            got = wo_part(gx_of(n - 1), c)
+            return rcopy(got, got, wn0 + n + 1, partner)
+        if n < 6:
+            on = wo_part(gx_of(1), c, 0, cut) if n == 4 else wo_part(gx_of(2), c, cut)
+            return rcopy(on, on, wn0 + n + 1, (z, gx_of(6 - n), c))
+        far = wo_part(gx_of(3), c)
+        return rcopy(far, far, wn0 + 7, partner)
+
+    def wo_first():
+        turned = jnp.transpose(wo[...])
+        wo_n[pl.ds(pl.multiple_of(g * hd, 16), hd), :] = turned[0:hd, :]
+        for n in (0, 1):
+            wo_copy(n).start()
+
+    def wo_second():
+        for step in (1, 2):
+            got = wo_part(gx_of(step), c)
+            rcopy(got, got, wn0 + step, partner).wait_recv()
+        for n in (4, 5, 2, 3):
+            wo_copy(n).start()
+
+    def wo_third():
+        for step, on in ((1, wo_part(gx_of(3), c, 0, cut)), (2, wo_part(gx_of(3), c, cut))):
+            rcopy(on, on, wn0 + 4 + step, partner).wait_recv()
+        wo_copy(6).start()
+
+    def wo_ready():
+        for step in (1, 2):
+            got = wo_part(gx_of(step), 1 - c)
+            rcopy(got, got, wn0 + 2 + step, partner).wait_recv()
+        far = wo_part(gx_of(3), 1 - c)
+        rcopy(far, far, wn0 + 7, partner).wait_recv()
 
     def head_rows(part, h):
         return pl.ds(pl.multiple_of((part * heads + h) * HEAD_PAD, 16), HEAD_PAD)
@@ -373,9 +421,9 @@
     z_recv_all(((0, 1), (1, 1), (2, 1)))
     z_send(3, 1)
     gather_relay(xs0, x_t, 0, th)
-    z_recv_all(((0, 2), (1, 2), (2, 2)))
+    z_recv_all(((0, 2), (1, 2)))
     gather_relay(xs0, x_t, 1, th)
-    z_recv_all(((3, 1),))
+    z_recv_all(((2, 2), (3, 1)))
 
     lcopy(prm_send, prm_all.at[me], p0).wait()
     for dd, dc in others:
@@ -389,15 +437,16 @@
     for i in range(3):
         weight_ready(i)
     gather_done(xs0, x_ref, x_t, 0, th)
-    gather_start(cs0, cot_ref, cot_t, 0, th)
+    for n in (0, 1):
+        gather_start(cs0, cot_ref, cot_t, n, tb)
     lax.fori_loop(0, 2, project, 0)
     z_recv_all(((3, 2),))
     z_send(4, 1)
     gather_done(xs0, x_ref, x_t, 1, th)
     lax.fori_loop(2, 4, project, 0)
     z_recv_all((3, step) for step in range(3, nz))
-    z_send(5, 1)
     weight_ready(3)
+    wo_first()
 
     def kept_of(h, t):
         scores = mm(qkv_t[head_rows(1, h), :], qkv_t[head_rows(0, h), t], TN) * factor
@@ -406,52 +455,6 @@
         allowed = jnp.concatenate([key_pic] * (tb // 128), axis=1) == query_pic
         return jnp.where(allowed, jnp.exp(scores), 0.0)
 
-    wn0 = take(8)
-
-    def wo_part(gx, core, first=0, last=None):
-        rows = (fb_rows if last is None else last) - first
-        return wo_n.at[pl.ds(pl.multiple_of(gx * hd + core * fb_rows + first, 16), rows), :]
-
-    cut = fb_rows // 32 * 16 + 16
-
-    def wo_copy(n):
-        if n < 2:
-            own = wo_part(g, c)
-            return rcopy(own, own, wn0 + n + 1, (z, gx_of(n + 1), c))
-        if n < 4:
-            got = wo_part(gx_of(n - 1), c)
-            return rcopy(got, got, wn0 + n + 1, partner)
-        if n < 6:
-            on = wo_part(gx_of(1), c, 0, cut) if n == 4 else wo_part(gx_of(2), c, cut)
-            return rcopy(on, on, wn0 + n + 1, (z, gx_of(6 - n), c))
-        far = wo_part(gx_of(3), c)
-        return rcopy(far, far, wn0 + 7, partner)
-
-    def wo_first():
-        turned = jnp.transpose(wo[...])
-        wo_n[pl.ds(pl.multiple_of(g * hd, 16), hd), :] = turned[0:hd, :]
-        for n in (0, 1):
-            wo_copy(n).start()
-
-    def wo_second():
-        for step in (1, 2):
-            got = wo_part(gx_of(step), c)
-            rcopy(got, got, wn0 + step, partner).wait_recv()
-        for n in (4, 5, 2, 3):
-            wo_copy(n).start()
-
-    def wo_third():
-        for step, on in ((1, wo_part(gx_of(3), c, 0, cut)), (2, wo_part(gx_of(3), c, cut))):
-            rcopy(on, on, wn0 + 4 + step, partner).wait_recv()
-        wo_copy(6).start()
-
-    def wo_ready():
-        for step in (1, 2):
-            got = wo_part(gx_of(step), 1 - c)
-            rcopy(got, got, wn0 + 2 + step, partner).wait_recv()
-        far = wo_part(gx_of(3), 1 - c)
-        rcopy(far, far, wn0 + 7, partner).wait_recv()
-
     at0 = take(4 * 3)
     own_heads = pl.ds(pl.multiple_of(g * hd, 16), hd)
 
@@ -468,12 +471,12 @@
         for step in (1, 2):
             piece = att_piece(step, j)
             rcopy(piece, piece, at0 + j * 3 + step - 1, partner).wait_recv()
-        step = 1 if j < 2 else 2
+        step = 1 + j % 2
         piece = att_piece(step, j)
         rcopy(piece, piece, at0 + j * 3 + 2, (z, gx_of(3 - step), c)).start()
 
     def att_relayed(j):
-        piece = att_piece(1 if j < 2 else 2, j)
+        piece = att_piece(1 + j % 2, j)
         rcopy(piece, piece, at0 + j * 3 + 2, partner).wait_send()
 
     def attend(j, carry):
@@ -497,37 +500,34 @@
 
         att_send(j, True)
 
+        @pl.when(j == 0)
+        def _():
+            z_recv_all(((4, 1),))
+            z_send(5, 1)
+
         @pl.when(j == 1)
         def _():
             wo_second()
-            z_recv_all(((4, 1),))
 
         @pl.when(j == 2)
         def _():
             att_relay(0)
+            z_recv_all(((4, 2),))
 
         return carry
 
-    wo_first()
     lax.fori_loop(0, 4, attend, 0)
+    att_relay(1)
     wo_third()
-    att_relay(1)
-    z_recv_all(((4, 2),))
+    z_recv_all(((5, 1),))
+    att_relay(2)
 
     def project_out(j, carry):
         t = toks(j)
 
         @pl.when(j == 0)
         def _():
-            att_relay(2)
             wo_ready()
-
-        @pl.when(j == 1)
-        def _():
-            att_relay(3)
-            gather_relay(cs0, cot_t, 0, th)
-            gather_start(cs0, cot_ref, cot_t, 1, th)
-            z_recv_all(((5, 1),))
 
         far = att_piece(3, j)
         rcopy(far, far, at0 + j * 3 + 2, partner).wait_recv()
@@ -543,10 +543,25 @@
         def _():
             resid[...] = residual
 
+        @pl.when(j == 0)
+        def _():
+            att_relay(3)
+            for n in (2, 3):
+                gather_start(cs0, cot_ref, cot_t, n, tb)
+            for n in (0, 1):
+                gather_relay(cs0, cot_t, n, tb)
+
+        @pl.when(j == 1)
+        def _():
+            z_recv_all((4, step) for step in range(3, nz))
+
+        @pl.when(j == 2)
+        def _():
+            z_recv_all(((5, 2),))
+
         return carry
 
     lax.fori_loop(0, 4, project_out, 0)
-    z_recv_all((4, step) for step in range(3, nz))
     weight_ready(4)
     for n in range(7):
         wo_copy(n).wait_send()
@@ -593,19 +608,16 @@
 
         lax.fori_loop(0, fa.shape[0] // 48, chunk, 0)
 
-        @pl.when(i == 0)
-        def _():
-            z_recv_all(((5, 2),))
-
         @pl.when(i == 1)
         def _():
-            gather_relay(cs0, cot_t, 1, th)
+            for n in (2, 3):
+                gather_relay(cs0, cot_t, n, tb)
 
         return carry
 
     lax.fori_loop(0, 4, mlp_up, 0)
-    for n in (0, 1):
-        gather_done(cs0, cot_ref, cot_t, n, th)
+    for n in range(4):
+        gather_done(cs0, cot_ref, cot_t, n, tb)
     z_recv_all((5, step) for step in range(3, nz))
     weight_ready(5)
 
@@ -699,7 +711,8 @@
         @pl.when(leaf)
         def _():
             for slot, zz in enumerate((far_end, far_inner, inner)):
-                z_piece(i, slot, zz, slot, inner).start()
+                if i or slot < 2:
+                    z_piece(i, slot, zz, slot, inner).start()
 
         @pl.when(jnp.logical_not(leaf))
         def _():
@@ -795,8 +808,8 @@
             leaving.append(cp)
 
     ml0, gh0, uv0, sm0 = cs0, xs0, at0, p0
-    for n in (0, 1):
-        gather_sent(cs0, cot_ref, cot_t, n, th)
+    for n in range(4):
+        gather_sent(cs0, cot_ref, cot_t, n, tb)
     for j in range(4):
         att_send(j, False)
         att_relayed(j)
@@ -847,6 +860,9 @@
 
     weight_grad(2, h2_t, gpre_t)
     send_core(2)
+    ones = jnp.ones((tok, 128), BF16)
+    sums_col[0 : act_t.shape[0], 6:7] = mm(gpre_t[...], ones, NN)[:, 0:1]
+    sum_core(2)
 
 
     def lower(j, carry):
@@ -856,9 +872,6 @@
 
     lax.fori_loop(0, 4, lower, 0)
     h2_t[:, own_t] = (mm(wd[...], act_t[:, own_t], NN) + resid[...] + par(5)).astype(BF16)
-    sum_core(2)
-    ones = jnp.ones((tok, 128), BF16)
-    sums_col[0 : act_t.shape[0], 6:7] = mm(gpre_t[...], ones, NN)[:, 0:1]
 
     for n in (2, 3, 4, 5):
         g2_copy(n).wait_recv()
@@ -897,6 +910,7 @@
         @pl.when(i == 1)
         def _():
             spread_relay(gb0, gb_t)
+            relay_z(2, 1)
             for n in (0, 1):
                 for k in range(4):
                     hand(h2_t, mrelay, ml0, k, n).start()
@@ -905,20 +919,18 @@
         @pl.when(i == 3)
         def _():
             spread_done(gb0, gb_t)
+            relay_z(3, 0)
 
         gatt = mm(wo[...], gb_t[:, t], TN)
         for h in range(heads):
             gatt_t[h * HEAD_PAD : h * HEAD_PAD + HEAD_DIM, :] = gatt[h * HEAD_DIM : (h + 1) * HEAD_DIM, :].astype(BF16)
 
-        @pl.when(i == 2)
-        def _():
-            relay_z(2, 1)
-
         @pl.when(i == 3)
         def _():
             weight_passed(3)
             wo[:, 0:hd] = mm(gb_t[...], att_t[own_heads, :], NT).astype(BF16)
             send_core(1)
+            add_relayed(h2_t, mrelay, mrecv, ml0)
 
         def head(h, inner):
             kept = kept_of(h, t)
@@ -949,9 +961,10 @@
         cols, rows = slice(kb * tb, (kb + 1) * tb), slice(kb * hd, (kb + 1) * hd)
         act_t[hd : 2 * hd, cols] = (fa[rows, :] * factor).astype(BF16)
         act_t[2 * hd : 3 * hd, cols] = fb[rows, :].astype(BF16)
-    add_relayed(h2_t, mrelay, mrecv, ml0)
+    relay_z(3, 1)
+    weight_grad(0, h1_t, act_t)
+    send_core(0)
     sum_core(1)
-    relay_z(3, 0)
 
     def back1(j, carry):
         t = toks(j)
@@ -980,24 +993,38 @@
         cot_t[:, t] = fa[...].astype(BF16)
         for n in (0, 1):
             hand(cot_t, grelay, gh0, j, n).start()
+
+        @pl.when(j == 0)
+        def _():
+            sum_core(0)
+
         return carry
 
     lax.fori_loop(0, 4, back1, 0)
-
-    scatter_start(cot_t, grecv, gh0)
-    weight_grad(0, h1_t, act_t)
-    send_core(0)
-    sums_col[0:kp, 7:8] = mm(act_t[0:kp, :], ones, NN)[:, 0:1]
-    relay_z(3, 1)
     relay_z(1, 0)
     relay_z(1, 1)
-    sum_core(0)
+
+    sums_col[0:kp, 7:8] = mm(act_t[0:kp, :], ones, NN)[:, 0:1]
 
     for n in range(0, sm_send.shape[1], 128):
         sm_send[:, n : n + 128] = jnp.transpose(sums_col[n : n + 128, :])[0:8, :]
-    exchange(sm0, sm_send, sm_recv.at[me])
     exchange(uv0, uv_send, uv_recv.at[me])
     lcopy(uv_send, uv_recv.at[me], uv0).start()
+    rcopy(sm_send, sm_part, sm0 + 1, partner).start()
+    rcopy(sm_send, sm_part, sm0 + 1, partner).wait_recv()
+    sm_chip[...] = sm_send[...] + sm_part[...]
+    win = sm_win.shape[2]
+
+    def window(dd):
+        first = (c * half + gx_of(dd) * fb_rows) // 128 * 128
+        return pl.ds(pl.multiple_of(jnp.minimum(first, sm_chip.shape[1] - win), 128), win)
+
+    def window_copy(dd):
+        return rcopy(sm_chip.at[:, window(dd)], sm_win.at[dd], sm0 + dd * 2, (z, gx_of(dd), c))
+
+    for dd in (1, 2, 3):
+        window_copy(dd).start()
+    scatter_start(cot_t, grecv, gh0)
     add_relayed(cot_t, grelay, grecv, gh0)
     relay_z(0, 0)
 
@@ -1006,14 +1033,15 @@
 
     sum_z(2)
     sum_z(3)
-
-    total_sm = sm_send[...]
-    row8 = lax.broadcasted_iota(jnp.int32, total_sm.shape, 0)
-    for dd, dc in others:
-        rcopy(sm_send, sm_recv.at[row_of(dc) * 4 + gx_of(dd)], sm0 + dd * 2 + dc, partner).wait_recv()
-        part = sm_recv[row_of(dc) * 4 + gx_of(dd)]
-        total_sm = total_sm + (part if dd == 0 else jnp.where(row8 < 6, part, 0.0))
-    smz_recv[0] = total_sm
+    relay_z(0, 1)
+
+    total_sm = sm_chip[:, window(0)]
+    for dd in (1, 2, 3):
+        window_copy(dd).wait_recv()
+        total_sm = total_sm + sm_win[dd]
+    smz_recv[0, 0:8, :] = total_sm
+    for n in range(6):
+        smz_recv[0, 8 + n : 9 + n, :] = sm_chip[6 + n // 3 : 7 + n // 3, n % 3 * win : (n % 3 + 1) * win]
     for k in range(1, nz):
 
         def make(k=k):
@@ -1022,7 +1050,12 @@
         make().start()
         pending.append(lambda make=make: make().wait_send())
 
-    relay_z(0, 1)
+    if zin:
+
+        @pl.when(leaf)
+        def _():
+            z_piece(0, 2, inner, 2, inner).start()
+
     sum_z(1)
 
     lcopy(uv_send, uv_recv.at[me], uv0).wait()
@@ -1048,6 +1081,9 @@
 
     for cp in leaving[-4:]:
         cp.wait()
+    rcopy(sm_send, sm_part, sm0 + 1, partner).wait_send()
+    for dd in (1, 2, 3):
+        window_copy(dd).wait_send()
     for wait in pending:
         wait()
     scatter_sent(h2_t, mrelay, mrecv, ml0)
@@ -1055,6 +1091,26 @@
     for i in range(4):
         z_sent(i)
     spread_sent(gb0, gb_t)
+
+
+def finish_kernel(cfg, out_in, ig_in, sm_in, *refs):
+    fb_rows, hd, n_dw = cfg["fb"], cfg["hd"], cfg["n_dw"]
+    dw_in, (out_ref, ig_ref, *small), dw_ref = refs[:n_dw], refs[n_dw : n_dw + 10], refs[n_dw + 10 :]
+    out_ref[...] = out_in[...]
+    ig_ref[...] = ig_in[...]
+    sums = sm_in[...]
+    win = sums.shape[1]
+    mine = lax.axis_index("gy") * (4 * fb_rows) + lax.axis_index("gx") * fb_rows
+    first = jnp.minimum(mine // 128 * 128, 2 * win)
+    turned = pltpu.roll(sums[0:8, :], (win - (mine - first)) % win, 1)
+    for k in range(6):
+        small[k][...] = turned[k : k + 1, 0:fb_rows]
+    up_row, qkv_row = (jnp.concatenate([sums[r + n : r + n + 1, :] for n in range(3)], axis=1) for r in (8, 11))
+    small[6][0:1, :] = qkv_row[:, 0:hd]
+    small[6][1:2, :] = qkv_row[:, 2 * hd : 3 * hd]
+    small[7][...] = up_row[:, 0 : small[7].shape[0]].reshape(small[7].shape[0])
+    for src, dst in zip(dw_in, dw_ref):
+        dst[...] = src[:, :, 0 : dst.shape[2]] if len(dst.shape) == 3 else src[:, 0 : dst.shape[1]]
 
 
 def local(
@@ -1099,11 +1155,14 @@
         wq = gather(w_qkv[0].reshape(zrow, 3 * hd), kp)
         wo, wu, wd = gather(wo, hw), gather(wu, kh), gather(wd, kh)
 
+    win = max(width, kh) // 3
+    if win % 128:
+        raise ValueError("window")
     cfg = dict(nz=nz, zin=zin, fb=fb_rows, tok=tok, heads=heads, hw=hw, kp=kp)
     tb = tok // 4
     half = width // 2
     vm = pltpu.VMEM
-    n_sems = 92 + nz + (12 * nz if zin else 12)
+    n_sems = 108 + nz + (12 * nz if zin else 12)
     dw_specs = [pl.BlockSpec(memory_space=pl.ANY)] * 4
     if zin:
         dw_shapes = (jax.ShapeDtypeStruct((3, fb_rows, hw), F32),)
@@ -1148,8 +1207,10 @@
         vm((tok // 64, 128), F32),
         vm((8, tok // 64, 128), F32),
         vm((8, max(width, kh)), F32),
-        vm((8, 8, max(width, kh)), F32),
-        vm((nz, 8, max(width, kh)), F32),
+        vm((8, max(width, kh)), F32),
+        vm((8, max(width, kh)), F32),
+        vm((4, 8, win), F32),
+        vm((nz, 16, win), F32),
         *core_shapes,
         *z_shapes,
         pltpu.SemaphoreType.DMA((n_sems,)),
@@ -1164,7 +1225,7 @@
             jax.ShapeDtypeStruct((fb_rows, tok2), BF16),
             jax.ShapeDtypeStruct((fb_rows, tok2), F32),
             *dw_shapes,
-            jax.ShapeDtypeStruct((8, max(width, kh)), F32),
+            jax.ShapeDtypeStruct((16, win), F32),
         ),
         in_specs=[pl.BlockSpec(memory_space=pltpu.SMEM)] + [vmem_spec] * 7 + [any_spec] + [w_spec] * 4 + [vmem_spec] * 2,
         out_specs=(vmem_spec, vmem_spec, *dw_specs, vmem_spec),
@@ -1200,23 +1261,41 @@
         dq, do, du, dd = reduce(dq), reduce(do), reduce(du), reduce(dd)
         dq = jnp.transpose(dq[:, : 3 * hd].reshape(zrow, 3, hd), (1, 0, 2))
 
-    mine = lax.axis_index("gy") * (width // 2) + lax.axis_index("gx") * fb_rows
-    feats = lax.dynamic_slice(sm, (0, mine), (6, fb_rows))
+    shapes = [(fb_rows, tok2, BF16), (fb_rows, tok2, F32)] + [(1, fb_rows, F32)] * 6 + [(2, hd, F32), (hid, F32)]
+    shapes = [jax.ShapeDtypeStruct(a[:-1], a[-1]) for a in shapes]
+    given = []
+    if zin:
+        given = [dq, do, du, dd]
+        shapes += [jax.ShapeDtypeStruct((3, fb_rows, hd), F32), jax.ShapeDtypeStruct((fb_rows, hd), F32)]
+        shapes += [jax.ShapeDtypeStruct((fb_rows, hid), F32)] * 2
+    final = pl.pallas_call(
+        functools.partial(finish_kernel, dict(fb=fb_rows, hd=hd, n_dw=len(given))),
+        out_shape=tuple(shapes),
+        in_specs=[vmem_spec] * (3 + len(given)),
+        out_specs=(vmem_spec,) * len(shapes),
+        compiler_params=pltpu.CompilerParams(vmem_limit_bytes=67043328),
+        name="finish",
+    )(out, ig, sm, *given)
+    out, ig, g1, b1, ob, g2, b2, db, qv, up = final[:10]
+    if zin:
+        dq, do, du, dd = final[10:]
+    else:
+        do, du, dd = do[:, :hd], du[:, :hid], dd[:, :hid]
     return (
         out[None],
         ig[None],
-        feats[0:1],
-        feats[1:2],
-        jnp.transpose(dq[:, :, :hd], (1, 0, 2))[None],
-        jnp.concatenate([sm[7:8, :hd], sm[7:8, 2 * hd : 3 * hd]], axis=0),
-        jnp.transpose(do[:, :hd])[:, None, :],
-        feats[2:3],
-        feats[3:4],
-        feats[4:5],
-        du[None, :, :hid],
-        sm[6, :hid],
-        jnp.transpose(dd[:, :hid])[:, None, :],
-        feats[5:6],
+        g1,
+        b1,
+        jnp.transpose(dq, (1, 0, 2))[None],
+        qv,
+        jnp.transpose(do)[:, None, :],
+        ob,
+        g2,
+        b2,
+        du[None],
+        up,
+        jnp.transpose(dd)[:, None, :],
+        db,
     )
 
 

time: 197 us -> 184 us (0.934)
  local copies, waits for them, and re-layouts: 11.1 us -> 0 us
    broadcast_in_dim x3 -> x0, local copies, waits for them, and re-layouts: 4.75 us -> none  [the longest x1 1.97 us: local(): jnp.transpose(dq[:, :, :hd], (1, 0, 2))[None]]
    pallas_call x0 -> x1, Pallas kernels: none -> 4.16 us  [local(): pl.pallas_call(functools.partial(finish_kernel, dict(fb=fb_rows, hd=hd, n...]
    slice x3 -> x0, local copies, waits for them, and re-layouts: 3.8 us -> none  [the longest x1 1.6 us: local(): feats[5:6]]
    pallas_call x1, Pallas kernels: 183 us -> 179 us  [local(): pl.pallas_call(functools.partial(block_kernel, cfg), out_shape=(jax.Shape...]
    unnamed x10 -> x0, local copies, waits for them, and re-layouts: 2.52 us -> none
where the time goes in v5:
time: 184 us
  Pallas kernels  183 us (99%)
    pallas_call x1, Pallas kernels, local(): pl.pallas_call(functools.partial(block_kernel, cfg), out_shape=(jax.Shape...  179 us
    pallas_call x1, Pallas kernels, local(): pl.pallas_call(functools.partial(finish_kernel, dict(fb=fb_rows, hd=hd, n...  4.16 us

profile of v5, /device:TPU:0, one launch (start us, length us, event | category | flops | bytes accessed | tf_op | source)
XLA Modules:
  0.0 183.8 jit_solution(18073088660054255722)
XLA Ops:
  0.7 179.0 %encoder_block.1 = (bf16[144,2048]{1,0:T(8,128)(2,1)}, f32[144,2048]{1,0:T(8,128)}, f32[3,144,384]{2,1,0:T(8,128)}, f32[144,384]{1,0:T(8,128)}, f32[144,1152]{1,...) custom-call(s32[1,6]{1,0:T(1,128)} %len_ref.1, f32[1,144]{1,0:T(1,128)} %g1_ref.1, f32[1,144]{1,0:T(1,128)} %b1_ref.1, ...), custom_call_target="tpu_custom_call" | custom-call | tf_op jit(solution)/shard_map/encoder_block/pallas_call | solution.py:1222
  179.7 4.2 %finish.1 = (bf16[144,2048]{1,0:T(8,128)(2,1)}, f32[144,2048]{1,0:T(8,128)}, f32[1,144]{1,0:T(1,128)}, f32[1,144]{1,0:T(1,128)}, f32[1,144]{1,0:T(1,128)}, /*ind...) custom-call(bf16[144,2048]{1,0:T(8,128)(2,1)} %get-tuple-element.35., ...), custom_call_target="tpu_custom_call" | custom-call | tf_op jit(solution)/shard_map/finish/pallas_call | solution.py:1271

commit v6 on v5

--- a/solution.py
+++ b/solution.py
@@ -93,10 +93,14 @@
     co,
     cu,
     cd,
+    cv,
     zq,
     zo,
     zu,
     zd,
+    zv,
+    out_s,
+    ig_s,
     sem_s,
     sem_r,
 ):
@@ -658,15 +662,17 @@
         wo_n[rows, cols] = (wo_n[rows, cols].astype(F32) + trecv[2, rows, :].astype(F32)).astype(BF16)
         g2_copy(then).start()
 
-    dwc0 = take(4)
-    dwz0 = take(4 * 6)
+    dwc0 = take(5)
+    dwz0 = take(5 * 6)
+    first_up = 2 * wu.shape[1] // 3
     do0 = take(4)
-    gath = ((0, 1, 2), (3,), (4,), (5,))
-    core_recv = (cq, co, cu, cd)
-    z_recvs = (zq, zo, zu, zd)
-    dw_refs = (wo_n, wo, wu, wd)
-    dw_cols = (kp, wo.shape[1], wu.shape[1], wd.shape[1])
-    dw_outs = (dq_out, do_out, du_out, dd_out)
+    gath = ((0, 1, 2), (3,), (4,), (5,), ())
+    core_recv = (cq, co, cu, cd, cv)
+    z_recvs = (zq, zo, zu, zd, zv)
+    dw_refs = (wo_n, wo, wu.at[:, 0:first_up], wd, wu.at[:, first_up : wu.shape[1]])
+    dw_cols = (kp, wo.shape[1], first_up, wd.shape[1], wu.shape[1] - first_up)
+    up_outs = (du_out.at[:, 0:first_up], du_out.at[:, first_up : wu.shape[1]])
+    dw_outs = (dq_out, do_out, up_outs[0], dd_out, up_outs[1])
     slots = [0]
     leaving = []
 
@@ -817,6 +823,7 @@
         wait()
     pending.clear()
     sz0 = take(nz)
+    fin0 = take(2)
 
     direct, added = ((1, 0), (2, 1), (0, 1)), ((1, 1), (2, 0))
 
@@ -860,9 +867,12 @@
 
     weight_grad(2, h2_t, gpre_t)
     send_core(2)
+    weight_grad(4, h2_t, gpre_t.at[first_up : wu.shape[1], :])
+    send_core(4)
+    sum_core(2)
     ones = jnp.ones((tok, 128), BF16)
     sums_col[0 : act_t.shape[0], 6:7] = mm(gpre_t[...], ones, NN)[:, 0:1]
-    sum_core(2)
+    sum_core(4)
 
 
     def lower(j, carry):
@@ -898,6 +908,7 @@
     weight_grad(3, cot_t, act_t)
     send_core(3)
     relay_z(2, 0)
+    relay_z(2, 1)
     sum_core(3)
 
     fa[...] = jnp.zeros_like(fa)
@@ -910,7 +921,8 @@
         @pl.when(i == 1)
         def _():
             spread_relay(gb0, gb_t)
-            relay_z(2, 1)
+            relay_z(4, 0)
+            relay_z(4, 1)
             for n in (0, 1):
                 for k in range(4):
                     hand(h2_t, mrelay, ml0, k, n).start()
@@ -1029,9 +1041,11 @@
     relay_z(0, 0)
 
     for dc in (0, 1):
-        out_ref[:, row_tok(dc)] = scatter_sum(h2_t, mrecv, ml0, dc).astype(BF16)
+        out_s[:, row_tok(dc)] = scatter_sum(h2_t, mrecv, ml0, dc).astype(BF16)
+    lcopy(out_s, out_ref, fin0).start()
 
     sum_z(2)
+    sum_z(4)
     sum_z(3)
     relay_z(0, 1)
 
@@ -1070,7 +1084,8 @@
         u_row = jnp.concatenate([uv[n : n + 1, :] for n in range(n_rows)], axis=1)
         v_row = jnp.concatenate([uv[n_rows + n : n_rows + n + 1, :] for n in range(n_rows)], axis=1)
         x_own = x_ref[:, row_tok(dc)].astype(F32)
-        ig_ref[:, row_tok(dc)] = acc - u_row - x_own * v_row
+        ig_s[:, row_tok(dc)] = acc - u_row - x_own * v_row
+    lcopy(ig_s, ig_ref, fin0 + 1).start()
 
     sum_z(0)
     total_z = smz_recv[0]
@@ -1081,6 +1096,8 @@
 
     for cp in leaving[-4:]:
         cp.wait()
+    lcopy(out_s, out_ref, fin0).wait()
+    lcopy(ig_s, ig_ref, fin0 + 1).wait()
     rcopy(sm_send, sm_part, sm0 + 1, partner).wait_send()
     for dd in (1, 2, 3):
         window_copy(dd).wait_send()
@@ -1088,7 +1105,7 @@
         wait()
     scatter_sent(h2_t, mrelay, mrecv, ml0)
     scatter_sent(cot_t, grelay, grecv, gh0)
-    for i in range(4):
+    for i in range(5):
         z_sent(i)
     spread_sent(gb0, gb_t)
 
@@ -1141,6 +1158,7 @@
     hid = w_up.shape[2]
     kh = round_up(hid, 384)
     kp = round_up(3 * hd, 128)
+    up_a = 2 * kh // 3
     zrow = w_qkv.shape[1]
     zin = zrow == fb_rows and nz == 4
 
@@ -1162,17 +1180,17 @@
     tb = tok // 4
     half = width // 2
     vm = pltpu.VMEM
-    n_sems = 108 + nz + (12 * nz if zin else 12)
+    n_sems = 118 + nz + (12 * nz if zin else 12)
     dw_specs = [pl.BlockSpec(memory_space=pl.ANY)] * 4
     if zin:
         dw_shapes = (jax.ShapeDtypeStruct((3, fb_rows, hw), F32),)
         dw_shapes += tuple(jax.ShapeDtypeStruct((fb_rows, k), F32) for k in (hw, kh, kh))
-        core_shapes = [vm((half, k), BF16) for k in (kp, hw, kh, kh)]
-        z_shapes = [vm((4, fb_rows, k), BF16) for k in (kp, hw, kh, kh)]
+        core_shapes = [vm((half, k), BF16) for k in (kp, hw, up_a, kh, kh - up_a)]
+        z_shapes = [vm((4, fb_rows, k), BF16) for k in (kp, hw, up_a, kh, kh - up_a)]
     else:
         dw_shapes = tuple(jax.ShapeDtypeStruct((width, k), BF16) for k in (kp, hw, kh, kh))
-        core_shapes = [vm((16, 128), BF16)] * 4
-        z_shapes = [vm((16, 128), BF16)] * 4
+        core_shapes = [vm((16, 128), BF16)] * 5
+        z_shapes = [vm((16, 128), BF16)] * 5
     scratch = [
         vm((8, 256), F32),
         vm((8, 8, 256), F32),
@@ -1213,6 +1231,8 @@
         vm((nz, 16, win), F32),
         *core_shapes,
         *z_shapes,
+        vm((fb_rows, tok2), BF16),
+        vm((fb_rows, tok2), F32),
         pltpu.SemaphoreType.DMA((n_sems,)),
         pltpu.SemaphoreType.DMA((n_sems,)),
     ]
@@ -1228,7 +1248,7 @@
             jax.ShapeDtypeStruct((16, win), F32),
         ),
         in_specs=[pl.BlockSpec(memory_space=pltpu.SMEM)] + [vmem_spec] * 7 + [any_spec] + [w_spec] * 4 + [vmem_spec] * 2,
-        out_specs=(vmem_spec, vmem_spec, *dw_specs, vmem_spec),
+        out_specs=(any_spec, any_spec, *dw_specs, vmem_spec),
         scratch_shapes=scratch,
         compiler_params=pltpu.CompilerParams(
             collective_id=0, has_side_effects=True, vmem_limit_bytes=67043328

time: 184 us -> 183 us (level)
  no operation moved by 1% of the time
where the time goes in v6:
time: 183 us
  Pallas kernels  182 us (99%)
    pallas_call x1, Pallas kernels, local(): pl.pallas_call(functools.partial(block_kernel, cfg), out_shape=(jax.Shape...  178 us
    pallas_call x1, Pallas kernels, local(): pl.pallas_call(functools.partial(finish_kernel, dict(fb=fb_rows, hd=hd, n...  4.16 us

profile of v6, /device:TPU:0, one launch (start us, length us, event | category | flops | bytes accessed | tf_op | source)
XLA Modules:
  0.0 182.5 jit_solution(16655376839000550033)
XLA Ops:
  0.7 177.7 %encoder_block.1 = (bf16[144,2048]{1,0:T(8,128)(2,1)}, f32[144,2048]{1,0:T(8,128)}, f32[3,144,384]{2,1,0:T(8,128)}, f32[144,384]{1,0:T(8,128)}, f32[144,1152]{1,...) custom-call(s32[1,6]{1,0:T(1,128)} %len_ref.1, f32[1,144]{1,0:T(1,128)} %g1_ref.1, f32[1,144]{1,0:T(1,128)} %b1_ref.1, ...), custom_call_target="tpu_custom_call" | custom-call | tf_op jit(solution)/shard_map/encoder_block/pallas_call | solution.py:1242
  178.4 4.2 %finish.1 = (bf16[144,2048]{1,0:T(8,128)(2,1)}, f32[144,2048]{1,0:T(8,128)}, f32[1,144]{1,0:T(1,128)}, f32[1,144]{1,0:T(1,128)}, f32[1,144]{1,0:T(1,128)}, /*ind...) custom-call(bf16[144,2048]{1,0:T(8,128)(2,1)} %get-tuple-element.35., ...), custom_call_target="tpu_custom_call" | custom-call | tf_op jit(solution)/shard_map/finish/pallas_call | solution.py:1291
